TPU v7x, 8 devices: a whole 2x2x1 slice. The times are simulated.
8 devices in a mesh: fsdp: 8 (over z, y, x, core).
Axes of the slice: x: 2, y: 2, z: 1, core: 2. Of those that a mesh axis runs over, the one named last changes fastest.
Arguments:
- act_in: bfloat16 [256, 196, 1024], P('fsdp')
- labels: int32 [256], P('fsdp')
- layer_p: float32 [2, 8599552], P(None, 'fsdp')
- head_w: float32 [1024, 21843], P('fsdp')
- small_p: float32 [24576], P('fsdp')
- layer_m: float32 [2, 8599552], P(None, 'fsdp')
- head_m: float32 [1024, 21843], P('fsdp')
- small_m: float32 [24576], P('fsdp')
- layer_v: float32 [2, 8599552], P(None, 'fsdp')
- head_v: float32 [1024, 21843], P('fsdp')
- small_v: float32 [24576], P('fsdp')
Outputs:
- output 1: float32 [], replicated
- output 2: float32 [2, 8599552], P(None, 'fsdp')
- output 3: float32 [1024, 21843], P('fsdp')
- output 4: float32 [24576], P('fsdp')
- output 5: float32 [2, 8599552], P(None, 'fsdp')
- output 6: float32 [1024, 21843], P('fsdp')
- output 7: float32 [24576], P('fsdp')
- output 8: float32 [2, 8599552], P(None, 'fsdp')
- output 9: float32 [1024, 21843], P('fsdp')
- output 10: float32 [24576], P('fsdp')
All inputs are finite; a program needn't handle non-finite values.
Results may differ from a plain program's by a relative error of at most 0.001.
Values are sent between devices in bfloat16 or wider.
A program may use at most 1 GiB of HBM per device.

v0:
```python
import math
import jax
import jax.numpy as jnp
from jax import lax
from jax.sharding import PartitionSpec as P

LN_EPS = 1e-6
LEARN_RATE = 0.003
BETA_ONE = 0.9
BETA_TWO = 0.999
ADAM_EPS = 1e-8
WEIGHT_DECAY = 0.03
ADAM_STEP = 10


def piece_shapes(num_tokens, num_chans):
    tok_hid = num_chans // 2
    ch_hid = 4 * num_chans
    return [(num_tokens, tok_hid), (tok_hid, num_tokens), (num_chans, ch_hid), (ch_hid, num_chans), (num_chans,), (num_chans,), (tok_hid,), (num_tokens,), (num_chans,), (num_chans,), (ch_hid,), (num_chans,)]


def layer_length(num_tokens, num_chans):
    return sum(math.prod(shape_one) for shape_one in piece_shapes(num_tokens, num_chans))


def unpack_layer(flat, num_tokens, num_chans):
    pieces = []
    piece_start = 0
    for shape_one in piece_shapes(num_tokens, num_chans):
        piece_len = math.prod(shape_one)
        pieces.append(flat[piece_start:piece_start + piece_len].reshape(shape_one))
        piece_start = piece_start + piece_len
    return pieces


def layer_norm(x_in, ln_gain, ln_shift):
    x_f = x_in.astype(jnp.float32)
    mean_val = jnp.mean(x_f, axis=-1, keepdims=True)
    var_val = jnp.mean(jnp.square(x_f - mean_val), axis=-1, keepdims=True)
    normed = (x_f - mean_val) * lax.rsqrt(var_val + LN_EPS)
    return (normed * ln_gain.astype(jnp.float32) + ln_shift.astype(jnp.float32)).astype(jnp.bfloat16)


def gelu_bf16(hidden):
    return jax.nn.gelu(hidden).astype(jnp.bfloat16)


def gelu_grad(hidden, d_act):
    _, pullback = jax.vjp(gelu_bf16, hidden)
    return pullback(d_act.astype(jnp.bfloat16))[0]


def norm_grad(x_in, ln_gain, ln_shift, d_normed):
    _, pullback = jax.vjp(layer_norm, x_in, ln_gain.astype(jnp.float32), ln_shift.astype(jnp.float32))
    d_x, d_gain, d_shift = pullback(d_normed.astype(jnp.bfloat16))
    return d_x.astype(jnp.float32), d_gain, d_shift


def layer_forward(x_in, flat, num_tokens, num_chans):
    w_tok1, w_tok2, w_ch1, w_ch2, ln1_g, ln1_b, b_tok1, b_tok2, ln2_g, ln2_b, b_ch1, b_ch2 = unpack_layer(flat, num_tokens, num_chans)
    normed = layer_norm(x_in, ln1_g, ln1_b)
    hid_tok = jnp.einsum('bsc,sj->bcj', normed, w_tok1, preferred_element_type=jnp.float32) + b_tok1.astype(jnp.float32)
    act_tok = gelu_bf16(hid_tok)
    tok_out = jnp.einsum('bcj,js->bsc', act_tok, w_tok2, preferred_element_type=jnp.float32) + b_tok2.astype(jnp.float32)[:, None]
    after_tok = (x_in.astype(jnp.float32) + tok_out).astype(jnp.bfloat16)
    normed2 = layer_norm(after_tok, ln2_g, ln2_b)
    hid_ch = jnp.einsum('bsc,cd->bsd', normed2, w_ch1, preferred_element_type=jnp.float32) + b_ch1.astype(jnp.float32)
    act_ch = gelu_bf16(hid_ch)
    ch_out = jnp.einsum('bsd,dc->bsc', act_ch, w_ch2, preferred_element_type=jnp.float32) + b_ch2.astype(jnp.float32)
    layer_out = (after_tok.astype(jnp.float32) + ch_out).astype(jnp.bfloat16)
    return layer_out, (x_in, normed, hid_tok, act_tok, after_tok, normed2, hid_ch, act_ch)


def layer_backward(d_out, flat, cache, num_tokens, num_chans):
    w_tok1, w_tok2, w_ch1, w_ch2, ln1_g, ln1_b, b_tok1, b_tok2, ln2_g, ln2_b, b_ch1, b_ch2 = unpack_layer(flat, num_tokens, num_chans)
    x_in, normed, hid_tok, act_tok, after_tok, normed2, hid_ch, act_ch = cache
    d_out_bf = d_out.astype(jnp.bfloat16)
    g_b_ch2 = jnp.sum(d_out, axis=(0, 1))
    g_w_ch2 = jnp.einsum('bsd,bsc->dc', act_ch, d_out_bf, preferred_element_type=jnp.float32)
    d_act_ch = jnp.einsum('bsc,dc->bsd', d_out_bf, w_ch2, preferred_element_type=jnp.float32)
    d_hid_ch = gelu_grad(hid_ch, d_act_ch)
    d_hid_ch_bf = d_hid_ch.astype(jnp.bfloat16)
    g_b_ch1 = jnp.sum(d_hid_ch, axis=(0, 1))
    g_w_ch1 = jnp.einsum('bsc,bsd->cd', normed2, d_hid_ch_bf, preferred_element_type=jnp.float32)
    d_normed2 = jnp.einsum('bsd,cd->bsc', d_hid_ch_bf, w_ch1, preferred_element_type=jnp.float32)
    d_after_ln, g_ln2_g, g_ln2_b = norm_grad(after_tok, ln2_g, ln2_b, d_normed2)
    d_after = d_after_ln + d_out
    d_after_bf = d_after.astype(jnp.bfloat16)
    g_b_tok2 = jnp.sum(d_after, axis=(0, 2))
    g_w_tok2 = jnp.einsum('bcj,bsc->js', act_tok, d_after_bf, preferred_element_type=jnp.float32)
    d_act_tok = jnp.einsum('bsc,js->bcj', d_after_bf, w_tok2, preferred_element_type=jnp.float32)
    d_hid_tok = gelu_grad(hid_tok, d_act_tok)
    d_hid_tok_bf = d_hid_tok.astype(jnp.bfloat16)
    g_b_tok1 = jnp.sum(d_hid_tok, axis=(0, 1))
    g_w_tok1 = jnp.einsum('bsc,bcj->sj', normed, d_hid_tok_bf, preferred_element_type=jnp.float32)
    d_normed = jnp.einsum('bcj,sj->bsc', d_hid_tok_bf, w_tok1, preferred_element_type=jnp.float32)
    d_in_ln, g_ln1_g, g_ln1_b = norm_grad(x_in, ln1_g, ln1_b, d_normed)
    d_in = d_in_ln + d_after
    pad_len = flat.shape[0] - layer_length(num_tokens, num_chans)
    flat_grad = jnp.concatenate([g_w_tok1.reshape(-1), g_w_tok2.reshape(-1), g_w_ch1.reshape(-1), g_w_ch2.reshape(-1), g_ln1_g, g_ln1_b, g_b_tok1, g_b_tok2, g_ln2_g, g_ln2_b, g_b_ch1, g_b_ch2, jnp.zeros((pad_len,), jnp.float32)])
    return d_in, flat_grad


def head_step(hidden, labels, small_full, head_full, global_b):
    num_tokens = hidden.shape[1]
    num_chans = hidden.shape[2]
    num_classes = head_full.shape[1]
    lnf_g = small_full[:num_chans]
    lnf_b = small_full[num_chans:2 * num_chans]
    head_b = small_full[2 * num_chans:2 * num_chans + num_classes]
    normed = layer_norm(hidden, lnf_g, lnf_b)
    pooled = (jnp.sum(normed, axis=1, dtype=jnp.float32) / num_tokens).astype(jnp.bfloat16)
    logits = jnp.dot(pooled, head_full, preferred_element_type=jnp.float32) + head_b.astype(jnp.float32)
    log_norm = jax.nn.logsumexp(logits, axis=-1)
    is_label = jnp.arange(num_classes)[None, :] == labels[:, None]
    picked = jnp.sum(jnp.where(is_label, logits, 0.0), axis=-1)
    loss_sum = jnp.sum(log_norm - picked)
    d_logits = (jnp.exp(logits - log_norm[:, None]) - is_label.astype(jnp.float32)) / global_b
    d_logits_bf = d_logits.astype(jnp.bfloat16)
    g_head_b = jnp.sum(d_logits, axis=0)
    g_head_w = jnp.einsum('bc,bk->ck', pooled, d_logits_bf, preferred_element_type=jnp.float32)
    d_pooled = jnp.einsum('bk,ck->bc', d_logits_bf, head_full, preferred_element_type=jnp.float32)
    d_normed = jnp.broadcast_to((d_pooled / num_tokens)[:, None, :], normed.shape)
    d_hidden, g_lnf_g, g_lnf_b = norm_grad(hidden, lnf_g, lnf_b, d_normed)
    g_small = jnp.concatenate([g_lnf_g, g_lnf_b, g_head_b])
    return loss_sum, d_hidden, g_head_w, g_small


def adam_update(master, gradient, moment, second, decay_rate):
    moment_new = BETA_ONE * moment + (1.0 - BETA_ONE) * gradient
    second_new = BETA_TWO * second + (1.0 - BETA_TWO) * gradient * gradient
    m_hat = moment_new / (1.0 - BETA_ONE ** ADAM_STEP)
    v_hat = second_new / (1.0 - BETA_TWO ** ADAM_STEP)
    master_new = master - LEARN_RATE * (m_hat / (jnp.sqrt(v_hat) + ADAM_EPS) + decay_rate * master)
    return master_new, moment_new, second_new


def solution(mesh):
    group = mesh.shape['fsdp']
    row_spec = P('fsdp')
    layer_spec = P(None, 'fsdp')
    in_specs = (row_spec, row_spec, layer_spec, row_spec, row_spec, layer_spec, row_spec, row_spec, layer_spec, row_spec, row_spec)
    out_specs = (P(),) + in_specs[2:]

    def device_step(act_in, labels, layer_p, head_w, small_p, layer_m, head_m, small_m, layer_v, head_v, small_v):
        local_b, num_tokens, num_chans = act_in.shape
        global_b = local_b * group
        num_layers = layer_p.shape[0]
        mat_len = 2 * num_tokens * (num_chans // 2) + 8 * num_chans * num_chans
        caches = []
        hidden = act_in
        for layer_idx in range(num_layers):
            flat_full = lax.all_gather(layer_p[layer_idx].astype(jnp.bfloat16), 'fsdp', tiled=True)
            hidden, cache = layer_forward(hidden, flat_full, num_tokens, num_chans)
            caches.append(cache)
        small_full = lax.all_gather(small_p.astype(jnp.bfloat16), 'fsdp', tiled=True)
        head_full = lax.all_gather(head_w.astype(jnp.bfloat16), 'fsdp', tiled=True)
        loss_sum, d_hidden, g_head_w, g_small = head_step(hidden, labels, small_full, head_full, global_b)
        layer_shards = [None] * num_layers
        for layer_idx in reversed(range(num_layers)):
            flat_full = lax.all_gather(layer_p[layer_idx].astype(jnp.bfloat16), 'fsdp', tiled=True)
            d_hidden, flat_grad = layer_backward(d_hidden, flat_full, caches[layer_idx], num_tokens, num_chans)
            layer_shards[layer_idx] = lax.psum_scatter(flat_grad, 'fsdp', scatter_dimension=0, tiled=True)
        layer_g = jnp.stack(layer_shards)
        head_g = lax.psum_scatter(g_head_w, 'fsdp', scatter_dimension=0, tiled=True)
        small_flat = jnp.concatenate([g_small, jnp.zeros((small_full.shape[0] - g_small.shape[0],), jnp.float32)])
        small_g = lax.psum_scatter(small_flat, 'fsdp', scatter_dimension=0, tiled=True)
        loss_value = lax.psum(loss_sum, 'fsdp') / global_b
        sq_local = jnp.sum(jnp.square(layer_g)) + jnp.sum(jnp.square(head_g)) + jnp.sum(jnp.square(small_g))
        grad_norm = jnp.sqrt(lax.psum(sq_local, 'fsdp'))
        clip_scale = 1.0 / jnp.maximum(1.0, grad_norm)
        shard_len = layer_p.shape[1]
        flat_pos = lax.axis_index('fsdp') * shard_len + jnp.arange(shard_len)
        layer_decay = jnp.where(flat_pos < mat_len, WEIGHT_DECAY, 0.0)[None, :]
        new_lp, new_lm, new_lv = adam_update(layer_p, layer_g * clip_scale, layer_m, layer_v, layer_decay)
        new_hw, new_hm, new_hv = adam_update(head_w, head_g * clip_scale, head_m, head_v, WEIGHT_DECAY)
        new_sp, new_sm, new_sv = adam_update(small_p, small_g * clip_scale, small_m, small_v, 0.0)
        return (loss_value, new_lp, new_hw, new_sp, new_lm, new_hm, new_sm, new_lv, new_hv, new_sv)

    return jax.shard_map(device_step, mesh=mesh, in_specs=in_specs, out_specs=out_specs, check_vma=False)
```

profile of v0, /device:TPU:0, one launch (start us, length us, event | category | flops | bytes accessed | tf_op | source)
XLA Modules:
  0.0 4718.9 jit_solution(3348669922905987282)
XLA Ops:
  80.8 102.2 %all-gather.10.cloned.1.call-done = bf16[1,8599552]{1,0:T(2,128)(2,1)} async-done(((bf16[1,1074944]{1,0:T(2,128)(2,1)}), bf16[1,8599552]{1,0:T(2,128)(2,1)}) %all-gather.10.cloned.1.call-update) | async-done | bytes 17199120 | tf_op jit(solution)/shard_map/all_gather | solution.py:153
  183.0 184.5 %slice_reduce_fusion = (bf16[4194304]{0:T(1024)(128)(2,1)}, bf16[4194304]{0:T(1024)(128)(2,1)}) fusion(bf16[1,8599552]{1,0:T(2,128)(2,1)} %all-gather.10.cloned.1.call-done), kind=kLoop, calls=%fused_computation.178 | loop fusion | bytes 33554432 | tf_op jit(solution)/shard_map/slice | solution.py:31
  385.2 184.6 %slice_reduce_fusion.2 = (bf16[4194304]{0:T(1024)(128)(2,1)}, bf16[4194304]{0:T(1024)(128)(2,1)}) fusion(bf16[1,8599552]{1,0:T(2,128)(2,1)} %all-gather.8.cloned.1.call-done), kind=kLoop, calls=%fused_computation.180 | loop fusion | bytes 33554432 | tf_op jit(solution)/shard_map/slice | solution.py:31
  622.3 51.9 %multiply_convert_fusion.3 = (bf16[32,1024,512]{2,1,0:T(8,128)(2,1)}, f32[32,1024,512]{2,1,0:T(8,128)}) fusion(f32[512]{0:T(512)S(1)} %bitcast.172, bf16[196,512,1]{1,0,2:T(8,128)(2,1)S(1)} %reshape.352, f32[1024]{0:T(1024)S(1)} %bitcast.160, f32[1024]{0:T(1024)S(1)} %bitcast.162, f32[32,196]{1,0:T(8,128)S(1)} %add_rsqrt_fusion, ...), kind=kOutput, calls=%fused_computation.55 | convolution fusion | flops 6782976000 | bytes 113769472 | tf_op jit(solution)/shard_map/bsc,sj->bcj/dot_general | solution.py:62
  716.3 90.1 %multiply_convert_fusion.1 = (bf16[32,196,4096]{2,1,0:T(8,128)(2,1)}, f32[32,196,4096]{2,1,0:T(8,128)}) fusion(f32[4096]{0:T(1024)S(1)} %bitcast.156, bf16[1024,4096,1]{1,0,2:T(8,128)(2,1)} %reshape.354, bf16[32,196,1024]{2,1,0:T(8,128)(2,1)} %get-tuple-element.72, f32[1024]{0:T(1024)S(1)} %bitcast.164, f32[1024]{0:T(1024)S(1)} %bitcast.144, ...), kind=kOutput, calls=%fused_computation.27 | convolution fusion | flops 52908785664 | bytes 175449088 | tf_op jit(solution)/shard_map/bsc,cd->bsd/dot_general | solution.py:67
  806.5 64.0 %convert_reduce_fusion.3 = (f32[32,196]{1,0:T(8,128)S(1)}, bf16[32,196,1024]{2,1,0:T(8,128)(2,1)}) fusion(f32[1024]{0:T(1024)S(1)} %bitcast.171, bf16[32,196,4096]{2,1,0:T(8,128)(2,1)} %get-tuple-element.73, bf16[4096,1024,1]{1,0,2:T(8,128)(2,1)} %reshape.355, bf16[32,196,1024]{2,1,0:T(8,128)(2,1)} %get-tuple-element.72), kind=kOutput, calls=%fused_computation.71 | convolution fusion | flops 52651876352 | bytes 85488128 | tf_op jit(solution)/shard_map/bsd,dc->bsc/dot_general | solution.py:69
  879.1 43.5 multiply_convert_fusion.2
  954.5 89.6 %multiply_convert_fusion = (bf16[32,196,4096]{2,1,0:T(8,128)(2,1)}, f32[32,196,4096]{2,1,0:T(8,128)}) fusion(f32[4096]{0:T(1024)S(1)} %bitcast.158, bf16[1024,4096,1]{1,0,2:T(8,128)(2,1)} %reshape.358, bf16[32,196,1024]{2,1,0:T(8,128)(2,1)} %get-tuple-element.80, f32[1024]{0:T(1024)S(1)} %bitcast.168, f32[1024]{0:T(1024)S(1)} %bitcast.152, ...), kind=kOutput, calls=%fused_computation.26 | convolution fusion | flops 52908785664 | bytes 175449088 | tf_op jit(solution)/shard_map/bsc,cd->bsd/dot_general | solution.py:67
  1044.1 64.0 %convert_reduce_fusion.9 = (f32[32,196]{1,0:T(8,128)S(1)}, bf16[32,196,1024]{2,1,0:T(8,128)(2,1)}) fusion(f32[1024]{0:T(1024)S(1)} %bitcast.170, bf16[32,196,4096]{2,1,0:T(8,128)(2,1)} %get-tuple-element.81, bf16[4096,1024,1]{1,0,2:T(8,128)(2,1)} %reshape.359, bf16[32,196,1024]{2,1,0:T(8,128)(2,1)} %get-tuple-element.80), kind=kOutput, calls=%fused_computation.99 | convolution fusion | flops 52651876352 | bytes 85488128 | tf_op jit(solution)/shard_map/bsd,dc->bsc/dot_general | solution.py:69
  1179.5 127.6 %fusion.217 = (f32[4096]{0:T(1024)}, bf16[32,196,4096]{2,1,0:T(8,128)(2,1)}) fusion(f32[32,196,4096]{2,1,0:T(8,128)} %get-tuple-element.82, f32[4096]{0:T(1024)S(1)} %bitcast.159, bf16[4096,1024,1]{1,0,2:T(8,128)(2,1)} %reshape.359, bf16[32,196,1024]{2,1,0:T(8,128)(2,1)} %get-tuple-element.84, f32[32,196]{1,0:T(8,128)S(1)} %add_multiply_fusion.3, ...), kind=kOutput, calls=%fused_computation.296 | convolution fusion | flops 53281288192 | bytes 175642624 | tf_op jit(solution)/shard_map/bsc,dc->bsd/dot_general | solution.py:80
  1307.2 70.0 %fusion.111 = (f32[1024]{0:T(1024)}, f32[32,196]{1,0:T(8,128)S(1)}, f32[32,196]{1,0:T(8,128)S(1)}, f32[1024]{0:T(1024)}, bf16[32,196,1024]{2,1,0:T(8,128)(2,1)}) fusion(bf16[32,196,1024]{2,1,0:T(8,128)(2,1)} %get-tuple-element.80, f32[32,196]{1,0:T(8,128)S(1)} %copy-done.51, f32[32,196]{1,0:T(8,128)S(1)} %copy-done.24, f32[1024]{0:T(1024)S(1)} %bitcast.153, ...), kind=kOutput, calls=%fused_computation.159 | convolution fusion | flops 52696825856 | bytes 85571584 | tf_op jit(solution)/shard_map/bsd,cd->bsc/dot_general | solution.py:85
  1377.3 68.6 %fusion.147 = f32[128,32,8,128]{3,2,1,0:T(8,128)} fusion(bf16[32,196,4096]{2,1,0:T(8,128)(2,1)} %get-tuple-element.92, bf16[32,196,1024]{2,1,0:T(8,128)(2,1)} %get-tuple-element.80, f32[1024]{0:T(1024)S(1)} %bitcast.169, f32[1024]{0:T(1024)S(1)} %bitcast.154, f32[32,196]{1,0:T(8,128)S(1)} %copy-done.51, f32[32,196]{1,0:T(8,128)S(1)} %copy-done.24), kind=kOutput, calls=%fused_computation.207 | convolution fusion | flops 52651884544 | bytes 81060864 | tf_op jit(solution)/shard_map/bsc,bsd->cd/dot_general | solution.py:84
  1445.9 70.3 %convolution_bitcast_fusion = f32[512,8,8,128]{3,2,1,0:T(8,128)} fusion(bf16[32,196,4096]{2,1,0:T(8,128)(2,1)} %get-tuple-element.81, bf16[32,196,1024]{2,1,0:T(8,128)(2,1)} %get-tuple-element.84, f32[32,196]{1,0:T(8,128)S(1)} %copy-done.19, f32[32,196]{1,0:T(8,128)S(1)} %copy-done.15, f32[32,1024]{1,0:T(8,128)S(1)} %copy-done.7, f32[1024]{0:T(1024)S(1)} %copy-done.43, ...), kind=kOutput, calls=%fused_computation.205 | convolution fusion | flops 52664729600 | bytes 81238016 | tf_op jit(solution)/shard_map/bsd,bsc->dc/dot_general | solution.py:79
  1568.6 68.2 %fusion.216 = (f32[512]{0:T(512)}, bf16[32,1024,512]{2,1,0:T(8,128)(2,1)}) fusion(f32[32,1024,512]{2,1,0:T(8,128)} %get-tuple-element.78, f32[512]{0:T(512)S(1)} %bitcast.175, bf16[512,196]{1,0:T(8,128)(2,1)S(1)} %copy-done.37, bf16[32,196,1024]{2,1,0:T(8,128)(2,1)} %get-tuple-element.54, f32[32,196]{1,0:T(8,128)S(1)} %copy-done.19, ...), kind=kOutput, calls=%fused_computation.295 | convolution fusion | flops 7056391680 | bytes 126793728 | tf_op jit(solution)/shard_map/bsc,js->bcj/dot_general | solution.py:91
  1718.4 124.3 %fusion.219 = (f32[4096]{0:T(1024)}, bf16[32,196,4096]{2,1,0:T(8,128)(2,1)}) fusion(f32[32,196,4096]{2,1,0:T(8,128)} %get-tuple-element.74, f32[4096]{0:T(1024)S(1)} %bitcast.157, bf16[4096,1024,1]{1,0,2:T(8,128)(2,1)} %reshape.355, f32[32,196,1024]{2,1,0:T(8,128)} %convert_add_fusion.6), kind=kOutput, calls=%fused_computation.298 | convolution fusion | flops 53236330496 | bytes 188252160 | tf_op jit(solution)/shard_map/bsc,dc->bsd/dot_general | solution.py:80
  1842.7 69.8 %fusion.112 = (f32[1024]{0:T(1024)}, f32[32,196]{1,0:T(8,128)S(1)}, f32[32,196]{1,0:T(8,128)S(1)}, f32[1024]{0:T(1024)}, bf16[32,196,1024]{2,1,0:T(8,128)(2,1)}) fusion(bf16[32,196,1024]{2,1,0:T(8,128)(2,1)} %get-tuple-element.72, f32[32,196]{1,0:T(8,128)S(1)} %copy-done.49, f32[32,196]{1,0:T(8,128)S(1)} %copy-done.21, f32[1024]{0:T(1024)S(1)} %bitcast.145, ...), kind=kOutput, calls=%fused_computation.160 | convolution fusion | flops 52696825856 | bytes 85571584 | tf_op jit(solution)/shard_map/bsd,cd->bsc/dot_general | solution.py:85
  1912.5 68.3 %fusion.150 = f32[128,32,8,128]{3,2,1,0:T(8,128)} fusion(bf16[32,196,4096]{2,1,0:T(8,128)(2,1)} %get-tuple-element.99, bf16[32,196,1024]{2,1,0:T(8,128)(2,1)} %get-tuple-element.72, f32[1024]{0:T(1024)S(1)} %bitcast.165, f32[1024]{0:T(1024)S(1)} %bitcast.146, f32[32,196]{1,0:T(8,128)S(1)} %copy-done.49, f32[32,196]{1,0:T(8,128)S(1)} %copy-done.21), kind=kOutput, calls=%fused_computation.208 | convolution fusion | flops 52651884544 | bytes 81060864 | tf_op jit(solution)/shard_map/bsc,bsd->cd/dot_general | solution.py:84
  1980.8 67.6 %convolution_bitcast_fusion.1 = f32[512,8,8,128]{3,2,1,0:T(8,128)} fusion(bf16[32,196,4096]{2,1,0:T(8,128)(2,1)} %get-tuple-element.73, f32[32,196,1024]{2,1,0:T(8,128)} %convert_add_fusion.6), kind=kOutput, calls=%fused_computation.206 | convolution fusion | flops 52619771904 | bytes 93847552 | tf_op jit(solution)/shard_map/bsd,bsc->dc/dot_general | solution.py:79
  2106.4 71.2 %fusion.218 = (f32[512]{0:T(512)S(1)}, bf16[32,1024,512]{2,1,0:T(8,128)(2,1)}) fusion(f32[32,1024,512]{2,1,0:T(8,128)} %get-tuple-element.70, f32[512]{0:T(512)S(1)} %bitcast.173, bf16[512,196]{1,0:T(8,128)(2,1)S(1)} %copy-done.35, f32[32,196,1024]{2,1,0:T(8,128)} %convert_add_fusion.6, bf16[32,196,1024]{2,1,0:T(8,128)(2,1)} %get-tuple-element.53), kind=kOutput, calls=%fused_computation.297 | convolution fusion | flops 6998588928 | bytes 139403264 | tf_op jit(solution)/shard_map/bsc,js->bcj/dot_general | solution.py:91
  2320.2 265.1 %concatenate.10 = f32[8599552]{0:T(1024)} concatenate(f32[100352]{0:T(1024)S(1)} %reshape.298, f32[100352]{0:T(1024)S(1)} %reshape.299, f32[4194304]{0:T(1024)} %bitcast.142, f32[4194304]{0:T(1024)} %bitcast.143, f32[1024]{0:T(1024)S(1)} %copy-done.82, f32[1024]{0:T(1024)S(1)} %copy-done.57, f32[512]{0:T(512)S(1)} %copy-done.99, f32[196]{0:T(256)S(1)} %copy-done.97, ...), dimensions={0} | concatenate | bytes 68796416 | tf_op jit(solution)/shard_map/concatenate | solution.py:100
  2585.3 265.0 %concatenate.9 = f32[8599552]{0:T(1024)} concatenate(f32[100352]{0:T(1024)S(1)} %reshape.294, f32[100352]{0:T(1024)S(1)} %reshape.295, f32[4194304]{0:T(1024)} %bitcast.140, f32[4194304]{0:T(1024)} %bitcast.141, f32[1024]{0:T(1024)S(1)} %get-tuple-element.94, f32[1024]{0:T(1024)S(1)} %convert_reduce_fusion.6, f32[512]{0:T(512)S(1)} %get-tuple-element.96, f32[196]{0:T(256)S(1)} %copy-done.98, ...), dimensions={0} | concatenate | bytes 68796416 | tf_op jit(solution)/shard_map/concatenate | solution.py:100
  2885.6 731.3 %all-reduce.11.cloned.1.call-done = (f32[8599552]{0:T(1024)}, f32[8599552]{0:T(1024)}, f32[24576]{0:T(1024)}) async-done(((f32[8599552]{0:T(1024)}, f32[8599552]{0:T(1024)}, f32[24576]{0:T(1024)}), (f32[8599552]{0:T(1024)}, f32[8599552]{0:T(1024)}, f32[24576]{0:T(1024)})) %all-reduce.11.cloned.1.call-update) | async-done | bytes 68894736
  3676.4 930.3 %all-reduce.9.cloned.1.call-done = f32[1024,21843]{0,1:T(8,128)} async-done(((f32[1024,21843]{0,1:T(8,128)}), f32[1024,21843]{0,1:T(8,128)}) %all-reduce.9.cloned.1.call-update) | async-done | bytes 89468944
  4643.0 38.7 multiply_subtract_fusion.1
  (323 shorter events, 788.1 us)
Async XLA Ops:
  7.2 175.8 %all-gather.10.cloned.1.call-start = ((), (), s32[]{:S(2)}) async-start(), calls=%async_computation.2 | async-start | bytes 38697984 | tf_op jit(solution)/shard_map/all_gather | solution.py:153
  19.4 365.8 %all-gather.8.cloned.1.call-start = ((), (), s32[]{:S(2)}) async-start(), calls=%async_computation.1 | async-start | bytes 38697984 | tf_op jit(solution)/shard_map/all_gather | solution.py:153
  20.1 1104.4 %all-gather.6.cloned.1.call-start = ((), (), s32[]{:S(2)}) async-start(), calls=%async_computation | async-start | bytes 50337792 | tf_op jit(solution)/shard_map/all_gather | solution.py:157
  27.5 3589.3 %all-reduce.11.cloned.1.call-start = ((), (), s32[]{:S(2)}) async-start(), calls=%async_computation.4 | async-start | bytes 137789440
  61.6 560.7 %copy-start.46 = (f32[32,196]{1,0:T(8,128)}, f32[32,196]{1,0:T(8,128)S(1)}, u32[]{:S(2)}) copy-start(f32[32,196]{1,0:T(8,128)S(1)} %broadcast_multiply_fusion.4) | copy-start | bytes 75268
  80.8 541.5 %copy-start.54 = (f32[32,196]{1,0:T(8,128)}, f32[32,196]{1,0:T(8,128)S(1)}, u32[]{:S(2)}) copy-start(f32[32,196]{1,0:T(8,128)S(1)} %add_rsqrt_fusion) | copy-start | bytes 75268
  1164.2 143.0 %copy-start.6 = (f32[32,1024]{1,0:T(8,128)}, f32[32,1024]{1,0:T(8,128)S(1)}, u32[]{:S(2)}) copy-start(f32[32,1024]{1,0:T(8,128)S(1)} %fusion.187) | copy-start | bytes 393220
  1172.4 134.7 %copy-start.14 = (f32[32,196]{1,0:T(8,128)}, f32[32,196]{1,0:T(8,128)S(1)}, u32[]{:S(2)}) copy-start(f32[32,196]{1,0:T(8,128)S(1)} %multiply_multiply_fusion.15) | copy-start | bytes 75268
  1179.5 127.7 %copy-start.18 = (f32[32,196]{1,0:T(8,128)}, f32[32,196]{1,0:T(8,128)S(1)}, u32[]{:S(2)}) copy-start(f32[32,196]{1,0:T(8,128)S(1)} %add_multiply_fusion.3) | copy-start | bytes 75268
  1179.5 127.7 %copy-start.24 = (f32[32,196]{1,0:T(8,128)S(1)}, f32[32,196]{1,0:T(8,128)}, u32[]{:S(2)}) copy-start(f32[32,196]{1,0:T(8,128)} %copy-done.23) | copy-start | bytes 75268
  1179.5 127.7 %copy-start.51 = (f32[32,196]{1,0:T(8,128)S(1)}, f32[32,196]{1,0:T(8,128)}, u32[]{:S(2)}) copy-start(f32[32,196]{1,0:T(8,128)} %copy-done.50) | copy-start | bytes 75268
  1179.5 127.7 %copy-start.66 = (f32[1,1024]{1,0:T(1,128)S(1)}, f32[1,1024]{1,0:T(1,128)}, u32[]{:S(2)}) copy-start(f32[1,1024]{1,0:T(1,128)} %get-tuple-element.57) | copy-start | bytes 12292
  1718.4 124.3 %copy-start.21 = (f32[32,196]{1,0:T(8,128)S(1)}, f32[32,196]{1,0:T(8,128)}, u32[]{:S(2)}) copy-start(f32[32,196]{1,0:T(8,128)} %copy-done.20) | copy-start | bytes 75268
  1718.4 124.3 %copy-start.49 = (f32[32,196]{1,0:T(8,128)S(1)}, f32[32,196]{1,0:T(8,128)}, u32[]{:S(2)}) copy-start(f32[32,196]{1,0:T(8,128)} %copy-done.48) | copy-start | bytes 75268
  1718.4 124.3 %copy-start.60 = (f32[1,1024]{1,0:T(1,128)S(1)}, f32[1,1024]{1,0:T(1,128)}, u32[]{:S(2)}) copy-start(f32[1,1024]{1,0:T(1,128)} %copy-done.59) | copy-start | bytes 12292
  2320.1 265.2 %copy-start.58 = (f32[1024]{0:T(1024)S(1)}, f32[1024]{0:T(1024)}, u32[]{:S(2)}) copy-start(f32[1024]{0:T(1024)} %get-tuple-element.24) | copy-start | bytes 12292
  2320.1 265.2 %copy-start.73 = (f32[4096]{0:T(1024)S(1)}, f32[4096]{0:T(1024)}, u32[]{:S(2)}) copy-start(f32[4096]{0:T(1024)} %get-tuple-element.98) | copy-start | bytes 49156
  2320.1 265.2 %copy-start.83 = (f32[1024]{0:T(1024)S(1)}, f32[1024]{0:T(1024)}, u32[]{:S(2)}) copy-start(f32[1024]{0:T(1024)} %get-tuple-element.18) | copy-start | bytes 12292
  2320.1 265.2 %copy-start.84 = (f32[1024]{0:T(1024)S(1)}, f32[1024]{0:T(1024)}, u32[]{:S(2)}) copy-start(f32[1024]{0:T(1024)} %get-tuple-element.32) | copy-start | bytes 12292
  2320.1 265.1 %copy-start.98 = (f32[196]{0:T(256)S(1)}, f32[196]{0:T(256)}, u32[]{:S(2)}) copy-start(f32[196]{0:T(256)} %get-tuple-element.25) | copy-start | bytes 2356
  2850.4 1756.3 %all-reduce.9.cloned.1.call-start = ((), (), s32[]{:S(2)}) async-start(), calls=%async_computation.3 | async-start | bytes 178978816
  3619.8 1021.9 %copy-start.53 = (f32[3072]{0:T(1024)S(1)}, f32[3072]{0:T(1024)}, u32[]{:S(2)}) copy-start(f32[3072]{0:T(1024)} %param.15) | copy-start | bytes 36868
  3619.8 1021.9 %copy-start.74 = (f32[3072]{0:T(1024)S(1)}, f32[3072]{0:T(1024)}, u32[]{:S(2)}) copy-start(f32[3072]{0:T(1024)} %param.18) | copy-start | bytes 36868
  3619.8 1021.9 %copy-start.75 = (f32[3072]{0:T(1024)S(1)}, f32[3072]{0:T(1024)}, u32[]{:S(2)}) copy-start(f32[3072]{0:T(1024)} %param.21) | copy-start | bytes 36868
  (87 other events, 4231.5 us)
Sparse Core Ops, SparseCore 0:
  19.5 163.4 all-gather.9
  185.4 159.9 all-gather.7
  347.9 212.1 all-gather.5
  2850.5 766.3 all-reduce.10
  3620.4 986.1 all-reduce.8
where the time goes:
time: 4770 us; the launch traced here: 4720 us
  waiting for transfers between devices  1760 us (37%)
  matrix products  1480 us (31%)
  local copies, waits for them, and re-layouts  1080 us (23%)
  other arithmetic  341 us (7%)
    unnamed x7, waiting for transfers between devices  1660 us
    concatenate x2, local copies, waits for them, and re-layouts, layer_backward(): jnp.concatenate([g_w_tok1.reshape(-1), g_w_tok2.reshape(-1), g_w_ch1.resh...  530 us
    slice x8, local copies, waits for them, and re-layouts, unpack_layer(): pieces.append(flat[piece_start:piece_start + piece_len].reshape(shape_one))  403 us
    dot_general x2, matrix products, layer_backward(): jnp.einsum('bsc,dc->bsd', d_out_bf, w_ch2, preferred_element_type=jnp.flo...  252 us
    dot_general x2, matrix products, layer_forward(): jnp.einsum('bsc,cd->bsd', normed2, w_ch1, preferred_element_type=jnp.floa...  180 us
    dot_general x2, matrix products, layer_backward(): jnp.einsum('bsd,cd->bsc', d_hid_ch_bf, w_ch1, preferred_element_type=jnp....  140 us
    dot_general x2, matrix products, layer_backward(): jnp.einsum('bsc,js->bcj', d_after_bf, w_tok2, preferred_element_type=jnp....  139 us
    dot_general x2, matrix products, layer_backward(): jnp.einsum('bsd,bsc->dc', act_ch, d_out_bf, preferred_element_type=jnp.fl...  138 us
  transfers between devices with their start and end apart: 5, of which 3 were waited for; matrix products, arithmetic and copies ran while one was open for 23% of the time, Pallas kernels for 0%

commit v1 on v0

v1 whole, which is shorter than its diff:
```python
import functools
import math
import jax
import jax.numpy as jnp
from jax import lax
from jax.experimental import pallas as pl
from jax.experimental.pallas import tpu as pltpu
from jax.experimental.layout import with_layout_constraint, Layout
from jax.sharding import PartitionSpec as P


F32 = jnp.float32
BF = jnp.bfloat16
LN_EPS = 1e-6
LEARN_RATE = 0.003
BETA_ONE = 0.9
BETA_TWO = 0.999
ADAM_EPS = 1e-8
WEIGHT_DECAY = 0.03
ADAM_STEP = 10
GC0 = math.sqrt(2 / math.pi)
GC1 = GC0 * 0.044715

LANE = 128
SUB = 8
ND = 8
AX = 'fsdp'
B = 32
S = 196
SP = 200
C = 1024
J = 512
D = 4096
NCLS = 21843
NIMG = 256
T = B * SP
KC = 2816
KR = KC // LANE
RSH = 8398
TOKR = 1568
HTOK = TOKR // 2
UNIT = 512
NU = 16
UR = UNIT * NU
STEPR = RSH - UR
SPILL = TOKR - STEPR
SPR = SPILL + 6
MATR = TOKR + ND * UR
SMR = 80
GROWS = RSH + SPILL + SUB
TP = 208
SMF = 192
SMD = SMF // ND
VROW = 16
VLIM = 64 * 1024 * 1024 - 65536
NT = (((1,), (1,)), ((), ()))
TN = (((0,), (0,)), ((), ()))
VM = pl.BlockSpec(memory_space=pltpu.VMEM)
HBM = pl.BlockSpec(memory_space=pl.ANY)
SMEM = pl.BlockSpec(memory_space=pltpu.SMEM)
SEM = pltpu.SemaphoreType.DMA
VG1, VS1, VG2, VS2, VB2, VB1, VLG, VLS = 0, 1, 2, 3, 4, 5, 9, 10


ZERO, ONE, TWO, THREE, FOUR, TEN = 0, 1, 2, 3, 4, 10


def sds(shape, dt):
    return jax.ShapeDtypeStruct(shape, dt)


def fixed(shape, idx=None, once=False):
    ix = tuple(idx) if idx else (0,) * len(shape)
    return pl.BlockSpec(shape, lambda i: ix, pipeline_mode=pl.Buffered(1) if once else None)


def run(body, ins, in_specs, outs, out_specs, scratch=(), grid=None, flops=10**9, nbytes=10**6, alias={}, cid=None, vlim=VLIM):
    kw = dict(vmem_limit_bytes=vlim)
    if cid is not None:
        kw.update(collective_id=cid, has_side_effects=True)
    if grid:
        kw.update(dimension_semantics=("arbitrary",))
    extra = dict(grid=(grid,)) if grid else {}
    return pl.pallas_call(body, in_specs=in_specs, out_specs=out_specs, out_shape=outs, scratch_shapes=list(scratch),
        input_output_aliases=alias, cost_estimate=pl.CostEstimate(flops=flops, bytes_accessed=nbytes, transcendentals=0),
        compiler_params=pltpu.CompilerParams(**kw), **extra)(*ins)


def on(cond):
    return pl.when(cond)


def unit_stats(xf):
    mean = jnp.sum(xf, axis=-ONE, keepdims=True) * (1.0 / C)
    xc = xf - mean
    rstd = lax.rsqrt(jnp.sum(xc * xc, axis=-ONE, keepdims=True) * (1.0 / C) + LN_EPS)
    return xc * rstd, rstd


def sum8(v):
    return jnp.sum(v.reshape(v.shape[ZERO] // SUB, SUB, v.shape[ONE]), axis=ZERO)


def ln_bwd(nh, rstd, dy, g):
    dxh = dy * g
    m1 = jnp.sum(dxh, axis=-ONE, keepdims=True) * (1.0 / C)
    m2 = jnp.sum(dxh * nh, axis=-ONE, keepdims=True) * (1.0 / C)
    return rstd * (dxh - m1 - nh * m2)


def gelu_both(h):
    u = h * h
    t = jnp.tanh(h * (GC0 + GC1 * u))
    cdf = 0.5 + 0.5 * t
    a = h * cdf
    return a.astype(BF), cdf + (a * (1.0 - t)) * (GC0 + (THREE * GC1) * u)


def wcols(w_ref, c0, n):
    r = w_ref.shape[ZERO] * 16
    return jnp.concatenate([w_ref[:, j].reshape(r, LANE) for j in range(c0 // LANE, (c0 + n) // LANE)], axis=ONE)


def wrows(w_ref, r0, n):
    return jnp.concatenate([w_ref[r0 // 16:(r0 + n) // 16, j].reshape(n, LANE) for j in range(w_ref.shape[ONE])], axis=ONE)


def dot(a, b):
    return jnp.dot(a, b, preferred_element_type=F32)


def dotg(a, b, dn):
    return lax.dot_general(a, b, dn, preferred_element_type=F32)


def entry_barrier():
    me = lax.axis_index(AX)
    b = pltpu.get_barrier_semaphore()
    for d in range(ONE, ND):
        pl.semaphore_signal(b, inc=ONE, device_id=(lax.rem(me + d, ND),), device_id_type=pl.DeviceIdType.MESH)
    pl.semaphore_wait(b, ND - ONE)
    return me


def rcopy(src, dst, ss, rs, dev):
    return pltpu.make_async_remote_copy(src_ref=src, dst_ref=dst, send_sem=ss, recv_sem=rs, device_id=(dev,), device_id_type=pl.DeviceIdType.MESH)


def ag_all(me, src, dst, ss, rs):
    cs = []
    for d in range(ONE, ND):
        c = rcopy(src, dst.at[me], ss.at[d], rs.at[d], lax.rem(me + d, ND))
        c.start()
        cs.append(c)
    return cs


def wait_all(cs):
    for c in cs:
        c.wait()


def rows3(a):
    b = with_layout_constraint(a.reshape(TWO, RSH, LANE), Layout(major_to_minor=(ONE, ZERO, TWO)))
    return b.transpose(ONE, ZERO, TWO)


def unrows3(a):
    b = with_layout_constraint(a.transpose(ONE, ZERO, TWO), Layout(major_to_minor=(ONE, ZERO, TWO)))
    return b.reshape(TWO, RSH * LANE)


def start_kernel(p_ref, misc_ref, o0_ref, o1_ref, tok_o, sm_o, misc_o, buf, shs, shr, toks, sms, ds1, ds2, ss_m, rs_m, ss_s, rs_s, ss_t, rs_t, ss_u, ss_h, rs_h):
    c1 = pltpu.make_async_copy(p_ref.at[:TOKR], buf.at[:TOKR], ds1)
    c1.start()
    c2 = pltpu.make_async_copy(p_ref.at[TOKR:], buf.at[TOKR:RSH], ds2)
    c2.start()
    me = entry_barrier()
    csm = ag_all(me, misc_ref, misc_o, ss_m, rs_m)
    misc_o[me] = misc_ref[:]
    c1.wait()
    shs[:] = buf[:SPILL].astype(BF)
    sh = rcopy(shs, shr, ss_h, rs_h, lax.rem(me + ND - ONE, ND))
    sh.start()
    q4 = TOKR // FOUR

    def first_send(d):
        return rcopy(toks.at[d], tok_o.at[d], ss_t.at[d], rs_t.at[d], d)

    def zero_send(d):
        return rcopy(toks.at[ZERO], tok_o.at[ZERO], ss_u.at[d], rs_t.at[ZERO], d)

    def piece(q, d):
        return rcopy(tok_o.at[q], tok_o.at[q], ss_t.at[d], rs_t.at[q], lax.rem(me - ONE + d, ND - ONE) + ONE)

    def small(d):
        return rcopy(sms, sm_o, ss_s.at[d], rs_s, d)

    @on(me == ZERO)
    def _():
        for l in range(TWO):
            for q in range(FOUR):
                toks[FOUR * l + q] = buf[q4 * q:q4 * (q + ONE), l, :].astype(BF)
        for d in range(ONE, ND):
            first_send(d).start()
        for d in range(ONE, ND):
            zero_send(d).start()
        tok_o[:] = toks[:]

    c2.wait()

    @on(me == ND - ONE)
    def _():
        for l in range(TWO):
            sms[l] = buf[RSH - SMR:RSH, l, :].astype(BF)
        for d in range(ND - ONE):
            small(d).start()
        sm_o[:] = sms[:]

    off = TOKR - STEPR * me

    def go(o_ref, l, nj, a, b):
        n = UNIT // nj // 16

        def step(i, _):
            for j in range(nj):
                o_ref[i * nj + j] = buf[pl.ds(off + i * 16 * nj + j, 16, stride=nj), l, :].astype(BF)
            return ZERO

        lax.fori_loop(a * n, b * n, step, ZERO)

    def both(l, a, b):
        o_ref = (o0_ref, o1_ref)[l]

        @on(me < ND // TWO)
        def _():
            go(o_ref, l, D // LANE, a, b)

        @on(me >= ND // TWO)
        def _():
            go(o_ref, l, C // LANE, a, b)

    own = NU - THREE
    both(ZERO, ZERO, own)

    @on(me > ZERO)
    def _():
        piece(me, ZERO).wait_recv()
        for d in range(ONE, ND - ONE):
            piece(me, d).start()

    both(ONE, ZERO, own)
    sh.wait()
    buf[RSH:RSH + SPILL] = shr[:].astype(F32)
    both(ZERO, own, NU)
    both(ONE, own, NU)
    wait_all(csm)

    @on(me < ND - ONE)
    def _():
        small(ZERO).wait_recv()

    @on(me > ZERO)
    def _():
        for d in range(ND - ONE):
            piece(lax.rem(me + ONE + d, ND), ZERO).wait_recv()
        for d in range(ONE, ND - ONE):
            piece(me, d).wait_send()

    @on(me == ZERO)
    def _():
        for d in range(ONE, ND):
            first_send(d).wait_send()
            zero_send(d).wait_send()

    @on(me == ND - ONE)
    def _():
        for d in range(ND - ONE):
            small(d).wait_send()


def start(p3, misc, cid):
    n = (ND,)
    return run(start_kernel, (p3, misc), [HBM, VM],
        [sds((UNIT, 16, LANE), BF)] * TWO + [sds((ND, TOKR // FOUR, LANE), BF), sds((TWO, SMR, LANE), BF), sds(n + misc.shape, F32)], [VM] * 5,
        scratch=[pltpu.VMEM((GROWS, TWO, LANE), F32), pltpu.VMEM((SPILL, TWO, LANE), BF), pltpu.VMEM((SPILL, TWO, LANE), BF),
            pltpu.VMEM((ND, TOKR // FOUR, LANE), BF), pltpu.VMEM((TWO, SMR, LANE), BF), SEM, SEM, SEM(n), SEM(n), SEM(n), SEM, SEM(n), SEM(n), SEM(n), SEM, SEM],
        flops=TEN**TEN, cid=cid)


def shift_pick(a, b, lane, r):
    return jnp.where(lane < LANE - r, pltpu.roll(a, (LANE - r) % LANE, ONE), pltpu.roll(b, (LANE - r) % LANE, ONE))


def wprep_kernel(tok_ref, sm_ref, misc_ref, w1a_ref, w1t_ref, w2p_ref, w2t_ref, b2c_ref, vec_ref, lab_ref, bias_ref, tf, w1s, w2l, w2h, sf, sg):
    me = lax.axis_index(AX)
    for k in range(ND):
        sf[k * SMD:(k + ONE) * SMD, :] = misc_ref[k, :SMD, :].astype(BF).astype(F32)
        lab_ref[:, k * B:(k + ONE) * B] = jnp.broadcast_to(misc_ref[k, SMD:SMD + ONE, :B], (SUB, B))
    bias_ref[:] = jnp.zeros(bias_ref.shape, F32)
    bias_ref[:KR, :] = sf[pl.ds(16 + KR * me, KR), :]
    vec_ref[:] = jnp.zeros(vec_ref.shape, F32)
    w1s[:] = jnp.zeros(w1s.shape, F32)
    lane = lax.broadcasted_iota(jnp.int32, (16, LANE), ONE)

    def put(l, row, src, r0, n):
        for i in range(n):
            vec_ref[l, row + i // SUB:row + i // SUB + ONE, (i % SUB) * LANE:(i % SUB + ONE) * LANE] = src[r0 + i:r0 + i + ONE, :]

    for l in range(TWO):
        for q in range(FOUR):
            tf[q * (TOKR // FOUR):(q + ONE) * (TOKR // FOUR), :] = tok_ref[FOUR * l + q].astype(F32)
        smf = sm_ref[l].astype(F32)
        sg[:SMR, :] = smf
        for j in range(FOUR):
            w1s[:S, j * LANE:(j + ONE) * LANE] = tf[pl.ds(j, S, stride=FOUR), :]
            w1s[S:S + ONE, j * LANE:(j + ONE) * LANE] = sg[16 + j:17 + j, :]
        for b in range(32):
            p = S * b
            r0 = HTOK + p // LANE
            o = p % LANE
            x = [tf[pl.ds(r0 + q, 16, stride=49), :] for q in range(THREE if o + S > TWO * LANE else TWO)]
            w2l[pl.ds(b, 16, stride=32), :] = shift_pick(x[ZERO], x[ONE], lane, o)
            hi = shift_pick(x[ONE], x[-ONE], lane, o)
            w2h[pl.ds(b, 16, stride=32), :] = jnp.where(lane < S - LANE, hi, 0.0)
        w1 = w1s[:]
        w2 = jnp.concatenate([w2l[:], w2h[:]], axis=ONE)
        w1a_ref[l] = w1[:SP].astype(BF)
        w1t_ref[l] = w1.T[:, :SP].astype(BF)
        w2p_ref[l] = w2[:, :SP].astype(BF)
        w2t_ref[l] = w2.T[:SP].astype(BF)
        put(l, VG1, sg, ZERO, SUB)
        put(l, VS1, sg, SUB, SUB)
        b2 = jnp.concatenate([sg[20:21, :], sg[21:22, :]], axis=ONE)
        b2 = jnp.broadcast_to(b2, (SUB, TWO * LANE)).T[:SP, :ONE]
        rowi = lax.broadcasted_iota(jnp.int32, (SP, LANE), ZERO)
        b2c_ref[l] = jnp.where(rowi < S, jnp.broadcast_to(b2, (SP, LANE)), 0.0)
        lane7 = lax.broadcasted_iota(jnp.int32, (56, LANE), ONE)
        sg[:56, :] = shift_pick(smf[21:77], smf[22:78], lane7, S - LANE)
        put(l, VG2, sg, ZERO, SUB)
        put(l, VS2, sg, SUB, SUB)
        put(l, VB1, sg, 16, 32)
        put(l, VB2, sg, 48, SUB)
        put(l, VLG, sf, ZERO, SUB)
        put(l, VLS, sf, SUB, SUB)


def wprep(tok, sm, misc):
    return run(wprep_kernel, (tok, sm, misc), [VM] * THREE,
        [sds((TWO, SP, J), BF), sds((TWO, J, SP), BF), sds((TWO, J, SP), BF), sds((TWO, SP, J), BF), sds((TWO, SP, LANE), F32), sds((TWO, VROW, C), F32), sds((SUB, NIMG), F32), sds((24, LANE), F32)],
        [VM] * 8, scratch=[pltpu.VMEM((TOKR, LANE), F32), pltpu.VMEM((256, J), F32), pltpu.VMEM((J, LANE), F32), pltpu.VMEM((J, LANE), F32), pltpu.VMEM((SMF, LANE), F32), pltpu.VMEM((SMR, LANE), F32)],
        flops=5 * TEN**9)


def vec_spec(l):
    return fixed((ONE, VROW, C), (l, ZERO, ZERO))


def lay(shape, l):
    return fixed((ONE,) + shape, (l, ZERO, ZERO))


CW = 256


def tok_fwd_kernel(x_ref, w1t_ref, w2t_ref, b2_ref, v_ref, out_ref, n2_ref, act_ref, gp_ref, n_s):
    @on(pl.program_id(ZERO) == ZERO)
    def _():
        r = lax.broadcasted_iota(jnp.int32, (SP, C), ZERO)
        for im in range(TWO):
            n_s[im] = jnp.where(r == S, 1.0, 0.0).astype(BF)

    for im in range(TWO):
        xf = x_ref[im, :S, :].astype(F32)
        nh, _ = unit_stats(xf)
        n_s[im, :S, :] = (nh * v_ref[ZERO, VG1:VG1 + ONE, :] + v_ref[ZERO, VS1:VS1 + ONE, :]).astype(BF)
    for im in range(TWO):
        cols = []
        for c in range(ZERO, C, CW):
            cs = slice(c, c + CW)
            a, gp = gelu_both(dot(w1t_ref[ZERO], n_s[im, :, cs]))
            act_ref[im, :, cs] = a
            gp_ref[im, :, cs] = gp
            o = dot(w2t_ref[ZERO], a) + b2_ref[ZERO, :, :ONE]
            cols.append((x_ref[im, :S, cs].astype(F32) + o[:S]).astype(BF))
        x1 = jnp.concatenate(cols, axis=ONE)
        out_ref[im, :S, :] = x1
        nh2, _ = unit_stats(x1.astype(F32))
        n2_ref[im, :S, :] = (nh2 * v_ref[ZERO, VG2:VG2 + ONE, :] + v_ref[ZERO, VS2:VS2 + ONE, :]).astype(BF)
        out_ref[im, S:, :] = jnp.zeros((SP - S, C), BF)
        n2_ref[im, S:, :] = jnp.zeros((SP - S, C), BF)


def img(r, n=C):
    return pl.BlockSpec((TWO, r, n), lambda i: (i, ZERO, ZERO))


def tok_fwd(x, wp, l):
    return run(tok_fwd_kernel, (x, wp[ONE], wp[THREE], wp[FOUR], wp[5]),
        [img(x.shape[ONE]), lay((J, SP), l), lay((SP, J), l), lay((SP, LANE), l), vec_spec(l)],
        [sds((B, SP, C), BF)] * TWO + [sds((B, J, C), BF), sds((B, J, C), F32)], [img(SP)] * TWO + [img(J)] * TWO,
        scratch=[pltpu.VMEM((TWO, SP, C), BF)], grid=B // TWO, flops=60 * TEN**9, nbytes=14 * TEN**7)


def tok_bwd_kernel(need_dx, x_ref, da_ref, act_ref, gp_ref, w1a_ref, w2p_ref, v_ref, *rest):
    if need_dx:
        dx_ref = rest[ZERO]
        rest = rest[ONE:]
    dw1_ref, dw2_ref, db1_ref, db2_ref, dg_ref, ds_ref, n_s, nh_s, dh_s, dn_s = rest

    @on(pl.program_id(ZERO) == ZERO)
    def _():
        for r in (dw1_ref, dw2_ref, db1_ref, db2_ref, dg_ref, ds_ref, n_s):
            r[:] = jnp.zeros(r.shape, r.dtype)

    rs = []
    for im in range(TWO):
        nh, rstd = unit_stats(x_ref[im, :S, :].astype(F32))
        nh_s[im, :S, :] = nh
        rs.append(rstd)
        n_s[:S, im * C:(im + ONE) * C] = (nh * v_ref[ZERO, VG1:VG1 + ONE, :] + v_ref[ZERO, VS1:VS1 + ONE, :]).astype(BF)
    db1 = db1_ref[:]
    for im in range(TWO):
        for c in range(ZERO, C, CW):
            cs = slice(c, c + CW)
            dact = dot(w2p_ref[ZERO], da_ref[im, :, cs]).astype(BF).astype(F32)
            dh = dact * gp_ref[im, :, cs]
            for k in range(ZERO, CW, LANE):
                db1 = db1 + dh[:, k:k + LANE]
            dhb = dh.astype(BF)
            dh_s[:, im * C + c:im * C + c + CW] = dhb
            dn_s[im, :, cs] = dot(w1a_ref[ZERO], dhb)
    db1_ref[:] = db1
    act2 = jnp.concatenate([act_ref[ZERO], act_ref[ONE]], axis=ONE)
    da2 = jnp.concatenate([da_ref[ZERO], da_ref[ONE]], axis=ONE)
    dw2_ref[:] += dotg(act2, da2, NT)
    dw1_ref[:] += dotg(dh_s[:], n_s[:], NT)
    db2 = db2_ref[:]
    s8 = S // SUB * SUB
    for im in range(TWO):
        for k in range(ZERO, C, LANE):
            db2 = db2 + da_ref[im, :, k:k + LANE].astype(F32)
        dn = dn_s[im, :S, :].astype(BF).astype(F32)
        nh = nh_s[im, :S, :]
        pr = dn * nh
        dg_ref[:] += sum8(pr[:s8])
        ds_ref[:] += sum8(dn[:s8])
        dg_ref[:S - s8] += pr[s8:]
        ds_ref[:S - s8] += dn[s8:]
        if need_dx:
            dx = ln_bwd(nh, rs[im], dn, v_ref[ZERO, VG1:VG1 + ONE, :])
            dx_ref[im, :S, :] = (da_ref[im, :S, :].astype(F32) + dx).astype(BF)
            dx_ref[im, S:, :] = jnp.zeros((SP - S, C), BF)
    db2_ref[:] = db2


def tok_bwd(x, da, act, gp, wp, l):
    acc = [(J, SP), (J, SP), (J, LANE), (SP, LANE), (SUB, C), (SUB, C)]
    dx = [sds((B, SP, C), BF)] if l else []
    return run(functools.partial(tok_bwd_kernel, bool(l)), (x, da, act, gp, wp[ZERO], wp[TWO], wp[5]),
        [img(x.shape[ONE]), img(SP), img(J), img(J), lay((SP, J), l), lay((J, SP), l), vec_spec(l)],
        dx + [sds(s, F32) for s in acc], [img(SP)] * len(dx) + [fixed(s) for s in acc],
        scratch=[pltpu.VMEM((SP, TWO * C), BF), pltpu.VMEM((TWO, SP, C), F32), pltpu.VMEM((J, TWO * C), BF), pltpu.VMEM((TWO, SP, C), F32)],
        grid=B // TWO, flops=60 * TEN**9, nbytes=14 * TEN**7)


M = 400
DC = 512


def row(n):
    return pl.BlockSpec((M, n), lambda i: (i, ZERO))


def wspec(h):
    return fixed((64, 32, 16, LANE) if h == ZERO else (256, SUB, 16, LANE), (h, ZERO, ZERO, ZERO), True)


def ch_fwd_kernel(n2_ref, x1_ref, w1_ref, w2_ref, v_ref, x2_ref, act_ref, gp_ref):
    n2 = n2_ref[:]
    for k in range(D // DC):
        ks = slice(k * DC, (k + ONE) * DC)
        r = VB1 + k // TWO
        b = v_ref[ZERO, r:r + ONE, (k % TWO) * DC:(k % TWO + ONE) * DC]
        act_ref[:, ks], gp_ref[:, ks] = gelu_both(dot(n2, wcols(w1_ref, k * DC, DC)) + b)
    for c in range(ZERO, C, CW):
        cs = slice(c, c + CW)
        o = dot(act_ref[:], wcols(w2_ref, c, CW)) + v_ref[ZERO, VB2:VB2 + ONE, cs]
        x2_ref[:, cs] = (x1_ref[:, cs].astype(F32) + o).astype(BF)


def w_views(wg):
    return wg.reshape(128, 32, 16, LANE), wg.reshape(512, SUB, 16, LANE)


def ch_fwd(n2, x1, wg, wp, l):
    return run(ch_fwd_kernel, (n2, x1) + w_views(wg) + (wp[5],), [row(C), row(C), wspec(ZERO), wspec(ONE), vec_spec(l)],
        [sds((T, C), BF), sds((T, D), BF), sds((T, D), F32)], [row(C), row(D), row(D)],
        grid=T // M, flops=FOUR * T * C * D, nbytes=T * D * 6)


def ch_bwd_a_kernel(do_ref, gp_ref, w2_ref, dh_ref, db1_ref, db2_ref):
    @on(pl.program_id(ZERO) == ZERO)
    def _():
        db1_ref[:] = jnp.zeros(db1_ref.shape, F32)
        db2_ref[:] = jnp.zeros(db2_ref.shape, F32)

    do = do_ref[:]
    db2_ref[:] += sum8(do.astype(F32))
    for k in range(D // DC):
        ks = slice(k * DC, (k + ONE) * DC)
        da = dotg(do, wrows(w2_ref, k * DC, DC), NT).astype(BF).astype(F32)
        dh = da * gp_ref[:, ks]
        db1_ref[:, ks] += sum8(dh)
        dh_ref[:, ks] = dh.astype(BF)


def ch_bwd_a(do, gp, wg):
    return run(ch_bwd_a_kernel, (do, gp, w_views(wg)[ONE]), [row(C), row(D), wspec(ONE)],
        [sds((T, D), BF), sds((SUB, D), F32), sds((SUB, C), F32)], [row(D), fixed((SUB, D)), fixed((SUB, C))],
        grid=T // M, flops=TWO * T * C * D, nbytes=T * D * 6)


def ch_bwd_b_kernel(dh_ref, w1_ref, x1_ref, do_ref, v_ref, da_ref, dg_ref, ds_ref, dn_s):
    @on(pl.program_id(ZERO) == ZERO)
    def _():
        dg_ref[:] = jnp.zeros(dg_ref.shape, F32)
        ds_ref[:] = jnp.zeros(ds_ref.shape, F32)

    for c in range(ZERO, C, CW):
        dn_s[:, c:c + CW] = dotg(dh_ref[:], wrows(w1_ref, c, CW), NT)
    dy = dn_s[:].astype(BF).astype(F32)
    nh, rstd = unit_stats(x1_ref[:].astype(F32))
    dx = ln_bwd(nh, rstd, dy, v_ref[ZERO, VG2:VG2 + ONE, :])
    dg_ref[:] += sum8(dy * nh)
    ds_ref[:] += sum8(dy)
    r = lax.rem(lax.broadcasted_iota(jnp.int32, (M, ONE), ZERO), SP)
    da_ref[:] = jnp.where(r < S, do_ref[:].astype(F32) + dx, 0.0).astype(BF)


def ch_bwd_b(dh, wg, x1, do, wp, l):
    return run(ch_bwd_b_kernel, (dh, w_views(wg)[ZERO], x1, do, wp[5]), [row(D), wspec(ZERO), row(C), row(C), vec_spec(l)],
        [sds((T, C), BF)] + [sds((SUB, C), F32)] * TWO, [row(C)] + [fixed((SUB, C))] * TWO,
        scratch=[pltpu.VMEM((M, C), F32)], grid=T // M, flops=TWO * T * C * D, nbytes=T * D * THREE)


def dw2_kernel(a_ref, b_ref, o_ref):
    r = dotg(a_ref[:], b_ref[:], TN)
    for j in range(C // LANE):
        o_ref[ZERO, :, j] = r[:, LANE * j:LANE * (j + ONE)].reshape(DC // SUB, SUB, LANE)


def dw2_call(act, do, h=None):
    q = C // DC
    own = ND // TWO
    full = h is None
    a_spec = pl.BlockSpec((T, DC), (lambda i: (ZERO, i)) if full else (lambda i: (ZERO, q * i + h)))
    o_map = (lambda i: (own + i // q, lax.rem(i, q), ZERO, ZERO, ZERO)) if full else (lambda i: (own + i, ZERO, ZERO, ZERO, ZERO))
    n = C if full else DC
    return run(dw2_kernel, (act, do), [a_spec, fixed((T, C), once=True)],
        sds((ND, n // SUB, SUB, SUB, LANE), F32), pl.BlockSpec((ONE, DC // SUB, SUB, SUB, LANE), o_map),
        grid=D // DC * n // C, flops=TWO * T * n * D, nbytes=T * D * THREE)


def dw1_kernel(*refs):
    a = jnp.concatenate([r[:] for r in refs[:-THREE]], axis=ONE)
    b_ref, _, o_ref = refs[-THREE:]
    r = dotg(a, b_ref[:], TN)
    for j in range(DC // LANE):
        o_ref[:, :, j] = r[:, LANE * j:LANE * (j + ONE)].reshape(o_ref.shape[:TWO] + (SUB, LANE))


def col_spec(k):
    return fixed((T, LANE), (ZERO, k), True)


def dw1_call(n2, dh, g, h=None):
    full = h is None
    own = ND // TWO
    specs = [fixed((T, C), once=True)] if full else [col_spec(TWO * k + h) for k in range(own)]
    rb = 32 if full else 16
    na = len(specs)
    shape = (ND, rb, 32, SUB, LANE)
    return run(dw1_kernel, (n2,) * na + (dh, g.reshape(shape)), specs + [pl.BlockSpec((T, DC), lambda i: (ZERO, i)), HBM],
        sds(shape, F32), pl.BlockSpec((own, rb, DC // LANE, SUB, LANE), lambda i: (ZERO, ZERO, i, ZERO, ZERO)), alias={na + ONE: ZERO},
        grid=D // DC, flops=TWO * T * (rb * 32) * D, nbytes=T * D * THREE)


PI = FOUR


def pimg():
    return pl.BlockSpec((PI, SP, C), lambda i: (i, ZERO, ZERO))


def pvec():
    return pl.BlockSpec((ONE, PI, C), lambda i: (i, ZERO, ZERO))


def pool_kernel(x_ref, v_ref, o_ref):
    for im in range(PI):
        nh, _ = unit_stats(x_ref[im, :S, :].astype(F32))
        n = (nh * v_ref[ZERO, VLG:VLG + ONE, :] + v_ref[ZERO, VLS:VLS + ONE, :]).astype(BF).astype(F32)
        o_ref[ZERO, im:im + ONE, :] = (jnp.sum(n, axis=ZERO, keepdims=True) * (1.0 / S)).astype(BF).astype(F32)


def pool(x2, wp):
    return run(pool_kernel, (x2, wp[5]), [pimg(), vec_spec(ZERO)], sds((B // PI, PI, C), F32), pvec(), grid=B // PI, flops=TEN**TEN, nbytes=T * C * TWO)


def lnf_kernel(x_ref, dp_ref, v_ref, d_ref, dg_ref, ds_ref):
    @on(pl.program_id(ZERO) == ZERO)
    def _():
        dg_ref[:] = jnp.zeros(dg_ref.shape, F32)
        ds_ref[:] = jnp.zeros(ds_ref.shape, F32)

    g = v_ref[ZERO, VLG:VLG + ONE, :]
    for im in range(PI):
        dn = (dp_ref[ZERO, im:im + ONE, :] * (1.0 / S)).astype(BF).astype(F32)
        nh, rstd = unit_stats(x_ref[im, :S, :].astype(F32))
        dxh = dn * g
        m1 = jnp.sum(dxh, axis=-ONE, keepdims=True) * (1.0 / C)
        m2 = jnp.sum(dxh * nh, axis=-ONE, keepdims=True) * (1.0 / C)
        d_ref[im, :S, :] = (rstd * ((dxh - m1) - nh * m2)).astype(BF)
        d_ref[im, S:, :] = jnp.zeros((SP - S, C), BF)
        dg_ref[ZERO:ONE, :] += dn * jnp.sum(nh, axis=ZERO, keepdims=True)
        ds_ref[ZERO:ONE, :] += dn * float(S)


def lnf_bwd(x2, dp, wp):
    return run(lnf_kernel, (x2, dp, wp[5]), [pimg(), pvec(), vec_spec(ZERO)], [sds((B, SP, C), BF), sds((SUB, C), F32), sds((SUB, C), F32)],
        [pimg(), fixed((SUB, C)), fixed((SUB, C))], grid=B // PI, flops=TEN**TEN, nbytes=T * C * FOUR)


HAB = 1408


def hconv_kernel(w_ref, o_ref):
    r = pl.program_id(ZERO) * HAB + lax.broadcasted_iota(jnp.int32, (HAB, LANE), ZERO)
    o_ref[:] = jnp.where(r < NCLS, w_ref[:], 0.0).astype(BF)


def hconv(wt):
    blk = pl.BlockSpec((HAB, LANE), lambda i: (i, ZERO))
    return run(hconv_kernel, (wt,), [blk], sds((ND * KC, LANE), BF), blk, grid=ND * KC // HAB, nbytes=TWO * TEN**7)


def head_kernel(*refs):
    wall_ref, pooled_ref, bias_ref, lab_ref, dl_ref, gb_ref, loss_ref, dpool_ref, pall_ref, w, lg, pb, st, sta, dps, dpr, ws, ss, rs, ss2, rs2, ss3, rs3 = refs
    pb[:] = pooled_ref[:].astype(BF)
    row0 = pl.multiple_of(KC * lax.axis_index(AX), KC)
    cw = [pltpu.make_async_copy(wall_ref.at[r, pl.ds(row0, KC)], w.at[r], ws.at[r]) for r in range(ND)]
    for c in cw:
        c.start()
    me = entry_barrier()
    cs = ag_all(me, pb, pall_ref, ss, rs)
    pall_ref[me] = pb[:]
    wait_all(cs)

    wait_all(cw)
    bt = bias_ref[:].T
    pm = pall_ref[:].reshape(NIMG, C)
    for q in range(KR // TWO):
        n = q * TWO * LANE
        acc = jnp.concatenate([jnp.broadcast_to(bt[:, TWO * q + k:TWO * q + k + ONE], (LANE, NIMG)) for k in range(TWO)], axis=ZERO)
        acc = acc + dotg(jnp.concatenate([w[r, n:n + TWO * LANE, :] for r in range(ND)], axis=ONE), pm, NT)
        cls = KC * me + n + lax.broadcasted_iota(jnp.int32, (TWO * LANE, NIMG), ZERO)
        lg[n:n + TWO * LANE, :] = jnp.where(cls < NCLS, acc, -1e30)
    lab = lab_ref[ZERO:ONE, :].astype(jnp.int32)
    lgv = lg[:]
    hit = KC * me + lax.broadcasted_iota(jnp.int32, (KC, NIMG), ZERO) == lab
    m = jnp.max(lgv, axis=ZERO, keepdims=True)
    st[ZERO:ONE, :] = m
    st[ONE:TWO, :] = jnp.sum(jnp.exp(lgv - m), axis=ZERO, keepdims=True)
    st[TWO:THREE, :] = jnp.sum(jnp.where(hit, lgv, 0.0), axis=ZERO, keepdims=True)
    st[THREE:, :] = jnp.zeros((SUB - THREE, NIMG), F32)
    cs = ag_all(me, st, sta, ss2, rs2)
    sta[me] = st[:]
    wait_all(cs)
    top = sta[ZERO, ZERO:ONE, :]
    for k in range(ONE, ND):
        top = jnp.maximum(top, sta[k, ZERO:ONE, :])
    z = jnp.zeros((ONE, NIMG), F32)
    picked = jnp.zeros((ONE, NIMG), F32)
    for k in range(ND):
        z = z + sta[k, ONE:TWO, :] * jnp.exp(sta[k, ZERO:ONE, :] - top)
        picked = picked + sta[k, TWO:THREE, :]
    logz = top + jnp.log(z)
    loss_ref[:] = jnp.broadcast_to(jnp.sum(logz - picked, axis=ONE, keepdims=True) * (1.0 / NIMG), (SUB, LANE))
    gb_ref[:] = jnp.zeros(gb_ref.shape, F32)
    for q in range(KR):
        n = q * LANE
        hit = KC * me + n + lax.broadcasted_iota(jnp.int32, (LANE, NIMG), ZERO) == lab
        d = (jnp.exp(lg[n:n + LANE, :] - logz) - jnp.where(hit, 1.0, 0.0)) * (1.0 / NIMG)
        dl_ref[n:n + LANE, :] = d.astype(BF)
        gb_ref[q:q + ONE, :] = jnp.sum((d[:, :LANE] + d[:, LANE:]).T, axis=ZERO, keepdims=True)
    for r in range(ZERO, ND, TWO):
        dp = dotg(dl_ref[:], jnp.concatenate([w[r], w[r + ONE]], axis=ONE), TN)
        dps[:, :, r * LANE:(r + TWO) * LANE] = dp.reshape(ND, B, TWO * LANE)
    cs = []
    for d in range(ONE, ND):
        peer = lax.rem(me + d, ND)
        c = rcopy(dps.at[peer], dpr.at[me], ss3.at[d], rs3.at[d], peer)
        c.start()
        cs.append(c)
    dpr[me] = dps[me]
    wait_all(cs)
    acc = dpr[ZERO]
    for k in range(ONE, ND):
        acc = acc + dpr[k]
    dpool_ref[:] = acc


def head(wall, pooled, wp, cid):
    n = (ND,)
    return run(head_kernel, (wall, pooled, wp[7], wp[6]), [HBM] + [VM] * THREE,
        [sds((KC, NIMG), BF), sds((24, LANE), F32), sds((SUB, LANE), F32), sds((B, C), F32), sds((ND, B, C), BF)], [VM] * 5,
        scratch=[pltpu.VMEM((ND, KC, LANE), BF), pltpu.VMEM((KC, NIMG), F32), pltpu.VMEM((B, C), BF), pltpu.VMEM((SUB, NIMG), F32), pltpu.VMEM((ND, SUB, NIMG), F32), pltpu.VMEM((ND, B, C), F32), pltpu.VMEM((ND, B, C), F32)] + [SEM(n)] * 7,
        flops=TWO * TEN**TEN, cid=cid)


def pack_small(dst, dw1_ref, dw2_ref, dbt1_ref, dbt2_ref, dg1_ref, ds1_ref, dg2_ref, ds2_ref, dbc1_ref, dbc2_ref, ws, wl, wh, xs):
    ws[:] = jnp.zeros(ws.shape, F32)
    ws[:, :SP] = dw1_ref[:]
    w1 = ws[:].T
    for j in range(FOUR):
        dst(j, S, FOUR, w1[:S, j * LANE:(j + ONE) * LANE])
    wl[:] = dw2_ref[:, :LANE]
    wh[:, :SP - LANE] = dw2_ref[:, LANE:]
    lane = lax.broadcasted_iota(jnp.int32, (16, LANE), ONE)
    for i in range(49):
        j0 = LANE * i // S
        s0 = LANE * i % S
        lo = wl[pl.ds(j0, 16, stride=32), :]
        hi = wh[pl.ds(j0, 16, stride=32), :]
        if s0 < LANE:
            v = shift_pick(lo, hi, lane, s0)
        else:
            v = pltpu.roll(hi, (TWO * LANE - s0) % LANE, ONE)
        left = S - s0
        if left < LANE:
            nx = wl[pl.ds(j0 + ONE, 16, stride=32), :]
            v = jnp.where(lane < left, v, pltpu.roll(nx, left, ONE))
        dst(HTOK + i, 16, 49, v)
    xs[:] = jnp.zeros(xs.shape, F32)

    def put(r0, v, n):
        for i in range(n):
            xs[r0 + i:r0 + i + ONE, :] = v[:, i * LANE:(i + ONE) * LANE]

    def tot(ref):
        return jnp.sum(ref[:], axis=ZERO, keepdims=True)

    put(ZERO, tot(dg2_ref), SUB)
    put(SUB, tot(ds2_ref), SUB)
    put(16, tot(dbc1_ref), 32)
    put(48, tot(dbc2_ref), SUB)
    x = xs[:]
    r = S - LANE
    lane8 = lax.broadcasted_iota(jnp.int32, (SMR, LANE), ONE)
    xr = pltpu.roll(x, r, ONE)
    xs[:] = jnp.zeros(xs.shape, F32)
    xs[21:77, :] = xr[:56]
    shifted = jnp.where(lane8 >= r, xs[:], 0.0)
    xs[22:78, :] = xr[:56]
    low = jnp.where(lane8 < r, xs[:], 0.0)
    row_i = lax.broadcasted_iota(jnp.int32, (SMR, LANE), ZERO)
    xs[:] = shifted + jnp.where(row_i >= 22, low, 0.0)
    put(ZERO, tot(dg1_ref), SUB)
    put(SUB, tot(ds1_ref), SUB)
    put(16, jnp.sum(dbt1_ref[:].T, axis=ZERO, keepdims=True), FOUR)
    bt2 = jnp.sum(dbt2_ref[:].T, axis=ZERO, keepdims=True)
    xs[20:21, :] = bt2[:, :LANE]
    xs[21:22, :r] = bt2[:, LANE:S]
    dst(TOKR, SMR, ONE, xs[:])
    dst(TOKR + SMR, ND * TP - TOKR - SMR, ONE, jnp.zeros((ND * TP - TOKR - SMR, LANE), F32))


PACK_SCR = [pltpu.VMEM((J, 256), F32), pltpu.VMEM((J, LANE), F32), pltpu.VMEM((J, LANE), F32), pltpu.VMEM((SMR, LANE), F32)]


def pack_kernel(*refs):
    ins = refs[:TEN]
    gb_ref, dgf_ref, dsf_ref, o_ref, ws, wl, wh, xs = refs[TEN:]
    me = lax.axis_index(AX)

    def dst(r0, n, stride, v):
        if stride == ONE:
            o_ref[r0:r0 + n, :] = v
        else:
            o_ref[pl.ds(r0, n, stride=stride), :] = v

    pack_small(dst, *ins, ws, wl, wh, xs)
    base = ND * TP
    o_ref[base:, :] = jnp.zeros((SMF, LANE), F32)
    for r0, ref in ((ZERO, dgf_ref), (SUB, dsf_ref)):
        v = jnp.sum(ref[:], axis=ZERO, keepdims=True)
        for i in range(SUB):
            o_ref[base + r0 + i:base + r0 + i + ONE, :] = v[:, i * LANE:(i + ONE) * LANE]
    o_ref[pl.ds(base + 16 + KR * me, KR), :] = gb_ref[:KR, :]


def pack(parts, gb, dgf, dsf):
    return run(pack_kernel, tuple(parts) + (gb, dgf, dsf), [VM] * 13, sds((ND * TP + SMF, LANE), F32), VM, scratch=PACK_SCR)


def untile(g_ref, o_ref, me, r0=ZERO):
    off = TOKR - STEPR * me + r0

    def go(nj, acc0):
        def step(i, acc):
            for j in range(nj):
                v = g_ref[i * nj + j]
                o_ref[pl.ds(off + i * SUB * nj + j, SUB, stride=nj), :] = v
                acc = acc + v * v
            return acc

        return lax.fori_loop(ZERO, g_ref.shape[ZERO] // nj, step, acc0)

    return go


def fin_kernel(g_ref, tot_ref, sqh_ref, o_ref, sg_ref, sq_ref):
    me = lax.axis_index(AX)
    go = untile(g_ref, o_ref, me)
    base = ND * TP
    sg = tot_ref[pl.ds(pl.multiple_of(base + SMD * me, SUB), SMD), :]
    sg_ref[:] = sg
    tl = tot_ref[:base, :]
    acc = sqh_ref[:] + sum8(sg * sg) + jnp.where(me == ZERO, 1.0, 0.0) * sum8(tl * tl)

    @on(me < ND // TWO)
    def _():
        sq_ref[:] = go(D // LANE, acc)

    @on(me >= ND // TWO)
    def _():
        sq_ref[:] = go(C // LANE, acc)


def fin(g, tot, sqh):
    return run(fin_kernel, (g, tot, sqh), [VM] * THREE, [sds((GROWS, LANE), F32), sds((SMD, LANE), F32), sds((SUB, LANE), F32)], [VM] * THREE)


def finh_kernel(g_ref, sqi_ref, o_ref, sq_ref):
    me = lax.axis_index(AX)
    go = untile(g_ref, o_ref, me, UR // TWO)

    @on(me < ND // TWO)
    def _():
        sq_ref[:] = go(D // LANE, sqi_ref[:])

    @on(me >= ND // TWO)
    def _():
        sq_ref[:] = go(C // LANE, sqi_ref[:])


def finh(g, sqi):
    return run(finh_kernel, (g, sqi), [VM] * TWO, [sds((GROWS, LANE), F32), sds((SUB, LANE), F32)], [VM] * TWO)


def tail_kernel(*refs):
    ins = refs[:TEN]
    g_ref, sqi_ref, gl_ref, o_ref, sca_ref, ws, wl, wh, xs, xb, rb, sb, sqb, sqa, ss, rs, ss2, rs2, ss5, rs5, ss7, rs7 = refs[TEN:]

    def dst(r0, n, stride, v):
        if stride == ONE:
            for q in range(ND):
                a = max(r0, q * TP)
                e = min(r0 + n, (q + ONE) * TP)
                if a < e:
                    xb[a:e, :] = v[a - r0:e - r0]
        else:
            xb[pl.ds(r0, n, stride=stride), :] = v

    pack_small(dst, *ins, ws, wl, wh, xs)
    me = entry_barrier()

    def part(q):
        return xb.at[pl.ds(pl.multiple_of(q * TP, SUB), TP)]

    cs = []
    for d in range(ONE, ND):
        peer = lax.rem(me + d, ND)
        c = rcopy(part(peer), rb.at[me], ss.at[d], rs.at[d], peer)
        c.start()
        cs.append(c)
    rb[me] = xb[pl.ds(pl.multiple_of(me * TP, SUB), TP), :]
    go = untile(g_ref, gl_ref, me)

    @on(me < ND // TWO)
    def _():
        sqb[:] = go(D // LANE, sqi_ref[:])

    @on(me >= ND // TWO)
    def _():
        sqb[:] = go(C // LANE, sqi_ref[:])

    wait_all(cs)
    a = rb[ZERO]
    for k in range(ONE, ND):
        a = a + rb[k]
    sb[:] = a
    sqb[:] += sum8(a * a)
    csq = ag_all(me, sqb, sqa, ss7, rs7)
    sqa[me] = sqb[:]

    def to_first():
        return rcopy(sb, o_ref.at[me], ss2, rs2.at[me], ZERO)

    def to_last():
        return rcopy(sb, o_ref.at[me], ss5, rs5.at[me], ND - ONE)

    @on(me != ZERO)
    def _():
        to_first().start()

    @on(me != ND - ONE)
    def _():
        to_last().start()

    o_ref[me] = sb[:]
    wait_all(csq)
    t = sqa[ZERO]
    for k in range(ONE, ND):
        t = t + sqa[k]
    t = jnp.sum(jnp.sum(t, axis=ZERO, keepdims=True), axis=ONE, keepdims=True)
    sca_ref[:] = jnp.broadcast_to(1.0 / jnp.maximum(1.0, jnp.sqrt(t)), (SUB, LANE))

    @on(me != ZERO)
    def _():
        to_first().wait_send()

    @on(me != ND - ONE)
    def _():
        to_last().wait_send()

    @on(me == ZERO)
    def _():
        for d in range(ONE, ND):
            rcopy(sb, o_ref.at[d], ss2, rs2.at[d], ZERO).wait_recv()

    @on(me == ND - ONE)
    def _():
        for d in range(ND - ONE):
            rcopy(sb, o_ref.at[d], ss5, rs5.at[d], ZERO).wait_recv()


def tail(parts, g, sqi, cid):
    n = (ND,)
    return run(tail_kernel, tuple(parts) + (g, sqi), [VM] * 12,
        [sds((GROWS, LANE), F32), sds((ND, TP, LANE), F32), sds((SUB, LANE), F32)], [VM] * THREE,
        scratch=PACK_SCR + [pltpu.VMEM((ND * TP, LANE), F32), pltpu.VMEM((ND, TP, LANE), F32), pltpu.VMEM((TP, LANE), F32), pltpu.VMEM((SUB, LANE), F32), pltpu.VMEM((ND, SUB, LANE), F32),
            SEM(n), SEM(n), SEM, SEM(n), SEM, SEM(n), SEM(n), SEM(n)], cid=cid)


def adam_math(p, m, v, g, decay):
    m2 = BETA_ONE * m + (1.0 - BETA_ONE) * g
    v2 = BETA_TWO * v + (1.0 - BETA_TWO) * g * g
    mh = m2 * (1.0 / (1.0 - BETA_ONE ** ADAM_STEP))
    vh = v2 * (1.0 / (1.0 - BETA_TWO ** ADAM_STEP))
    return p - LEARN_RATE * (mh / (jnp.sqrt(vh) + ADAM_EPS) + decay * p), m2, v2


HBR = 2816


def head_gsq_kernel(dl_ref, p_ref, sqi_ref, sq_ref):
    @on(pl.program_id(ZERO) == ZERO)
    def _():
        sq_ref[:] = sqi_ref[:]

    g = dot(dl_ref[:], p_ref[:])
    sq_ref[:] += sum8(g * g)


def head_gsq(dl, pc, sq):
    return run(head_gsq_kernel, (dl, pc, sq), [pl.BlockSpec((HBR, NIMG), lambda i: (i, ZERO)), fixed((NIMG, LANE)), fixed((SUB, LANE))],
        sds((SUB, LANE), F32), fixed((SUB, LANE)), grid=ND, flops=TEN**9, nbytes=TEN**7)


ABR = 656
NAB = -(-RSH // ABR)


def head_adam_kernel(sc_ref, dl_ref, pc_ref, p_ref, m_ref, v_ref, po_ref, mo_ref, vo_ref):
    g = dot(dl_ref[:], pc_ref[:]) * sc_ref[ZERO, ZERO]
    po_ref[:], mo_ref[:], vo_ref[:] = adam_math(p_ref[:], m_ref[:], v_ref[:], g, WEIGHT_DECAY)


def head_adam(sc, dl, pc, p, m, v):
    blk = pl.BlockSpec((HAB, LANE), lambda i: (i, ZERO))
    return run(head_adam_kernel, (sc, dl, pc, p, m, v), [SMEM, pl.BlockSpec((HAB, NIMG), lambda i: (i, ZERO)), fixed((NIMG, LANE)), blk, blk, blk],
        [sds(p.shape, F32)] * THREE, [blk] * THREE, grid=-(-NCLS // HAB), flops=TEN**TEN, nbytes=8 * TEN**7)


def layer_adam_kernel(sc_ref, g0_ref, h0_ref, g1_ref, t0_ref, t1_ref, s0_ref, s1_ref, p_ref, m_ref, v_ref, po_ref, mo_ref, vo_ref, gs):
    k = lax.axis_index(AX)
    i = pl.program_id(ZERO)
    off = TOKR - STEPR * k
    sc = sc_ref[ZERO, ZERO]
    lays = ((g0_ref, t0_ref, s0_ref), (g1_ref, t1_ref, s1_ref))
    ri = i * ABR + lax.broadcasted_iota(jnp.int32, (ABR, LANE), ZERO)
    gs[pl.ds(ZERO, ABR, stride=TWO), :] = jnp.where(ri < off + UR // TWO, g0_ref[:], h0_ref[:]) * sc
    gs[pl.ds(ONE, ABR, stride=TWO), :] = g1_ref[:] * sc
    for b in range(THREE):
        @on(i == b)
        def _():
            n = min(ABR, TOKR - b * ABR)
            r = b * ABR + lax.broadcasted_iota(jnp.int32, (n, LANE), ZERO)
            for l in range(TWO):
                g_ref, t_ref, s_ref = lays[l]
                e = min(n, SPR - b * ABR)
                sp = s_ref[b * ABR:b * ABR + e, :]
                if e < n:
                    sp = jnp.concatenate([sp, jnp.zeros((n - e, LANE), F32)], axis=ZERO)
                alt = jnp.where(k == ZERO, t_ref[b * ABR:b * ABR + n, :], sp)
                gs[pl.ds(l, n, stride=TWO), :] = jnp.where(r < off, alt, g_ref[:n, :]) * sc

    @on(jnp.logical_and(i == NAB - ONE, k == ND - ONE))
    def _():
        r0 = RSH - SMR - (NAB - ONE) * ABR
        for l in range(TWO):
            gs[pl.ds(TWO * r0 + l, SMR, stride=TWO), :] = lays[l][ONE][TOKR:TOKR + SMR, :] * sc

    n2 = TWO * ABR
    r2 = TWO * (RSH * k + i * ABR) + lax.broadcasted_iota(jnp.int32, (n2, LANE), ZERO)
    decay = jnp.where(r2 < TWO * MATR, WEIGHT_DECAY, 0.0)
    a, b, c = adam_math(p_ref.reshape(n2, LANE)[:], m_ref.reshape(n2, LANE)[:], v_ref.reshape(n2, LANE)[:], gs[:], decay)
    po_ref.reshape(n2, LANE)[:] = a
    mo_ref.reshape(n2, LANE)[:] = b
    vo_ref.reshape(n2, LANE)[:] = c


def layer_adam(sc, g0, h0, g1, t0, t1, s0, s1, p, m, v):
    blk = pl.BlockSpec((ABR, TWO, LANE), lambda i: (i, ZERO, ZERO))
    gb = pl.BlockSpec((ABR, LANE), lambda i: (i, ZERO))
    return run(layer_adam_kernel, (sc, g0, h0, g1, t0, t1, s0, s1, p, m, v),
        [SMEM, gb, gb, gb] + [fixed(t.shape) for t in (t0, t1, s0, s1)] + [blk] * THREE, [sds(p.shape, F32)] * THREE, [blk] * THREE,
        scratch=[pltpu.VMEM((TWO * ABR, LANE), F32)], grid=NAB, nbytes=6 * TEN**7)


def solution(mesh):
    row_spec = P(AX)
    layer_spec = P(None, AX)
    in_specs = (row_spec, row_spec, layer_spec, row_spec, row_spec, layer_spec, row_spec, row_spec, layer_spec, row_spec, row_spec)
    out_specs = (P(),) + in_specs[TWO:]
    up = [(i, (i + ONE) % ND) for i in range(ND)]

    def scatter(grad, n):
        return lax.psum_scatter(grad.reshape(ND, n, LANE), AX, scatter_dimension=ZERO, tiled=True).reshape(n // SUB, SUB, LANE)

    def device_step(act_in, labels, layer_p, head_w, small_p, layer_m, head_m, small_m, layer_v, head_v, small_v):
        me = lax.axis_index(AX)
        p3 = rows3(layer_p)
        lab = jnp.pad(labels.astype(F32)[None, :], ((ZERO, SUB - ONE), (ZERO, LANE - B)))
        misc = jnp.concatenate([small_p.reshape(SMD, LANE), lab], axis=ZERO)
        t0, t1, tok_all, sm_all, misc_all = start(p3, misc, ONE)
        wg = [lax.all_gather(t, AX, tiled=True) for t in (t0, t1)]
        wp = wprep(tok_all, sm_all, misc_all)
        hidden = act_in
        saved = []
        for l in range(TWO):
            x1, n2, ta, tg = tok_fwd(hidden, wp, l)
            if l == ZERO:
                hw, x1 = lax.optimization_barrier((head_w, x1))
                wall = lax.all_gather(hconv(hw.T), AX)
            x1 = x1.reshape(T, C)
            n2 = n2.reshape(T, C)
            x2, act, gp = ch_fwd(n2, x1, wg[l], wp, l)
            saved.append((hidden, ta, tg, x1, n2, act, gp))
            hidden = x2.reshape(B, SP, C)
        pooled = pool(hidden, wp).reshape(B, C)
        dl, gb, loss, dpool, pall = head(wall, pooled, wp, TWO)
        dl_all = lax.all_gather(dl, AX, tiled=True)
        pc = lax.dynamic_slice_in_dim(pall.reshape(NIMG, C), LANE * me, LANE, axis=ONE)
        d_out, dgf, dsf = lnf_bwd(hidden, dpool.reshape(B // PI, PI, C), wp)
        d_out = d_out.reshape(T, C)
        for l in (ONE, ZERO):
            hid_in, ta, tg, x1, n2, act, gp = saved[l]
            if l:
                dh, dbc1, dbc2 = ch_bwd_a(d_out, gp, wg[l])
                dh, dl_all = lax.optimization_barrier((dh, dl_all))
                grad = dw1_call(n2, dh, dw2_call(act, d_out))
                dh, grad = lax.optimization_barrier((dh, grad))
                shard1 = scatter(grad, UR)
            else:
                g2 = dw2_call(act, d_out, ONE)
                g2, d_out = lax.optimization_barrier((g2, d_out))
                dh, dbc1, dbc2 = ch_bwd_a(d_out, gp, wg[l])
                grad = dw1_call(n2, dh, g2, ONE)
                dh, grad, tot, act = lax.optimization_barrier((dh, grad, tot, act))
                shard_b = scatter(grad, UR // TWO)
                gl1, small_g, sq = fin(shard1, tot, jnp.zeros((SUB, LANE), F32))
                sp1 = lax.ppermute(gl1[RSH:RSH + SPR], AX, up)
                dh, sq, act = lax.optimization_barrier((dh, sq, act))
                grad = dw1_call(n2, dh, dw2_call(act, d_out, ZERO), ZERO)
                dh, grad = lax.optimization_barrier((dh, grad))
                shard_a = scatter(grad, UR // TWO)
            da, dg2, ds2 = ch_bwd_b(dh, wg[l], x1, d_out, wp, l)
            if l == ZERO:
                h0, sq = finh(shard_b, sq)
                sp0 = lax.ppermute(h0[RSH:RSH + SPR], AX, up)
                da, sq = lax.optimization_barrier((da, sq))
            o = tok_bwd(hid_in, da.reshape(B, SP, C), ta, tg, wp, l)
            if l:
                d_out = o[ZERO].reshape(T, C)
                o = o[ONE:]
            parts = tuple(o) + (dg2, ds2, dbc1, dbc2)
            if l:
                sv, d_out = lax.optimization_barrier((pack(parts, gb, dgf, dsf), d_out))
                tot = lax.psum(sv, AX)
        dl_b, first, sp0 = lax.optimization_barrier((dl_all, parts[ZERO], sp0))
        sq = head_gsq(dl_b, pc, sq)
        gl0, tsm, sca = tail((first,) + parts[ONE:], shard_a, sq, FOUR)
        np3, nm3, nv3 = layer_adam(sca, gl0, h0, gl1, tsm.reshape(ND * TP, LANE), tot, sp0, sp1, p3, rows3(layer_m), rows3(layer_v))
        nh, nhm, nhv = head_adam(sca, dl_all, pc, head_w.T, head_m.T, head_v.T)
        nsp, nsm, nsv = adam_math(small_p, small_m, small_v, small_g.reshape(SMD * LANE) * sca[ZERO, ZERO], 0.0)
        return (loss[ZERO, ZERO], unrows3(np3), nh.T, nsp, unrows3(nm3), nhm.T, nsm, unrows3(nv3), nhv.T, nsv)

    return jax.shard_map(device_step, mesh=mesh, in_specs=in_specs, out_specs=out_specs, check_vma=False)
```

time: 4770 us -> 1580 us (0.33)
  waiting for transfers between devices: 1760 us -> 124 us
  matrix products: 1480 us -> 0 us
  Pallas kernels: 0 us -> 1410 us
  local copies, waits for them, and re-layouts: 1080 us -> 23.3 us
  other arithmetic: 341 us -> 4 us
    unnamed x7 -> x8, waiting for transfers between devices: 1660 us -> 1.32 us
    dot_general x27 -> x0, matrix products: 1480 us -> none  [the longest x2 252 us: layer_backward(): jnp.einsum('bsc,dc->bsd', d_out_bf, w_ch2, preferred_element_type=jnp.flo...]
    pallas_call x0 -> x29, Pallas kernels: none -> 1410 us  [run(): pl.pallas_call(body, in_specs=in_specs, out_specs=out_specs, out_shape=ou...]
    concatenate x3 -> x0, local copies, waits for them, and re-layouts: 531 us -> none  [the longest x2 530 us: layer_backward(): jnp.concatenate([g_w_tok1.reshape(-1), g_w_tok2.reshape(-1), g_w_ch1.resh...]
    slice x9 -> x4, local copies, waits for them, and re-layouts: 411 us -> 6.39 us  [the longest x1 2.01 us: device_step(): sp0 = lax.ppermute(h0[RSH:RSH + SPR], AX, up)]
    reduce_sum x22 -> x0, other arithmetic: 203 us -> none  [the longest x9 81.3 us: layer_norm(): var_val = jnp.mean(jnp.square(x_f - mean_val), axis=-1, keepdims=True)]
    reduce_scatter x0 -> x3, waiting for transfers between devices: none -> 122 us  [scatter(): lax.psum_scatter(grad.reshape(ND, n, LANE), AX, scatter_dimension=ZERO, t...]
    all_gather x3 -> x4, waiting for transfers between devices: 102 us -> 0.03 us  [the longest x2 0.02 us: device_step(): wg = [lax.all_gather(t, AX, tiled=True) for t in (t0, t1)]]
  transfers between devices with their start and end apart: 5 -> 10, of which waited for: 3 -> 2; matrix products, arithmetic and copies ran while one was open for 23% -> 2% of each run, Pallas kernels for 0% -> 69%
where the time goes in v1:
time: 1580 us; the launch traced here: 1570 us
  Pallas kernels  1410 us (89%)
  waiting for transfers between devices  124 us (8%)
  local copies, waits for them, and re-layouts  23.3 us (1%)
    pallas_call x29, Pallas kernels, run(): pl.pallas_call(body, in_specs=in_specs, out_specs=out_specs, out_shape=ou...  1410 us
    reduce_scatter x3, waiting for transfers between devices, scatter(): lax.psum_scatter(grad.reshape(ND, n, LANE), AX, scatter_dimension=ZERO, t...  122 us
  transfers between devices with their start and end apart: 10, of which 2 were waited for; matrix products, arithmetic and copies ran while one was open for 2% of the time, Pallas kernels for 69%

profile of v1, /device:TPU:0, one launch (start us, length us, event | category | flops | bytes accessed | tf_op | source)
XLA Modules:
  0.0 1573.8 jit_solution(7004850960315259216)
XLA Ops:
  9.2 30.0 %shard_map.186 = (bf16[512,16,128]{2,1,0:T(8,128)(2,1)}, bf16[512,16,128]{2,1,0:T(8,128)(2,1)}, bf16[8,392,128]{2,1,0:T(8,128)(2,1)}, bf16[2,80,128]{2,1,0:T(8,128)(2,1)}, f32[8,32,128]{2,1,0:T(8,128)}) custom-call(f32[8398,2,128]{2,1,0:T(2,128)} %bitcast.82, f32[32,128]{1,0:T(8,128)} %select_maximum_fusion.misc_ref), custom_call_target="tpu_custom_call" | custom-call | flops 10000000000 | bytes 1000000 | tf_op jit(solution)/shard_map/pallas_call | solution.py:84
  56.1 77.4 %shard_map.188 = (bf16[32,200,1024]{2,1,0:T(8,128)(2,1)}, bf16[32,200,1024]{2,1,0:T(8,128)(2,1)}, bf16[32,512,1024]{2,1,0:T(8,128)(2,1)}, f32[32,512,1024]{2,1,0:T(8,128)}) custom-call(bf16[32,196,1024]{2,1,0:T(8,128)(2,1)} %copy.26.x_ref, bf16[2,512,200]{2,1,0:T(8,128)(2,1)} %get-tuple-element.111.w1t_ref, bf16[2,200,512]{2,1,0:T(8,128)(2,1)} %get-tuple-element.112.w2t_ref, ...), custom_call_target="tpu_custom_call" | custom-call | flops 60000002048 | bytes 140000000 | tf_op jit(solution)/shard_map/pallas_call | solution.py:84
  146.8 143.3 %shard_map.190 = (bf16[6400,1024]{1,0:T(8,128)(2,1)}, bf16[6400,4096]{1,0:T(8,128)(2,1)}, f32[6400,4096]{1,0:T(8,128)}) custom-call(bf16[6400,1024]{1,0:T(8,128)(2,1)} %bitcast.63, bf16[6400,1024]{1,0:T(8,128)(2,1)} %bitcast.107, bf16[128,32,16,128]{3,2,1,0:T(8,128)(2,1)} %bitcast.92, bf16[512,8,16,128]{3,2,1,0:T(8,128)(2,1)} %bitcast.93, ...), custom_call_target="tpu_custom_call" | custom-call | flops 107374182400 | bytes 157286400 | tf_op jit(solution)/shard_map/pallas_call | solution.py:84
  290.1 77.9 %shard_map.191 = (bf16[32,200,1024]{2,1,0:T(8,128)(2,1)}, bf16[32,200,1024]{2,1,0:T(8,128)(2,1)}, bf16[32,512,1024]{2,1,0:T(8,128)(2,1)}, f32[32,512,1024]{2,1,0:T(8,128)}) custom-call(bf16[32,200,1024]{2,1,0:T(8,128)(2,1)} %bitcast.113, bf16[2,512,200]{2,1,0:T(8,128)(2,1)} %get-tuple-element.111.w1t_ref, bf16[2,200,512]{2,1,0:T(8,128)(2,1)} %get-tuple-element.112.w2t_ref, ...), custom_call_target="tpu_custom_call" | custom-call | flops 60000002048 | bytes 140000000 | tf_op jit(solution)/shard_map/pallas_call | solution.py:84
  367.9 153.2 %shard_map.192 = (bf16[6400,1024]{1,0:T(8,128)(2,1)}, bf16[6400,4096]{1,0:T(8,128)(2,1)}, f32[6400,4096]{1,0:T(8,128)}) custom-call(bf16[6400,1024]{1,0:T(8,128)(2,1)} %bitcast.117, bf16[6400,1024]{1,0:T(8,128)(2,1)} %bitcast.115, bf16[128,32,16,128]{3,2,1,0:T(8,128)(2,1)} %bitcast.96, bf16[512,8,16,128]{3,2,1,0:T(8,128)(2,1)} %bitcast.97, ...), custom_call_target="tpu_custom_call" | custom-call | flops 107374182400 | bytes 157286400 | tf_op jit(solution)/shard_map/pallas_call | solution.py:84
  539.3 35.9 %shard_map.194 = (bf16[2816,256]{1,0:T(8,128)(2,1)}, f32[24,128]{1,0:T(8,128)}, f32[8,128]{1,0:T(8,128)}, f32[32,1024]{1,0:T(8,128)}, bf16[8,32,1024]{2,1,0:T(8,128)(2,1)}) custom-call(bf16[8,22528,128]{2,1,0:T(8,128)(2,1)} %bitcast.91, f32[32,1024]{1,0:T(8,128)} %reshape.141.refs_1_, f32[24,128]{1,0:T(8,128)} %get-tuple-element.125.refs_2_, ...), custom_call_target="tpu_custom_call" | custom-call | flops 20000000000 | bytes 1000000 | tf_op jit(solution)/shard_map/pallas_call | solution.py:84
  576.9 17.8 %shard_map.195 = (bf16[32,200,1024]{2,1,0:T(8,128)(2,1)}, f32[8,1024]{1,0:T(8,128)}, f32[8,1024]{1,0:T(8,128)}) custom-call(bf16[32,200,1024]{2,1,0:T(8,128)(2,1)} %bitcast.120, f32[8,4,1024]{2,1,0:T(4,128)} %reshape.142.dp_ref, f32[2,16,1024]{2,1,0:T(8,128)} %get-tuple-element.114.v_ref), custom_call_target="tpu_custom_call" | custom-call | flops 10000000000 | bytes 26214400 | tf_op jit(solution)/shard_map/pallas_call | solution.py:84
  594.7 63.7 %shard_map.197 = f32[8,128,8,8,128]{4,3,2,1,0:T(8,128)} custom-call(bf16[6400,4096]{1,0:T(8,128)(2,1)} %get-tuple-element.136.a_ref, bf16[6400,1024]{1,0:T(8,128)(2,1)} %bitcast.122), custom_call_target="tpu_custom_call" | custom-call | flops 53687091200 | bytes 78643200 | tf_op jit(solution)/shard_map/pallas_call | solution.py:84
  658.4 70.4 %shard_map.196 = (bf16[6400,4096]{1,0:T(8,128)(2,1)}, f32[8,4096]{1,0:T(8,128)}, f32[8,1024]{1,0:T(8,128)}) custom-call(bf16[6400,1024]{1,0:T(8,128)(2,1)} %bitcast.123, f32[6400,4096]{1,0:T(8,128)} %get-tuple-element.130.gp_ref, bf16[512,8,16,128]{3,2,1,0:T(8,128)(2,1)} %bitcast.98), custom_call_target="tpu_custom_call" | custom-call | flops 53687091200 | bytes 157286400 | tf_op jit(solution)/shard_map/pallas_call | solution.py:84
  728.8 64.1 %shard_map.198 = f32[8,32,32,8,128]{4,3,2,1,0:T(8,128)} custom-call(bf16[6400,1024]{1,0:T(8,128)(2,1)} %bitcast.118, bf16[6400,4096]{1,0:T(8,128)(2,1)} %get-tuple-element.137.refs_1_.dh_ref, f32[8,32,32,8,128]{4,3,2,1,0:T(8,128)} %bitcast.78), custom_call_target="tpu_custom_call", output_to_operand_aliasing={{}: (2, {})} | custom-call | flops 53687091200 | bytes 78643200 | tf_op jit(solution)/shard_map/pallas_call | solution.py:84
  792.9 78.5 %shard_map.199 = (bf16[6400,1024]{1,0:T(8,128)(2,1)}, f32[8,1024]{1,0:T(8,128)}, f32[8,1024]{1,0:T(8,128)}) custom-call(bf16[6400,4096]{1,0:T(8,128)(2,1)} %get-tuple-element.137.refs_1_.dh_ref, bf16[128,32,16,128]{3,2,1,0:T(8,128)(2,1)} %bitcast.99, bf16[6400,1024]{1,0:T(8,128)(2,1)} %bitcast.116, bf16[6400,1024]{1,0:T(8,128)(2,1)} %bitcast.124, ...), custom_call_target="tpu_custom_call" | custom-call | flops 53687091200 | bytes 78643200 | tf_op jit(solution)/shard_map/pallas_call | solution.py:84
  871.4 74.6 %shard_map.200 = (bf16[32,200,1024]{2,1,0:T(8,128)(2,1)}, f32[512,200]{1,0:T(8,128)}, f32[512,200]{1,0:T(8,128)}, f32[512,128]{1,0:T(8,128)}, f32[200,128]{1,0:T...) custom-call(bf16[32,200,1024]{2,1,0:T(8,128)(2,1)} %bitcast.114, bf16[32,200,1024]{2,1,0:T(8,128)(2,1)} %bitcast.125, ...), custom_call_target="tpu_custom_call" | custom-call | flops 60000002048 | bytes 140000000 | tf_op jit(solution)/shard_map/pallas_call | solution.py:84
  949.8 36.2 %shard_map.202 = f32[8,64,8,8,128]{4,3,2,1,0:T(8,128)} custom-call(bf16[6400,4096]{1,0:T(8,128)(2,1)} %get-tuple-element.169.a_ref, bf16[6400,1024]{1,0:T(8,128)(2,1)} %bitcast.109), custom_call_target="tpu_custom_call" | custom-call | flops 26843545600 | bytes 78643200 | tf_op jit(solution)/shard_map/pallas_call | solution.py:84
  986.0 78.6 %shard_map.203 = (bf16[6400,4096]{1,0:T(8,128)(2,1)}, f32[8,4096]{1,0:T(8,128)}, f32[8,1024]{1,0:T(8,128)}) custom-call(bf16[6400,1024]{1,0:T(8,128)(2,1)} %bitcast.110, f32[6400,4096]{1,0:T(8,128)} %get-tuple-element.159.gp_ref, bf16[512,8,16,128]{3,2,1,0:T(8,128)(2,1)} %bitcast.94), custom_call_target="tpu_custom_call" | custom-call | flops 53687091200 | bytes 157286400 | tf_op jit(solution)/shard_map/pallas_call | solution.py:84
  1064.5 34.9 %shard_map.204 = f32[8,16,32,8,128]{4,3,2,1,0:T(8,128)} custom-call(bf16[6400,1024]{1,0:T(8,128)(2,1)} %bitcast.64, bf16[6400,1024]{1,0:T(8,128)(2,1)} %bitcast.65, bf16[6400,1024]{1,0:T(8,128)(2,1)} %bitcast.66, bf16[6400,1024]{1,0:T(8,128)(2,1)} %bitcast.67, bf16[6400,4096]{1,0:T(8,128)(2,1)} %get-tuple-element.170.refs_4_.dh_ref, ...), custom_call_target="tpu_custom_call", output_to_operand_aliasing={{}: (5, {})} | custom-call | flops 26843545600 | bytes 78643200 | tf_op jit(solution)/shard_map/pallas_call | solution.py:84
  1099.5 96.2 %reduce-scatter.4.cloned.1.call-done = f32[1,8192,128]{2,1,0:T(8,128)} async-done(((f32[8,8192,128]{2,1,0:T(8,128)}), f32[1,8192,128]{2,1,0:T(8,128)}) %reduce-scatter.4.cloned.1.call-update) | async-done | bytes 4194320 | tf_op jit(solution)/shard_map/reduce_scatter | solution.py:1051
  1203.7 39.7 %shard_map.206 = f32[8,64,8,8,128]{4,3,2,1,0:T(8,128)} custom-call(bf16[6400,4096]{1,0:T(8,128)(2,1)} %get-tuple-element.169.a_ref, bf16[6400,1024]{1,0:T(8,128)(2,1)} %bitcast.111), custom_call_target="tpu_custom_call" | custom-call | flops 26843545600 | bytes 78643200 | tf_op jit(solution)/shard_map/pallas_call | solution.py:84
  1243.4 34.9 %shard_map.207 = f32[8,16,32,8,128]{4,3,2,1,0:T(8,128)} custom-call(bf16[6400,1024]{1,0:T(8,128)(2,1)} %bitcast.68, bf16[6400,1024]{1,0:T(8,128)(2,1)} %bitcast.69, bf16[6400,1024]{1,0:T(8,128)(2,1)} %bitcast.70, bf16[6400,1024]{1,0:T(8,128)(2,1)} %bitcast.71, bf16[6400,4096]{1,0:T(8,128)(2,1)} %get-tuple-element.170.refs_4_.dh_ref, ...), custom_call_target="tpu_custom_call", output_to_operand_aliasing={{}: (5, {})} | custom-call | flops 26843545600 | bytes 78643200 | tf_op jit(solution)/shard_map/pallas_call | solution.py:84
  1281.1 26.0 %reduce-scatter.6.cloned.1.call-done = f32[1,4096,128]{2,1,0:T(8,128)} async-done(((f32[8,4096,128]{2,1,0:T(8,128)}), f32[1,4096,128]{2,1,0:T(8,128)}) %reduce-scatter.6.cloned.1.call-update) | async-done | bytes 2097168 | tf_op jit(solution)/shard_map/reduce_scatter | solution.py:1051
  1312.2 80.8 %shard_map.208 = (bf16[6400,1024]{1,0:T(8,128)(2,1)}, f32[8,1024]{1,0:T(8,128)}, f32[8,1024]{1,0:T(8,128)}) custom-call(bf16[6400,4096]{1,0:T(8,128)(2,1)} %get-tuple-element.170.refs_4_.dh_ref, bf16[128,32,16,128]{3,2,1,0:T(8,128)(2,1)} %bitcast.95, bf16[6400,1024]{1,0:T(8,128)(2,1)} %bitcast.108, bf16[6400,1024]{1,0:T(8,128)(2,1)} %bitcast.112, ...), custom_call_target="tpu_custom_call" | custom-call | flops 53687091200 | bytes 78643200 | tf_op jit(solution)/shard_map/pallas_call | solution.py:84
  1398.5 68.5 %shard_map.210 = (f32[512,200]{1,0:T(8,128)}, f32[512,200]{1,0:T(8,128)}, f32[512,128]{1,0:T(8,128)}, f32[200,128]{1,0:T(8,128)}, f32[8,1024]{1,0:T(8,128)}, /*index=5*/f32[8,1024]{1,0:T(8,128)}) custom-call(bf16[32,196,1024]{2,1,0:T(8,128)(2,1)} %copy.26.x_ref, bf16[32,200,1024]{2,1,0:T(8,128)(2,1)} %bitcast.121, ...), custom_call_target="tpu_custom_call" | custom-call | flops 60000002048 | bytes 140000000 | tf_op jit(solution)/shard_map/pallas_call | solution.py:84
  1477.0 24.5 %shard_map.212 = (f32[9768,128]{1,0:T(8,128)}, f32[8,208,128]{2,1,0:T(8,128)}, f32[8,128]{1,0:T(8,128)}) custom-call(f32[512,200]{1,0:T(8,128)} %get-tuple-element.180.refs_0_, f32[512,200]{1,0:T(8,128)} %get-tuple-element.181.refs_1_, f32[512,128]{1,0:T(8,128)} %get-tuple-element.182.refs_2_, f32[200,128]{1,0:T(8,128)} %get-tuple-element.183.refs_3_, ...), custom_call_target="tpu_custom_call" | custom-call | flops 1000000000 | bytes 1000000 | tf_op jit(solution)/shard_map/pallas_call | solution.py:84
  1504.7 33.1 %shard_map.214 = (f32[21843,128]{1,0:T(8,128)}, f32[21843,128]{1,0:T(8,128)}, f32[21843,128]{1,0:T(8,128)}) custom-call(f32[8,128]{1,0:T(8,128)} %get-tuple-element.194.sc_ref, bf16[22528,256]{1,0:T(8,128)(2,1)} %all-gather.10.cloned.1.call-done.dl_ref, bf16[256,128]{1,0:T(8,128)(2,1)} %constant_dynamic-slice_fusion.p_ref.pc_ref, f32[21843,128]{1,0:T(8,128)} %bitcast.77, ...), custom_call_target="tpu_custom_call" | custom-call | flops 10000000000 | bytes 80000000 | tf_op jit(solution)/shard_map/pallas_call | solution.py:84
  1537.8 28.7 %shard_map.213 = (f32[8398,2,128]{2,1,0:T(2,128)}, f32[8398,2,128]{2,1,0:T(2,128)}, f32[8398,2,128]{2,1,0:T(2,128)}) custom-call(f32[8,128]{1,0:T(8,128)} %get-tuple-element.194.sc_ref, f32[9768,128]{1,0:T(8,128)} %get-tuple-element.195.g0_ref, f32[9768,128]{1,0:T(8,128)} %get-tuple-element.179.h0_ref, f32[9768,128]{1,0:T(8,128)} %get-tuple-element.196.g1_ref, ...), custom_call_target="tpu_custom_call" | custom-call | flops 1000000000 | bytes 60000000 | tf_op jit(solution)/shard_map/pallas_call | solution.py:84
  (45 shorter events, 90.3 us)
Async XLA Ops:
  7.2 139.6 %all-gather.6.cloned.1.call-start = ((), (), s32[]{:S(2)}) async-start(), calls=%async_computation.3 | async-start | bytes 18874368 | tf_op jit(solution)/shard_map/all_gather | solution.py:1059
  39.3 328.7 %all-gather.8.cloned.1.call-start = ((), (), s32[]{:S(2)}) async-start(), calls=%async_computation.4 | async-start | bytes 18874368 | tf_op jit(solution)/shard_map/all_gather | solution.py:1059
  40.0 499.3 %all-gather.12.cloned.1.call-start = ((), (), s32[]{:S(2)}) async-start(), calls=%async_computation.10 | async-start | bytes 51904512 | tf_op jit(solution)/shard_map/all_gather | solution.py:1067
  146.4 582.4 %all-gather.10.cloned.1.call-start = ((), (), s32[]{:S(2)}) async-start(), calls=%async_computation.5 | async-start | bytes 12976128 | tf_op jit(solution)/shard_map/all_gather | solution.py:1075
  575.3 524.2 %all-reduce.3.cloned.1.call-start = ((), (), s32[]{:S(2)}) async-start(), calls=%async_computation.6 | async-start | bytes 1900544 | tf_op jit(solution)/shard_map/psum | solution.py:1112
  949.1 246.6 %reduce-scatter.4.cloned.1.call-start = ((), (), s32[]{:S(2)}) async-start(), calls=%async_computation.7 | async-start | bytes 37748736 | tf_op jit(solution)/shard_map/reduce_scatter | solution.py:1051
  949.7 357.4 %reduce-scatter.6.cloned.1.call-start = ((), (), s32[]{:S(2)}) async-start(), calls=%async_computation.8 | async-start | bytes 18874368 | tf_op jit(solution)/shard_map/reduce_scatter | solution.py:1051
  1099.4 377.6 %reduce-scatter.8.cloned.1.call-start = ((), (), s32[]{:S(2)}) async-start(), calls=%async_computation.9 | async-start | bytes 18874368 | tf_op jit(solution)/shard_map/reduce_scatter | solution.py:1051
  1394.9 72.1 %collective-permute-start = (f32[1368,128]{1,0:T(8,128)}, f32[1368,128]{1,0:T(8,128)}, u32[]{:S(2)}, u32[]{:S(2)}) collective-permute-start(f32[1368,128]{1,0:T(8,128)} %slice.13), channel_id=1, source_target_pairs={{0,1},{1,2},{2,3},{3,4},{4,5},{5,6},{6,7},{7,0}} | collective-permute-start | bytes 2101256 | tf_op jit(solution)/shard_map/ppermute | solution.py:1103
  1397.0 140.9 %collective-permute-start.1 = (f32[1368,128]{1,0:T(8,128)}, f32[1368,128]{1,0:T(8,128)}, u32[]{:S(2)}, u32[]{:S(2)}) collective-permute-start(f32[1368,128]{1,0:T(8,128)} %slice.14), channel_id=1, source_target_pairs={{0,1},{1,2},{2,3},{3,4},{4,5},{5,6},{6,7},{7,0}} | collective-permute-start | bytes 2101256 | tf_op jit(solution)/shard_map/ppermute | solution.py:1095
Sparse Core Ops, SparseCore 0:
  39.4 88.7 all-gather.5
  130.0 84.1 all-gather.7
  216.6 208.9 all-gather.11
  575.4 63.3 all-gather.9
  949.3 46.6 all-reduce.2
  999.3 196.3 reduce-scatter.3
  1199.2 107.8 reduce-scatter.5
  1310.6 117.2 reduce-scatter.7

commit v2 on v1

--- a/solution.py
+++ b/solution.py
@@ -53,6 +53,7 @@
 SMD = SMF // ND
 VROW = 16
 VLIM = 64 * 1024 * 1024 - 65536
+VTAIL = 16 * 1024 * 1024
 NT = (((1,), (1,)), ((), ()))
 TN = (((0,), (0,)), ((), ()))
 VM = pl.BlockSpec(memory_space=pltpu.VMEM)
@@ -170,19 +171,96 @@
     return b.reshape(TWO, RSH * LANE)
 
 
-def start_kernel(p_ref, misc_ref, o0_ref, o1_ref, tok_o, sm_o, misc_o, buf, shs, shr, toks, sms, ds1, ds2, ss_m, rs_m, ss_s, rs_s, ss_t, rs_t, ss_u, ss_h, rs_h):
-    c1 = pltpu.make_async_copy(p_ref.at[:TOKR], buf.at[:TOKR], ds1)
-    c1.start()
-    c2 = pltpu.make_async_copy(p_ref.at[TOKR:], buf.at[TOKR:RSH], ds2)
-    c2.start()
+OWN = NU - THREE
+LEFT = RSH - (TOKR - STEPR * (ND - ONE)) - UNIT * OWN
+NTILE = UNIT // 16
+
+
+def tiles(o_ref, src, r0, step_rows, nj, n, t0):
+    def step(i, _):
+        for j in range(nj):
+            o_ref[t0 + i * nj + j] = src[pl.ds(r0 + (i * 16 * nj + j) * step_rows, 16, stride=nj * step_rows), :].astype(BF)
+        return ZERO
+
+    lax.fori_loop(ZERO, n * NTILE // nj, step, ZERO)
+
+
+def by_half(me, f):
+    @on(me < ND // TWO)
+    def _():
+        f(D // LANE)
+
+    @on(me >= ND // TWO)
+    def _():
+        f(C // LANE)
+
+
+TQ = TOKR // ND
+
+
+def prep_kernel(p_ref, o0_ref, o1_ref, shs0_ref, shs1_ref, toks_ref, tok1_ref, sms_ref, left0_ref, left1_ref):
+    me = lax.axis_index(AX)
+    src = p_ref.reshape(TWO * RSH, LANE)
+    for l in range(TWO):
+        (shs0_ref, shs1_ref)[l][:] = src[pl.ds(l, SPR, stride=TWO), :].astype(BF)
+        (left0_ref, left1_ref)[l][:] = src[pl.ds(TWO * (RSH - LEFT) + l, LEFT, stride=TWO), :]
+        sms_ref[l] = src[pl.ds(TWO * (RSH - SMR) + l, SMR, stride=TWO), :].astype(BF)
+    off = TOKR - STEPR * me
+
+    def go(nj):
+        for l in range(TWO):
+            tiles((o0_ref, o1_ref)[l], src, TWO * off + l, TWO, nj, OWN, ZERO)
+
+    by_half(me, go)
+
+    @on(me == ZERO)
+    def _():
+        for q in range(ND):
+            toks_ref[q] = src[pl.ds(TWO * TQ * q, TQ, stride=TWO), :].astype(BF)
+        tok1_ref[:] = src[pl.ds(ONE, TOKR, stride=TWO), :].astype(BF).astype(F32)
+
+    @on(me != ZERO)
+    def _():
+        toks_ref[:] = jnp.zeros(toks_ref.shape, BF)
+        tok1_ref[:] = jnp.zeros(tok1_ref.shape, F32)
+
+
+def prep(p3):
+    tile = sds((NU * NTILE, 16, LANE), BF)
+    sh = sds((SPR, LANE), BF)
+    left = sds((LEFT, LANE), F32)
+    return run(prep_kernel, (p3,), [VM], [tile, tile, sh, sh, sds((ND, TQ, LANE), BF), sds((TOKR, LANE), F32), sds((TWO, SMR, LANE), BF), left, left], [VM] * 9)
+
+
+def last_units(me, left_ref, shr_ref, z, w):
+    z[:LEFT, :] = left_ref[:]
+    z[LEFT:, :] = shr_ref[:].astype(F32)
+    r0 = LEFT - (RSH - (TOKR - STEPR * me) - UNIT * OWN)
+    by_half(me, lambda nj: tiles(w, z, r0, ONE, nj, NU - OWN, ZERO))
+
+
+def put_last(w, o_ref, sem):
+    c = pltpu.make_async_copy(w, o_ref.at[pl.ds(OWN * NTILE, (NU - OWN) * NTILE)], sem)
+    c.start()
+    return c
+
+
+LAST_SCR = [pltpu.VMEM((LEFT + SPR, LANE), F32), pltpu.VMEM(((NU - OWN) * NTILE, 16, LANE), BF)]
+
+
+def fix_kernel(shr_ref, left_ref, u_ref, o_ref, z, w, sem):
+    last_units(lax.axis_index(AX), left_ref, shr_ref, z, w)
+    put_last(w, o_ref, sem).wait()
+
+
+def fix(shr, left, t):
+    return run(fix_kernel, (shr, left, t), [VM, VM, HBM], sds(t.shape, BF), HBM, scratch=LAST_SCR + [SEM], alias={TWO: ZERO})
+
+
+def start_kernel(shs, toks, sms, misc_ref, left_ref, u_ref, o_ref, tok_o, sm_o, misc_o, z, w, shr, ss_m, rs_m, ss_s, rs_s, ss_t, rs_t, ss_u, ss_h, rs_h, ss_w):
     me = entry_barrier()
-    csm = ag_all(me, misc_ref, misc_o, ss_m, rs_m)
-    misc_o[me] = misc_ref[:]
-    c1.wait()
-    shs[:] = buf[:SPILL].astype(BF)
     sh = rcopy(shs, shr, ss_h, rs_h, lax.rem(me + ND - ONE, ND))
     sh.start()
-    q4 = TOKR // FOUR
 
     def first_send(d):
         return rcopy(toks.at[d], tok_o.at[d], ss_t.at[d], rs_t.at[d], d)
@@ -198,50 +276,20 @@
 
     @on(me == ZERO)
     def _():
-        for l in range(TWO):
-            for q in range(FOUR):
-                toks[FOUR * l + q] = buf[q4 * q:q4 * (q + ONE), l, :].astype(BF)
         for d in range(ONE, ND):
             first_send(d).start()
         for d in range(ONE, ND):
             zero_send(d).start()
         tok_o[:] = toks[:]
 
-    c2.wait()
-
     @on(me == ND - ONE)
     def _():
-        for l in range(TWO):
-            sms[l] = buf[RSH - SMR:RSH, l, :].astype(BF)
         for d in range(ND - ONE):
             small(d).start()
         sm_o[:] = sms[:]
 
-    off = TOKR - STEPR * me
-
-    def go(o_ref, l, nj, a, b):
-        n = UNIT // nj // 16
-
-        def step(i, _):
-            for j in range(nj):
-                o_ref[i * nj + j] = buf[pl.ds(off + i * 16 * nj + j, 16, stride=nj), l, :].astype(BF)
-            return ZERO
-
-        lax.fori_loop(a * n, b * n, step, ZERO)
-
-    def both(l, a, b):
-        o_ref = (o0_ref, o1_ref)[l]
-
-        @on(me < ND // TWO)
-        def _():
-            go(o_ref, l, D // LANE, a, b)
-
-        @on(me >= ND // TWO)
-        def _():
-            go(o_ref, l, C // LANE, a, b)
-
-    own = NU - THREE
-    both(ZERO, ZERO, own)
+    csm = ag_all(me, misc_ref, misc_o, ss_m, rs_m)
+    misc_o[me] = misc_ref[:]
 
     @on(me > ZERO)
     def _():
@@ -249,11 +297,9 @@
         for d in range(ONE, ND - ONE):
             piece(me, d).start()
 
-    both(ONE, ZERO, own)
     sh.wait()
-    buf[RSH:RSH + SPILL] = shr[:].astype(F32)
-    both(ZERO, own, NU)
-    both(ONE, own, NU)
+    last_units(me, left_ref, shr, z, w)
+    cw = put_last(w, o_ref, ss_w)
     wait_all(csm)
 
     @on(me < ND - ONE)
@@ -278,86 +324,92 @@
         for d in range(ND - ONE):
             small(d).wait_send()
 
-
-def start(p3, misc, cid):
+    cw.wait()
+
+
+def start(shs, toks, sms, misc, left, t, cid):
     n = (ND,)
-    return run(start_kernel, (p3, misc), [HBM, VM],
-        [sds((UNIT, 16, LANE), BF)] * TWO + [sds((ND, TOKR // FOUR, LANE), BF), sds((TWO, SMR, LANE), BF), sds(n + misc.shape, F32)], [VM] * 5,
-        scratch=[pltpu.VMEM((GROWS, TWO, LANE), F32), pltpu.VMEM((SPILL, TWO, LANE), BF), pltpu.VMEM((SPILL, TWO, LANE), BF),
-            pltpu.VMEM((ND, TOKR // FOUR, LANE), BF), pltpu.VMEM((TWO, SMR, LANE), BF), SEM, SEM, SEM(n), SEM(n), SEM(n), SEM, SEM(n), SEM(n), SEM(n), SEM, SEM],
-        flops=TEN**TEN, cid=cid)
+    return run(start_kernel, (shs, toks, sms, misc, left, t), [VM] * 5 + [HBM],
+        [sds(t.shape, BF), sds(toks.shape, BF), sds(sms.shape, BF), sds(n + misc.shape, F32)], [HBM] + [VM] * THREE,
+        scratch=LAST_SCR + [pltpu.VMEM((SPR, LANE), BF), SEM(n), SEM(n), SEM(n), SEM, SEM(n), SEM(n), SEM(n), SEM, SEM, SEM],
+        alias={5: ZERO}, flops=TEN**TEN, cid=cid)
 
 
 def shift_pick(a, b, lane, r):
     return jnp.where(lane < LANE - r, pltpu.roll(a, (LANE - r) % LANE, ONE), pltpu.roll(b, (LANE - r) % LANE, ONE))
 
 
-def wprep_kernel(tok_ref, sm_ref, misc_ref, w1a_ref, w1t_ref, w2p_ref, w2t_ref, b2c_ref, vec_ref, lab_ref, bias_ref, tf, w1s, w2l, w2h, sf, sg):
+def wprep_kernel(l, tok_ref, sm_ref, misc_ref, w1a_ref, w1t_ref, w2p_ref, w2t_ref, b2c_ref, vec_ref, *rest):
+    tf, w1s, w2l, w2h, sf, sg = rest[-6:]
     me = lax.axis_index(AX)
     for k in range(ND):
         sf[k * SMD:(k + ONE) * SMD, :] = misc_ref[k, :SMD, :].astype(BF).astype(F32)
-        lab_ref[:, k * B:(k + ONE) * B] = jnp.broadcast_to(misc_ref[k, SMD:SMD + ONE, :B], (SUB, B))
-    bias_ref[:] = jnp.zeros(bias_ref.shape, F32)
-    bias_ref[:KR, :] = sf[pl.ds(16 + KR * me, KR), :]
+    if l == ZERO:
+        lab_ref, bias_ref = rest[:TWO]
+        for k in range(ND):
+            lab_ref[:, k * B:(k + ONE) * B] = jnp.broadcast_to(misc_ref[k, SMD:SMD + ONE, :B], (SUB, B))
+            tf[k * TQ:(k + ONE) * TQ, :] = tok_ref[k].astype(F32)
+        bias_ref[:] = jnp.zeros(bias_ref.shape, F32)
+        bias_ref[:KR, :] = sf[pl.ds(16 + KR * me, KR), :]
+    else:
+        tf[:TOKR, :] = tok_ref[:]
     vec_ref[:] = jnp.zeros(vec_ref.shape, F32)
     w1s[:] = jnp.zeros(w1s.shape, F32)
     lane = lax.broadcasted_iota(jnp.int32, (16, LANE), ONE)
 
-    def put(l, row, src, r0, n):
+    def put(row, src, r0, n):
         for i in range(n):
-            vec_ref[l, row + i // SUB:row + i // SUB + ONE, (i % SUB) * LANE:(i % SUB + ONE) * LANE] = src[r0 + i:r0 + i + ONE, :]
-
-    for l in range(TWO):
-        for q in range(FOUR):
-            tf[q * (TOKR // FOUR):(q + ONE) * (TOKR // FOUR), :] = tok_ref[FOUR * l + q].astype(F32)
-        smf = sm_ref[l].astype(F32)
-        sg[:SMR, :] = smf
-        for j in range(FOUR):
-            w1s[:S, j * LANE:(j + ONE) * LANE] = tf[pl.ds(j, S, stride=FOUR), :]
-            w1s[S:S + ONE, j * LANE:(j + ONE) * LANE] = sg[16 + j:17 + j, :]
-        for b in range(32):
-            p = S * b
-            r0 = HTOK + p // LANE
-            o = p % LANE
-            x = [tf[pl.ds(r0 + q, 16, stride=49), :] for q in range(THREE if o + S > TWO * LANE else TWO)]
-            w2l[pl.ds(b, 16, stride=32), :] = shift_pick(x[ZERO], x[ONE], lane, o)
-            hi = shift_pick(x[ONE], x[-ONE], lane, o)
-            w2h[pl.ds(b, 16, stride=32), :] = jnp.where(lane < S - LANE, hi, 0.0)
-        w1 = w1s[:]
-        w2 = jnp.concatenate([w2l[:], w2h[:]], axis=ONE)
-        w1a_ref[l] = w1[:SP].astype(BF)
-        w1t_ref[l] = w1.T[:, :SP].astype(BF)
-        w2p_ref[l] = w2[:, :SP].astype(BF)
-        w2t_ref[l] = w2.T[:SP].astype(BF)
-        put(l, VG1, sg, ZERO, SUB)
-        put(l, VS1, sg, SUB, SUB)
-        b2 = jnp.concatenate([sg[20:21, :], sg[21:22, :]], axis=ONE)
-        b2 = jnp.broadcast_to(b2, (SUB, TWO * LANE)).T[:SP, :ONE]
-        rowi = lax.broadcasted_iota(jnp.int32, (SP, LANE), ZERO)
-        b2c_ref[l] = jnp.where(rowi < S, jnp.broadcast_to(b2, (SP, LANE)), 0.0)
-        lane7 = lax.broadcasted_iota(jnp.int32, (56, LANE), ONE)
-        sg[:56, :] = shift_pick(smf[21:77], smf[22:78], lane7, S - LANE)
-        put(l, VG2, sg, ZERO, SUB)
-        put(l, VS2, sg, SUB, SUB)
-        put(l, VB1, sg, 16, 32)
-        put(l, VB2, sg, 48, SUB)
-        put(l, VLG, sf, ZERO, SUB)
-        put(l, VLS, sf, SUB, SUB)
-
-
-def wprep(tok, sm, misc):
-    return run(wprep_kernel, (tok, sm, misc), [VM] * THREE,
-        [sds((TWO, SP, J), BF), sds((TWO, J, SP), BF), sds((TWO, J, SP), BF), sds((TWO, SP, J), BF), sds((TWO, SP, LANE), F32), sds((TWO, VROW, C), F32), sds((SUB, NIMG), F32), sds((24, LANE), F32)],
-        [VM] * 8, scratch=[pltpu.VMEM((TOKR, LANE), F32), pltpu.VMEM((256, J), F32), pltpu.VMEM((J, LANE), F32), pltpu.VMEM((J, LANE), F32), pltpu.VMEM((SMF, LANE), F32), pltpu.VMEM((SMR, LANE), F32)],
+            vec_ref[ZERO, row + i // SUB:row + i // SUB + ONE, (i % SUB) * LANE:(i % SUB + ONE) * LANE] = src[r0 + i:r0 + i + ONE, :]
+
+    smf = sm_ref[l].astype(F32)
+    sg[:SMR, :] = smf
+    for j in range(FOUR):
+        w1s[:S, j * LANE:(j + ONE) * LANE] = tf[pl.ds(j, S, stride=FOUR), :]
+        w1s[S:S + ONE, j * LANE:(j + ONE) * LANE] = sg[16 + j:17 + j, :]
+    for b in range(32):
+        p = S * b
+        r0 = HTOK + p // LANE
+        o = p % LANE
+        x = [tf[pl.ds(r0 + q, 16, stride=49), :] for q in range(THREE if o + S > TWO * LANE else TWO)]
+        w2l[pl.ds(b, 16, stride=32), :] = shift_pick(x[ZERO], x[ONE], lane, o)
+        hi = shift_pick(x[ONE], x[-ONE], lane, o)
+        w2h[pl.ds(b, 16, stride=32), :] = jnp.where(lane < S - LANE, hi, 0.0)
+    w1 = w1s[:]
+    w2 = jnp.concatenate([w2l[:], w2h[:]], axis=ONE)
+    w1a_ref[ZERO] = w1[:SP].astype(BF)
+    w1t_ref[ZERO] = w1.T[:, :SP].astype(BF)
+    w2p_ref[ZERO] = w2[:, :SP].astype(BF)
+    w2t_ref[ZERO] = w2.T[:SP].astype(BF)
+    put(VG1, sg, ZERO, SUB)
+    put(VS1, sg, SUB, SUB)
+    b2 = jnp.concatenate([sg[20:21, :], sg[21:22, :]], axis=ONE)
+    b2 = jnp.broadcast_to(b2, (SUB, TWO * LANE)).T[:SP, :ONE]
+    rowi = lax.broadcasted_iota(jnp.int32, (SP, LANE), ZERO)
+    b2c_ref[ZERO] = jnp.where(rowi < S, jnp.broadcast_to(b2, (SP, LANE)), 0.0)
+    lane7 = lax.broadcasted_iota(jnp.int32, (56, LANE), ONE)
+    sg[:56, :] = shift_pick(smf[21:77], smf[22:78], lane7, S - LANE)
+    put(VG2, sg, ZERO, SUB)
+    put(VS2, sg, SUB, SUB)
+    put(VB1, sg, 16, 32)
+    put(VB2, sg, 48, SUB)
+    put(VLG, sf, ZERO, SUB)
+    put(VLS, sf, SUB, SUB)
+
+
+def wprep(l, tok, sm, misc):
+    extra = [] if l else [sds((SUB, NIMG), F32), sds((24, LANE), F32)]
+    outs = [sds((ONE, SP, J), BF), sds((ONE, J, SP), BF), sds((ONE, J, SP), BF), sds((ONE, SP, J), BF), sds((ONE, SP, LANE), F32), sds((ONE, VROW, C), F32)] + extra
+    return run(functools.partial(wprep_kernel, l), (tok, sm, misc), [VM] * THREE, outs, [VM] * len(outs),
+        scratch=[pltpu.VMEM((TOKR + SUB, LANE), F32), pltpu.VMEM((256, J), F32), pltpu.VMEM((J, LANE), F32), pltpu.VMEM((J, LANE), F32), pltpu.VMEM((SMF, LANE), F32), pltpu.VMEM((SMR, LANE), F32)],
         flops=5 * TEN**9)
 
 
-def vec_spec(l):
-    return fixed((ONE, VROW, C), (l, ZERO, ZERO))
-
-
-def lay(shape, l):
-    return fixed((ONE,) + shape, (l, ZERO, ZERO))
+def vec_spec():
+    return fixed((ONE, VROW, C))
+
+
+def lay(shape):
+    return fixed((ONE,) + shape)
 
 
 CW = 256
@@ -395,9 +447,9 @@
     return pl.BlockSpec((TWO, r, n), lambda i: (i, ZERO, ZERO))
 
 
-def tok_fwd(x, wp, l):
+def tok_fwd(x, wp):
     return run(tok_fwd_kernel, (x, wp[ONE], wp[THREE], wp[FOUR], wp[5]),
-        [img(x.shape[ONE]), lay((J, SP), l), lay((SP, J), l), lay((SP, LANE), l), vec_spec(l)],
+        [img(x.shape[ONE]), lay((J, SP)), lay((SP, J)), lay((SP, LANE)), vec_spec()],
         [sds((B, SP, C), BF)] * TWO + [sds((B, J, C), BF), sds((B, J, C), F32)], [img(SP)] * TWO + [img(J)] * TWO,
         scratch=[pltpu.VMEM((TWO, SP, C), BF)], grid=B // TWO, flops=60 * TEN**9, nbytes=14 * TEN**7)
 
@@ -458,7 +510,7 @@
     acc = [(J, SP), (J, SP), (J, LANE), (SP, LANE), (SUB, C), (SUB, C)]
     dx = [sds((B, SP, C), BF)] if l else []
     return run(functools.partial(tok_bwd_kernel, bool(l)), (x, da, act, gp, wp[ZERO], wp[TWO], wp[5]),
-        [img(x.shape[ONE]), img(SP), img(J), img(J), lay((SP, J), l), lay((J, SP), l), vec_spec(l)],
+        [img(x.shape[ONE]), img(SP), img(J), img(J), lay((SP, J)), lay((J, SP)), vec_spec()],
         dx + [sds(s, F32) for s in acc], [img(SP)] * len(dx) + [fixed(s) for s in acc],
         scratch=[pltpu.VMEM((SP, TWO * C), BF), pltpu.VMEM((TWO, SP, C), F32), pltpu.VMEM((J, TWO * C), BF), pltpu.VMEM((TWO, SP, C), F32)],
         grid=B // TWO, flops=60 * TEN**9, nbytes=14 * TEN**7)
@@ -476,7 +528,11 @@
     return fixed((64, 32, 16, LANE) if h == ZERO else (256, SUB, 16, LANE), (h, ZERO, ZERO, ZERO), True)
 
 
-def ch_fwd_kernel(n2_ref, x1_ref, w1_ref, w2_ref, v_ref, x2_ref, act_ref, gp_ref):
+def pair(n):
+    return pl.BlockSpec((ONE, TWO, n), lambda i: (i, ZERO, ZERO))
+
+
+def ch_fwd_kernel(n2_ref, x1_ref, w1_ref, w2_ref, v_ref, x2_ref, act_ref, gp_ref, *pool_ref):
     n2 = n2_ref[:]
     for k in range(D // DC):
         ks = slice(k * DC, (k + ONE) * DC)
@@ -487,6 +543,11 @@
         cs = slice(c, c + CW)
         o = dot(act_ref[:], wcols(w2_ref, c, CW)) + v_ref[ZERO, VB2:VB2 + ONE, cs]
         x2_ref[:, cs] = (x1_ref[:, cs].astype(F32) + o).astype(BF)
+    if pool_ref:
+        nh, _ = unit_stats(x2_ref[:].astype(F32))
+        n = (nh * v_ref[ZERO, VLG:VLG + ONE, :] + v_ref[ZERO, VLS:VLS + ONE, :]).astype(BF).astype(F32)
+        for im in range(TWO):
+            pool_ref[ZERO][ZERO, im:im + ONE, :] = jnp.sum(n[im * SP:im * SP + S], axis=ZERO, keepdims=True) * (1.0 / S)
 
 
 def w_views(wg):
@@ -494,8 +555,8 @@
 
 
 def ch_fwd(n2, x1, wg, wp, l):
-    return run(ch_fwd_kernel, (n2, x1) + w_views(wg) + (wp[5],), [row(C), row(C), wspec(ZERO), wspec(ONE), vec_spec(l)],
-        [sds((T, C), BF), sds((T, D), BF), sds((T, D), F32)], [row(C), row(D), row(D)],
+    return run(ch_fwd_kernel, (n2, x1) + w_views(wg) + (wp[5],), [row(C), row(C), wspec(ZERO), wspec(ONE), vec_spec()],
+        [sds((T, C), BF), sds((T, D), BF), sds((T, D), F32)] + [sds((B // TWO, TWO, C), F32)] * l, [row(C), row(D), row(D)] + [pair(C)] * l,
         grid=T // M, flops=FOUR * T * C * D, nbytes=T * D * 6)
 
 
@@ -515,9 +576,39 @@
         dh_ref[:, ks] = dh.astype(BF)
 
 
+def ch_bwd_top_kernel(x2_ref, dp_ref, v_ref, gp_ref, w2_ref, dh_ref, db1_ref, db2_ref, do_ref, dg_ref, ds_ref):
+    @on(pl.program_id(ZERO) == ZERO)
+    def _():
+        dg_ref[:] = jnp.zeros(dg_ref.shape, F32)
+        ds_ref[:] = jnp.zeros(ds_ref.shape, F32)
+
+    g = v_ref[ZERO, VLG:VLG + ONE, :]
+    r = lax.broadcasted_iota(jnp.int32, (SP, ONE), ZERO)
+    xf = x2_ref[:].astype(F32)
+    out = []
+    for im in range(TWO):
+        dn = (dp_ref[ZERO, im:im + ONE, :] * (1.0 / S)).astype(BF).astype(F32)
+        nh, rstd = unit_stats(xf[im * SP:(im + ONE) * SP])
+        dxh = dn * g
+        m1 = jnp.sum(dxh, axis=-ONE, keepdims=True) * (1.0 / C)
+        m2 = jnp.sum(dxh * nh, axis=-ONE, keepdims=True) * (1.0 / C)
+        out.append(jnp.where(r < S, rstd * ((dxh - m1) - nh * m2), 0.0))
+        dg_ref[ZERO:ONE, :] += dn * jnp.sum(nh[:S], axis=ZERO, keepdims=True)
+        ds_ref[ZERO:ONE, :] += dn * float(S)
+    do_ref[:] = jnp.concatenate(out, axis=ZERO).astype(BF)
+    ch_bwd_a_kernel(do_ref, gp_ref, w2_ref, dh_ref, db1_ref, db2_ref)
+
+
 def ch_bwd_a(do, gp, wg):
     return run(ch_bwd_a_kernel, (do, gp, w_views(wg)[ONE]), [row(C), row(D), wspec(ONE)],
         [sds((T, D), BF), sds((SUB, D), F32), sds((SUB, C), F32)], [row(D), fixed((SUB, D)), fixed((SUB, C))],
+        grid=T // M, flops=TWO * T * C * D, nbytes=T * D * 6)
+
+
+def ch_bwd_top(x2, dp, gp, wg, wp):
+    return run(ch_bwd_top_kernel, (x2, dp, wp[5], gp, w_views(wg)[ONE]), [row(C), pair(C), vec_spec(), row(D), wspec(ONE)],
+        [sds((T, D), BF), sds((SUB, D), F32), sds((SUB, C), F32), sds((T, C), BF), sds((SUB, C), F32), sds((SUB, C), F32)],
+        [row(D), fixed((SUB, D)), fixed((SUB, C)), row(C), fixed((SUB, C)), fixed((SUB, C))],
         grid=T // M, flops=TWO * T * C * D, nbytes=T * D * 6)
 
 
@@ -538,8 +629,8 @@
     da_ref[:] = jnp.where(r < S, do_ref[:].astype(F32) + dx, 0.0).astype(BF)
 
 
-def ch_bwd_b(dh, wg, x1, do, wp, l):
-    return run(ch_bwd_b_kernel, (dh, w_views(wg)[ZERO], x1, do, wp[5]), [row(D), wspec(ZERO), row(C), row(C), vec_spec(l)],
+def ch_bwd_b(dh, wg, x1, do, wp):
+    return run(ch_bwd_b_kernel, (dh, w_views(wg)[ZERO], x1, do, wp[5]), [row(D), wspec(ZERO), row(C), row(C), vec_spec()],
         [sds((T, C), BF)] + [sds((SUB, C), F32)] * TWO, [row(C)] + [fixed((SUB, C))] * TWO,
         scratch=[pltpu.VMEM((M, C), F32)], grid=T // M, flops=TWO * T * C * D, nbytes=T * D * THREE)
 
@@ -586,53 +677,8 @@
         grid=D // DC, flops=TWO * T * (rb * 32) * D, nbytes=T * D * THREE)
 
 
-PI = FOUR
-
-
-def pimg():
-    return pl.BlockSpec((PI, SP, C), lambda i: (i, ZERO, ZERO))
-
-
-def pvec():
-    return pl.BlockSpec((ONE, PI, C), lambda i: (i, ZERO, ZERO))
-
-
-def pool_kernel(x_ref, v_ref, o_ref):
-    for im in range(PI):
-        nh, _ = unit_stats(x_ref[im, :S, :].astype(F32))
-        n = (nh * v_ref[ZERO, VLG:VLG + ONE, :] + v_ref[ZERO, VLS:VLS + ONE, :]).astype(BF).astype(F32)
-        o_ref[ZERO, im:im + ONE, :] = (jnp.sum(n, axis=ZERO, keepdims=True) * (1.0 / S)).astype(BF).astype(F32)
-
-
-def pool(x2, wp):
-    return run(pool_kernel, (x2, wp[5]), [pimg(), vec_spec(ZERO)], sds((B // PI, PI, C), F32), pvec(), grid=B // PI, flops=TEN**TEN, nbytes=T * C * TWO)
-
-
-def lnf_kernel(x_ref, dp_ref, v_ref, d_ref, dg_ref, ds_ref):
-    @on(pl.program_id(ZERO) == ZERO)
-    def _():
-        dg_ref[:] = jnp.zeros(dg_ref.shape, F32)
-        ds_ref[:] = jnp.zeros(ds_ref.shape, F32)
-
-    g = v_ref[ZERO, VLG:VLG + ONE, :]
-    for im in range(PI):
-        dn = (dp_ref[ZERO, im:im + ONE, :] * (1.0 / S)).astype(BF).astype(F32)
-        nh, rstd = unit_stats(x_ref[im, :S, :].astype(F32))
-        dxh = dn * g
-        m1 = jnp.sum(dxh, axis=-ONE, keepdims=True) * (1.0 / C)
-        m2 = jnp.sum(dxh * nh, axis=-ONE, keepdims=True) * (1.0 / C)
-        d_ref[im, :S, :] = (rstd * ((dxh - m1) - nh * m2)).astype(BF)
-        d_ref[im, S:, :] = jnp.zeros((SP - S, C), BF)
-        dg_ref[ZERO:ONE, :] += dn * jnp.sum(nh, axis=ZERO, keepdims=True)
-        ds_ref[ZERO:ONE, :] += dn * float(S)
-
-
-def lnf_bwd(x2, dp, wp):
-    return run(lnf_kernel, (x2, dp, wp[5]), [pimg(), pvec(), vec_spec(ZERO)], [sds((B, SP, C), BF), sds((SUB, C), F32), sds((SUB, C), F32)],
-        [pimg(), fixed((SUB, C)), fixed((SUB, C))], grid=B // PI, flops=TEN**TEN, nbytes=T * C * FOUR)
-
-
-HAB = 1408
+HAB = 5632
+HAA = 5632
 
 
 def hconv_kernel(w_ref, o_ref):
@@ -646,8 +692,9 @@
 
 
 def head_kernel(*refs):
-    wall_ref, pooled_ref, bias_ref, lab_ref, dl_ref, gb_ref, loss_ref, dpool_ref, pall_ref, w, lg, pb, st, sta, dps, dpr, ws, ss, rs, ss2, rs2, ss3, rs3 = refs
-    pb[:] = pooled_ref[:].astype(BF)
+    wall_ref, pooled_ref, bias_ref, lab_ref, dl_ref, gb_ref, loss_ref, dpool_ref, pall_ref, sqh_ref, w, lg, pb, st, sta, dps, dpr, ws, ss, rs, ss2, rs2, ss3, rs3 = refs
+    for i in range(B // TWO):
+        pb[TWO * i:TWO * i + TWO, :] = pooled_ref[i].astype(BF)
     row0 = pl.multiple_of(KC * lax.axis_index(AX), KC)
     cw = [pltpu.make_async_copy(wall_ref.at[r, pl.ds(row0, KC)], w.at[r], ws.at[r]) for r in range(ND)]
     for c in cw:
@@ -704,17 +751,20 @@
         c.start()
         cs.append(c)
     dpr[me] = dps[me]
+    gram = dotg(pm, pm, NT) * dotg(dl_ref[:], dl_ref[:], TN)
+    sqh_ref[:] = sum8(gram[:, :LANE] + gram[:, LANE:])
     wait_all(cs)
     acc = dpr[ZERO]
     for k in range(ONE, ND):
         acc = acc + dpr[k]
-    dpool_ref[:] = acc
+    for i in range(B // TWO):
+        dpool_ref[i] = acc[TWO * i:TWO * i + TWO]
 
 
 def head(wall, pooled, wp, cid):
     n = (ND,)
     return run(head_kernel, (wall, pooled, wp[7], wp[6]), [HBM] + [VM] * THREE,
-        [sds((KC, NIMG), BF), sds((24, LANE), F32), sds((SUB, LANE), F32), sds((B, C), F32), sds((ND, B, C), BF)], [VM] * 5,
+        [sds((KC, NIMG), BF), sds((24, LANE), F32), sds((SUB, LANE), F32), sds((B // TWO, TWO, C), F32), sds((ND, B, C), BF), sds((SUB, LANE), F32)], [VM] * 6,
         scratch=[pltpu.VMEM((ND, KC, LANE), BF), pltpu.VMEM((KC, NIMG), F32), pltpu.VMEM((B, C), BF), pltpu.VMEM((SUB, NIMG), F32), pltpu.VMEM((ND, SUB, NIMG), F32), pltpu.VMEM((ND, B, C), F32), pltpu.VMEM((ND, B, C), F32)] + [SEM(n)] * 7,
         flops=TWO * TEN**TEN, cid=cid)
 
@@ -779,10 +829,9 @@
 PACK_SCR = [pltpu.VMEM((J, 256), F32), pltpu.VMEM((J, LANE), F32), pltpu.VMEM((J, LANE), F32), pltpu.VMEM((SMR, LANE), F32)]
 
 
-def pack_kernel(*refs):
+def pack_kernel(extra, *refs):
     ins = refs[:TEN]
-    gb_ref, dgf_ref, dsf_ref, o_ref, ws, wl, wh, xs = refs[TEN:]
-    me = lax.axis_index(AX)
+    o_ref, ws, wl, wh, xs = refs[-5:]
 
     def dst(r0, n, stride, v):
         if stride == ONE:
@@ -791,6 +840,10 @@
             o_ref[pl.ds(r0, n, stride=stride), :] = v
 
     pack_small(dst, *ins, ws, wl, wh, xs)
+    if not extra:
+        return
+    gb_ref, dgf_ref, dsf_ref = refs[TEN:13]
+    me = lax.axis_index(AX)
     base = ND * TP
     o_ref[base:, :] = jnp.zeros((SMF, LANE), F32)
     for r0, ref in ((ZERO, dgf_ref), (SUB, dsf_ref)):
@@ -800,8 +853,10 @@
     o_ref[pl.ds(base + 16 + KR * me, KR), :] = gb_ref[:KR, :]
 
 
-def pack(parts, gb, dgf, dsf):
-    return run(pack_kernel, tuple(parts) + (gb, dgf, dsf), [VM] * 13, sds((ND * TP + SMF, LANE), F32), VM, scratch=PACK_SCR)
+def pack(parts, extra=()):
+    ins = tuple(parts) + extra
+    rows = ND * TP + (SMF if extra else ZERO)
+    return run(functools.partial(pack_kernel, bool(extra)), ins, [VM] * len(ins), sds((rows, LANE), F32), VM, scratch=PACK_SCR)
 
 
 def untile(g_ref, o_ref, me, r0=ZERO):
@@ -820,7 +875,7 @@
     return go
 
 
-def fin_kernel(g_ref, tot_ref, sqh_ref, o_ref, sg_ref, sq_ref):
+def fin_kernel(g_ref, tot_ref, sqh_ref, o_ref, sg_ref, sq_ref, sp_ref):
     me = lax.axis_index(AX)
     go = untile(g_ref, o_ref, me)
     base = ND * TP
@@ -837,12 +892,14 @@
     def _():
         sq_ref[:] = go(C // LANE, acc)
 
+    sp_ref[:] = o_ref[RSH:RSH + SPR, :]
+
 
 def fin(g, tot, sqh):
-    return run(fin_kernel, (g, tot, sqh), [VM] * THREE, [sds((GROWS, LANE), F32), sds((SMD, LANE), F32), sds((SUB, LANE), F32)], [VM] * THREE)
-
-
-def finh_kernel(g_ref, sqi_ref, o_ref, sq_ref):
+    return run(fin_kernel, (g, tot, sqh), [VM] * THREE, [sds((GROWS, LANE), F32), sds((SMD, LANE), F32), sds((SUB, LANE), F32), sds((SPR, LANE), F32)], [VM] * FOUR)
+
+
+def finh_kernel(g_ref, sqi_ref, o_ref, sq_ref, sp_ref):
     me = lax.axis_index(AX)
     go = untile(g_ref, o_ref, me, UR // TWO)
 
@@ -854,26 +911,14 @@
     def _():
         sq_ref[:] = go(C // LANE, sqi_ref[:])
 
+    sp_ref[:] = o_ref[RSH:RSH + SPR, :]
+
 
 def finh(g, sqi):
-    return run(finh_kernel, (g, sqi), [VM] * TWO, [sds((GROWS, LANE), F32), sds((SUB, LANE), F32)], [VM] * TWO)
-
-
-def tail_kernel(*refs):
-    ins = refs[:TEN]
-    g_ref, sqi_ref, gl_ref, o_ref, sca_ref, ws, wl, wh, xs, xb, rb, sb, sqb, sqa, ss, rs, ss2, rs2, ss5, rs5, ss7, rs7 = refs[TEN:]
-
-    def dst(r0, n, stride, v):
-        if stride == ONE:
-            for q in range(ND):
-                a = max(r0, q * TP)
-                e = min(r0 + n, (q + ONE) * TP)
-                if a < e:
-                    xb[a:e, :] = v[a - r0:e - r0]
-        else:
-            xb[pl.ds(r0, n, stride=stride), :] = v
-
-    pack_small(dst, *ins, ws, wl, wh, xs)
+    return run(finh_kernel, (g, sqi), [VM] * TWO, [sds((GROWS, LANE), F32), sds((SUB, LANE), F32), sds((SPR, LANE), F32)], [VM] * THREE)
+
+
+def tail_kernel(xb, g_ref, sqi_ref, gl_ref, o_ref, sca_ref, rb, sb, sqb, sqa, ss, rs, ss2, rs2, ss5, rs5, ss7, rs7):
     me = entry_barrier()
 
     def part(q):
@@ -946,12 +991,12 @@
             rcopy(sb, o_ref.at[d], ss5, rs5.at[d], ZERO).wait_recv()
 
 
-def tail(parts, g, sqi, cid):
+def tail(x, g, sqi, cid):
     n = (ND,)
-    return run(tail_kernel, tuple(parts) + (g, sqi), [VM] * 12,
+    return run(tail_kernel, (x, g, sqi), [VM] * THREE,
         [sds((GROWS, LANE), F32), sds((ND, TP, LANE), F32), sds((SUB, LANE), F32)], [VM] * THREE,
-        scratch=PACK_SCR + [pltpu.VMEM((ND * TP, LANE), F32), pltpu.VMEM((ND, TP, LANE), F32), pltpu.VMEM((TP, LANE), F32), pltpu.VMEM((SUB, LANE), F32), pltpu.VMEM((ND, SUB, LANE), F32),
-            SEM(n), SEM(n), SEM, SEM(n), SEM, SEM(n), SEM(n), SEM(n)], cid=cid)
+        scratch=[pltpu.VMEM((ND, TP, LANE), F32), pltpu.VMEM((TP, LANE), F32), pltpu.VMEM((SUB, LANE), F32), pltpu.VMEM((ND, SUB, LANE), F32),
+            SEM(n), SEM(n), SEM, SEM(n), SEM, SEM(n), SEM(n), SEM(n)], cid=cid, vlim=VTAIL, flops=40 * TEN**9)
 
 
 def adam_math(p, m, v, g, decay):
@@ -962,24 +1007,7 @@
     return p - LEARN_RATE * (mh / (jnp.sqrt(vh) + ADAM_EPS) + decay * p), m2, v2
 
 
-HBR = 2816
-
-
-def head_gsq_kernel(dl_ref, p_ref, sqi_ref, sq_ref):
-    @on(pl.program_id(ZERO) == ZERO)
-    def _():
-        sq_ref[:] = sqi_ref[:]
-
-    g = dot(dl_ref[:], p_ref[:])
-    sq_ref[:] += sum8(g * g)
-
-
-def head_gsq(dl, pc, sq):
-    return run(head_gsq_kernel, (dl, pc, sq), [pl.BlockSpec((HBR, NIMG), lambda i: (i, ZERO)), fixed((NIMG, LANE)), fixed((SUB, LANE))],
-        sds((SUB, LANE), F32), fixed((SUB, LANE)), grid=ND, flops=TEN**9, nbytes=TEN**7)
-
-
-ABR = 656
+ABR = 2800
 NAB = -(-RSH // ABR)
 
 
@@ -989,9 +1017,9 @@
 
 
 def head_adam(sc, dl, pc, p, m, v):
-    blk = pl.BlockSpec((HAB, LANE), lambda i: (i, ZERO))
-    return run(head_adam_kernel, (sc, dl, pc, p, m, v), [SMEM, pl.BlockSpec((HAB, NIMG), lambda i: (i, ZERO)), fixed((NIMG, LANE)), blk, blk, blk],
-        [sds(p.shape, F32)] * THREE, [blk] * THREE, grid=-(-NCLS // HAB), flops=TEN**TEN, nbytes=8 * TEN**7)
+    blk = pl.BlockSpec((HAA, LANE), lambda i: (i, ZERO))
+    return run(head_adam_kernel, (sc, dl, pc, p, m, v), [SMEM, pl.BlockSpec((HAA, NIMG), lambda i: (i, ZERO)), fixed((NIMG, LANE)), blk, blk, blk],
+        [sds(p.shape, F32)] * THREE, [blk] * THREE, grid=-(-NCLS // HAA), flops=30 * TEN**9, nbytes=8 * TEN**7)
 
 
 def layer_adam_kernel(sc_ref, g0_ref, h0_ref, g1_ref, t0_ref, t1_ref, s0_ref, s1_ref, p_ref, m_ref, v_ref, po_ref, mo_ref, vo_ref, gs):
@@ -1003,7 +1031,7 @@
     ri = i * ABR + lax.broadcasted_iota(jnp.int32, (ABR, LANE), ZERO)
     gs[pl.ds(ZERO, ABR, stride=TWO), :] = jnp.where(ri < off + UR // TWO, g0_ref[:], h0_ref[:]) * sc
     gs[pl.ds(ONE, ABR, stride=TWO), :] = g1_ref[:] * sc
-    for b in range(THREE):
+    for b in range(-(-TOKR // ABR)):
         @on(i == b)
         def _():
             n = min(ABR, TOKR - b * ABR)
@@ -1055,31 +1083,35 @@
         p3 = rows3(layer_p)
         lab = jnp.pad(labels.astype(F32)[None, :], ((ZERO, SUB - ONE), (ZERO, LANE - B)))
         misc = jnp.concatenate([small_p.reshape(SMD, LANE), lab], axis=ZERO)
-        t0, t1, tok_all, sm_all, misc_all = start(p3, misc, ONE)
-        wg = [lax.all_gather(t, AX, tiled=True) for t in (t0, t1)]
-        wp = wprep(tok_all, sm_all, misc_all)
+        t0, t1, sh0, sh1, toks, tok1, sms, left0, left1 = prep(p3)
+        sh1 = lax.ppermute(sh1, AX, [(b, a) for a, b in up])
+        t0, tok0, sm_all, misc_all = start(sh0, toks, sms, misc, left0, t0, ONE)
+        t1 = fix(sh1, left1, t1)
+        wg = []
+        for t in (t0, t1):
+            wg.append(lax.all_gather(t, AX, tiled=True))
+        tok1 = lax.psum(tok1, AX)
+        wp = [wprep(ZERO, tok0, sm_all, misc_all)]
         hidden = act_in
         saved = []
         for l in range(TWO):
-            x1, n2, ta, tg = tok_fwd(hidden, wp, l)
+            x1, n2, ta, tg = tok_fwd(hidden, wp[l])
             if l == ZERO:
                 hw, x1 = lax.optimization_barrier((head_w, x1))
                 wall = lax.all_gather(hconv(hw.T), AX)
+                wp.append(wprep(ONE, tok1, sm_all, misc_all))
             x1 = x1.reshape(T, C)
             n2 = n2.reshape(T, C)
-            x2, act, gp = ch_fwd(n2, x1, wg[l], wp, l)
+            x2, act, gp, *pooled = ch_fwd(n2, x1, wg[l], wp[l], l)
             saved.append((hidden, ta, tg, x1, n2, act, gp))
             hidden = x2.reshape(B, SP, C)
-        pooled = pool(hidden, wp).reshape(B, C)
-        dl, gb, loss, dpool, pall = head(wall, pooled, wp, TWO)
+        dl, gb, loss, dpool, pall, sqh = head(wall, pooled[ZERO], wp[ZERO], TWO)
         dl_all = lax.all_gather(dl, AX, tiled=True)
         pc = lax.dynamic_slice_in_dim(pall.reshape(NIMG, C), LANE * me, LANE, axis=ONE)
-        d_out, dgf, dsf = lnf_bwd(hidden, dpool.reshape(B // PI, PI, C), wp)
-        d_out = d_out.reshape(T, C)
         for l in (ONE, ZERO):
             hid_in, ta, tg, x1, n2, act, gp = saved[l]
             if l:
-                dh, dbc1, dbc2 = ch_bwd_a(d_out, gp, wg[l])
+                dh, dbc1, dbc2, d_out, dgf, dsf = ch_bwd_top(x2, dpool, gp, wg[l], wp[l])
                 dh, dl_all = lax.optimization_barrier((dh, dl_all))
                 grad = dw1_call(n2, dh, dw2_call(act, d_out))
                 dh, grad = lax.optimization_barrier((dh, grad))
@@ -1088,31 +1120,31 @@
                 g2 = dw2_call(act, d_out, ONE)
                 g2, d_out = lax.optimization_barrier((g2, d_out))
                 dh, dbc1, dbc2 = ch_bwd_a(d_out, gp, wg[l])
+                dh, tot = lax.optimization_barrier((dh, tot))
                 grad = dw1_call(n2, dh, g2, ONE)
                 dh, grad, tot, act = lax.optimization_barrier((dh, grad, tot, act))
                 shard_b = scatter(grad, UR // TWO)
-                gl1, small_g, sq = fin(shard1, tot, jnp.zeros((SUB, LANE), F32))
-                sp1 = lax.ppermute(gl1[RSH:RSH + SPR], AX, up)
+                gl1, small_g, sq, sp1 = fin(shard1, tot, sqh)
+                sp1 = lax.ppermute(sp1, AX, up)
                 dh, sq, act = lax.optimization_barrier((dh, sq, act))
                 grad = dw1_call(n2, dh, dw2_call(act, d_out, ZERO), ZERO)
                 dh, grad = lax.optimization_barrier((dh, grad))
                 shard_a = scatter(grad, UR // TWO)
-            da, dg2, ds2 = ch_bwd_b(dh, wg[l], x1, d_out, wp, l)
+            da, dg2, ds2 = ch_bwd_b(dh, wg[l], x1, d_out, wp[l])
             if l == ZERO:
-                h0, sq = finh(shard_b, sq)
-                sp0 = lax.ppermute(h0[RSH:RSH + SPR], AX, up)
+                h0, sq, sp0 = finh(shard_b, sq)
+                sp0 = lax.ppermute(sp0, AX, up)
                 da, sq = lax.optimization_barrier((da, sq))
-            o = tok_bwd(hid_in, da.reshape(B, SP, C), ta, tg, wp, l)
+            o = tok_bwd(hid_in, da.reshape(B, SP, C), ta, tg, wp[l], l)
             if l:
                 d_out = o[ZERO].reshape(T, C)
                 o = o[ONE:]
             parts = tuple(o) + (dg2, ds2, dbc1, dbc2)
             if l:
-                sv, d_out = lax.optimization_barrier((pack(parts, gb, dgf, dsf), d_out))
+                sv, d_out = lax.optimization_barrier((pack(parts, (gb, dgf, dsf)), d_out))
                 tot = lax.psum(sv, AX)
-        dl_b, first, sp0 = lax.optimization_barrier((dl_all, parts[ZERO], sp0))
-        sq = head_gsq(dl_b, pc, sq)
-        gl0, tsm, sca = tail((first,) + parts[ONE:], shard_a, sq, FOUR)
+        px, sp0 = lax.optimization_barrier((pack(parts), sp0))
+        gl0, tsm, sca = tail(px, shard_a, sq, FOUR)
         np3, nm3, nv3 = layer_adam(sca, gl0, h0, gl1, tsm.reshape(ND * TP, LANE), tot, sp0, sp1, p3, rows3(layer_m), rows3(layer_v))
         nh, nhm, nhv = head_adam(sca, dl_all, pc, head_w.T, head_m.T, head_v.T)
         nsp, nsm, nsv = adam_math(small_p, small_m, small_v, small_g.reshape(SMD * LANE) * sca[ZERO, ZERO], 0.0)

time: 1580 us -> 1550 us (0.981)
  Pallas kernels: 1410 us -> 1360 us
    pallas_call x29 -> x30, Pallas kernels: 1410 us -> 1360 us  [run(): pl.pallas_call(body, in_specs=in_specs, out_specs=out_specs, out_shape=ou...]
  transfers between devices with their start and end apart: 10 -> 12, of which waited for: 2 -> 3; matrix products, arithmetic and copies ran while one was open for 2% -> 1% of each run, Pallas kernels for 69% -> 70%
where the time goes in v2:
time: 1550 us; the launch traced here: 1540 us
  Pallas kernels  1360 us (88%)
  waiting for transfers between devices  131 us (8%)
  local copies, waits for them, and re-layouts  22.3 us (1%)
    pallas_call x30, Pallas kernels, run(): pl.pallas_call(body, in_specs=in_specs, out_specs=out_specs, out_shape=ou...  1360 us
    reduce_scatter x3, waiting for transfers between devices, scatter(): lax.psum_scatter(grad.reshape(ND, n, LANE), AX, scatter_dimension=ZERO, t...  124 us
  transfers between devices with their start and end apart: 12, of which 3 were waited for; matrix products, arithmetic and copies ran while one was open for 1% of the time, Pallas kernels for 70%

profile of v2, /device:TPU:0, one launch (start us, length us, event | category | flops | bytes accessed | tf_op | source)
XLA Modules:
  0.0 1542.1 jit_solution(15335065468757742389)
XLA Ops:
  20.1 20.6 %shard_map.187 = (bf16[512,16,128]{2,1,0:T(8,128)(2,1)}, bf16[8,196,128]{2,1,0:T(8,128)(2,1)}, bf16[2,80,128]{2,1,0:T(8,128)(2,1)}, f32[8,32,128]{2,1,0:T(8,128)}) custom-call(bf16[1368,128]{1,0:T(8,128)(2,1)} %get-tuple-element.127.shs, bf16[8,196,128]{2,1,0:T(8,128)(2,1)} %get-tuple-element.128.toks, ...), custom_call_target="tpu_custom_call", output_to_operand_aliasing={{0}: (5, {})} | custom-call | flops 10000000000 | bytes 1000000 | tf_op jit(solution)/shard_map/pallas_call | solution.py:85
  54.8 11.3 copy.28.x_ref
  68.9 77.3 %shard_map.189 = (bf16[32,200,1024]{2,1,0:T(8,128)(2,1)}, bf16[32,200,1024]{2,1,0:T(8,128)(2,1)}, bf16[32,512,1024]{2,1,0:T(8,128)(2,1)}, f32[32,512,1024]{2,1,0:T(8,128)}) custom-call(bf16[32,196,1024]{2,1,0:T(8,128)(2,1)} %copy.28.x_ref, bf16[1,512,200]{2,1,0:T(8,128)(2,1)} %get-tuple-element.135.w1t_ref, bf16[1,200,512]{2,1,0:T(8,128)(2,1)} %get-tuple-element.136.w2t_ref, ...), custom_call_target="tpu_custom_call" | custom-call | flops 60000002048 | bytes 140000000 | tf_op jit(solution)/shard_map/pallas_call | solution.py:85
  156.7 144.3 %shard_map.191 = (bf16[6400,1024]{1,0:T(8,128)(2,1)}, bf16[6400,4096]{1,0:T(8,128)(2,1)}, f32[6400,4096]{1,0:T(8,128)}) custom-call(bf16[6400,1024]{1,0:T(8,128)(2,1)} %bitcast.63, bf16[6400,1024]{1,0:T(8,128)(2,1)} %bitcast.102, bf16[128,32,16,128]{3,2,1,0:T(8,128)(2,1)} %bitcast.88, bf16[512,8,16,128]{3,2,1,0:T(8,128)(2,1)} %bitcast.89, ...), custom_call_target="tpu_custom_call" | custom-call | flops 107374182400 | bytes 157286400 | tf_op jit(solution)/shard_map/pallas_call | solution.py:85
  301.0 77.7 %shard_map.193 = (bf16[32,200,1024]{2,1,0:T(8,128)(2,1)}, bf16[32,200,1024]{2,1,0:T(8,128)(2,1)}, bf16[32,512,1024]{2,1,0:T(8,128)(2,1)}, f32[32,512,1024]{2,1,0:T(8,128)}) custom-call(bf16[32,200,1024]{2,1,0:T(8,128)(2,1)} %bitcast.108, bf16[1,512,200]{2,1,0:T(8,128)(2,1)} %get-tuple-element.146.w1t_ref, bf16[1,200,512]{2,1,0:T(8,128)(2,1)} %get-tuple-element.147.w2t_ref, ...), custom_call_target="tpu_custom_call" | custom-call | flops 60000002048 | bytes 140000000 | tf_op jit(solution)/shard_map/pallas_call | solution.py:85
  378.8 155.9 %shard_map.195 = (bf16[6400,1024]{1,0:T(8,128)(2,1)}, bf16[6400,4096]{1,0:T(8,128)(2,1)}, f32[6400,4096]{1,0:T(8,128)}, f32[16,2,1024]{2,1,0:T(2,128)}) custom-call(bf16[6400,1024]{1,0:T(8,128)(2,1)} %bitcast.112, bf16[6400,1024]{1,0:T(8,128)(2,1)} %bitcast.110, bf16[128,32,16,128]{3,2,1,0:T(8,128)(2,1)} %bitcast.92, bf16[512,8,16,128]{3,2,1,0:T(8,128)(2,1)} %bitcast.93, ...), custom_call_target="tpu_custom_call" | custom-call | flops 107374182400 | bytes 157286400 | tf_op jit(solution)/shard_map/pallas_call | solution.py:85
  534.6 34.4 %shard_map.196 = (bf16[2816,256]{1,0:T(8,128)(2,1)}, f32[24,128]{1,0:T(8,128)}, f32[8,128]{1,0:T(8,128)}, f32[16,2,1024]{2,1,0:T(2,128)}, bf16[8,32,1024]{2,1,0:T(8,128)(2,1)}, /*index=5*/f32[8,128]{1,0:T(8,128)}) custom-call(bf16[8,22528,128]{2,1,0:T(8,128)(2,1)} %bitcast.87, f32[16,2,1024]{2,1,0:T(2,128)} %get-tuple-element.155.refs_1_, ...), custom_call_target="tpu_custom_call" | custom-call | flops 20000000000 | bytes 1000000 | tf_op jit(solution)/shard_map/pallas_call | solution.py:85
  569.1 83.4 %shard_map.197 = (bf16[6400,4096]{1,0:T(8,128)(2,1)}, f32[8,4096]{1,0:T(8,128)}, f32[8,1024]{1,0:T(8,128)}, bf16[6400,1024]{1,0:T(8,128)(2,1)}, f32[8,1024]{1,0:T(8,128)}, /*index=5*/f32[8,1024]{1,0:T(8,128)}) custom-call(bf16[6400,1024]{1,0:T(8,128)(2,1)} %get-tuple-element.160.x2_ref, f32[16,2,1024]{2,1,0:T(2,128)} %get-tuple-element.161.dp_ref, ...), custom_call_target="tpu_custom_call" | custom-call | flops 53687091200 | bytes 157286400 | tf_op jit(solution)/shard_map/pallas_call | solution.py:85
  652.5 63.7 %shard_map.198 = f32[8,128,8,8,128]{4,3,2,1,0:T(8,128)} custom-call(bf16[6400,4096]{1,0:T(8,128)(2,1)} %get-tuple-element.166.a_ref, bf16[6400,1024]{1,0:T(8,128)(2,1)} %get-tuple-element.167.b_ref.do_ref), custom_call_target="tpu_custom_call" | custom-call | flops 53687091200 | bytes 78643200 | tf_op jit(solution)/shard_map/pallas_call | solution.py:85
  716.2 63.8 %shard_map.199 = f32[8,32,32,8,128]{4,3,2,1,0:T(8,128)} custom-call(bf16[6400,1024]{1,0:T(8,128)(2,1)} %bitcast.113, bf16[6400,4096]{1,0:T(8,128)(2,1)} %get-tuple-element.168.refs_1_.dh_ref, f32[8,32,32,8,128]{4,3,2,1,0:T(8,128)} %bitcast.78), custom_call_target="tpu_custom_call", output_to_operand_aliasing={{}: (2, {})} | custom-call | flops 53687091200 | bytes 78643200 | tf_op jit(solution)/shard_map/pallas_call | solution.py:85
  780.0 78.4 %shard_map.200 = (bf16[6400,1024]{1,0:T(8,128)(2,1)}, f32[8,1024]{1,0:T(8,128)}, f32[8,1024]{1,0:T(8,128)}) custom-call(bf16[6400,4096]{1,0:T(8,128)(2,1)} %get-tuple-element.168.refs_1_.dh_ref, bf16[128,32,16,128]{3,2,1,0:T(8,128)(2,1)} %bitcast.95, bf16[6400,1024]{1,0:T(8,128)(2,1)} %bitcast.111, bf16[6400,1024]{1,0:T(8,128)(2,1)} %get-tuple-element.167.b_ref.do_ref, ...), custom_call_target="tpu_custom_call" | custom-call | flops 53687091200 | bytes 78643200 | tf_op jit(solution)/shard_map/pallas_call | solution.py:85
  858.4 74.6 %shard_map.201 = (bf16[32,200,1024]{2,1,0:T(8,128)(2,1)}, f32[512,200]{1,0:T(8,128)}, f32[512,200]{1,0:T(8,128)}, f32[512,128]{1,0:T(8,128)}, f32[200,128]{1,0:T...) custom-call(bf16[32,200,1024]{2,1,0:T(8,128)(2,1)} %bitcast.109, bf16[32,200,1024]{2,1,0:T(8,128)(2,1)} %bitcast.115, ...), custom_call_target="tpu_custom_call" | custom-call | flops 60000002048 | bytes 140000000 | tf_op jit(solution)/shard_map/pallas_call | solution.py:85
  936.9 36.2 %shard_map.203 = f32[8,64,8,8,128]{4,3,2,1,0:T(8,128)} custom-call(bf16[6400,4096]{1,0:T(8,128)(2,1)} %get-tuple-element.203.a_ref, bf16[6400,1024]{1,0:T(8,128)(2,1)} %bitcast.104), custom_call_target="tpu_custom_call" | custom-call | flops 26843545600 | bytes 78643200 | tf_op jit(solution)/shard_map/pallas_call | solution.py:85
  973.1 78.1 %shard_map.204 = (bf16[6400,4096]{1,0:T(8,128)(2,1)}, f32[8,4096]{1,0:T(8,128)}, f32[8,1024]{1,0:T(8,128)}) custom-call(bf16[6400,1024]{1,0:T(8,128)(2,1)} %bitcast.105, f32[6400,4096]{1,0:T(8,128)} %get-tuple-element.190.gp_ref, bf16[512,8,16,128]{3,2,1,0:T(8,128)(2,1)} %bitcast.90), custom_call_target="tpu_custom_call" | custom-call | flops 53687091200 | bytes 157286400 | tf_op jit(solution)/shard_map/pallas_call | solution.py:85
  1051.2 34.9 %shard_map.205 = f32[8,16,32,8,128]{4,3,2,1,0:T(8,128)} custom-call(bf16[6400,1024]{1,0:T(8,128)(2,1)} %bitcast.64, bf16[6400,1024]{1,0:T(8,128)(2,1)} %bitcast.65, bf16[6400,1024]{1,0:T(8,128)(2,1)} %bitcast.66, bf16[6400,1024]{1,0:T(8,128)(2,1)} %bitcast.67, bf16[6400,4096]{1,0:T(8,128)(2,1)} %get-tuple-element.204.refs_4_.dh_ref, ...), custom_call_target="tpu_custom_call", output_to_operand_aliasing={{}: (5, {})} | custom-call | flops 26843545600 | bytes 78643200 | tf_op jit(solution)/shard_map/pallas_call | solution.py:85
  1086.1 97.6 %reduce-scatter.4.cloned.1.call-done = f32[1,8192,128]{2,1,0:T(8,128)} async-done(((f32[8,8192,128]{2,1,0:T(8,128)}), f32[1,8192,128]{2,1,0:T(8,128)}) %reduce-scatter.4.cloned.1.call-update) | async-done | bytes 4194320 | tf_op jit(solution)/shard_map/reduce_scatter | solution.py:1079
  1191.5 39.8 %shard_map.207 = f32[8,64,8,8,128]{4,3,2,1,0:T(8,128)} custom-call(bf16[6400,4096]{1,0:T(8,128)(2,1)} %get-tuple-element.203.a_ref, bf16[6400,1024]{1,0:T(8,128)(2,1)} %bitcast.106), custom_call_target="tpu_custom_call" | custom-call | flops 26843545600 | bytes 78643200 | tf_op jit(solution)/shard_map/pallas_call | solution.py:85
  1231.3 34.8 %shard_map.208 = f32[8,16,32,8,128]{4,3,2,1,0:T(8,128)} custom-call(bf16[6400,1024]{1,0:T(8,128)(2,1)} %bitcast.68, bf16[6400,1024]{1,0:T(8,128)(2,1)} %bitcast.69, bf16[6400,1024]{1,0:T(8,128)(2,1)} %bitcast.70, bf16[6400,1024]{1,0:T(8,128)(2,1)} %bitcast.71, bf16[6400,4096]{1,0:T(8,128)(2,1)} %get-tuple-element.204.refs_4_.dh_ref, ...), custom_call_target="tpu_custom_call", output_to_operand_aliasing={{}: (5, {})} | custom-call | flops 26843545600 | bytes 78643200 | tf_op jit(solution)/shard_map/pallas_call | solution.py:85
  1268.9 26.3 %reduce-scatter.6.cloned.1.call-done = f32[1,4096,128]{2,1,0:T(8,128)} async-done(((f32[8,4096,128]{2,1,0:T(8,128)}), f32[1,4096,128]{2,1,0:T(8,128)}) %reduce-scatter.6.cloned.1.call-update) | async-done | bytes 2097168 | tf_op jit(solution)/shard_map/reduce_scatter | solution.py:1079
  1300.5 80.5 %shard_map.209 = (bf16[6400,1024]{1,0:T(8,128)(2,1)}, f32[8,1024]{1,0:T(8,128)}, f32[8,1024]{1,0:T(8,128)}) custom-call(bf16[6400,4096]{1,0:T(8,128)(2,1)} %get-tuple-element.204.refs_4_.dh_ref, bf16[128,32,16,128]{3,2,1,0:T(8,128)(2,1)} %bitcast.91, bf16[6400,1024]{1,0:T(8,128)(2,1)} %bitcast.103, bf16[6400,1024]{1,0:T(8,128)(2,1)} %bitcast.107, ...), custom_call_target="tpu_custom_call" | custom-call | flops 53687091200 | bytes 78643200 | tf_op jit(solution)/shard_map/pallas_call | solution.py:85
  1382.8 68.3 %shard_map.211 = (f32[512,200]{1,0:T(8,128)}, f32[512,200]{1,0:T(8,128)}, f32[512,128]{1,0:T(8,128)}, f32[200,128]{1,0:T(8,128)}, f32[8,1024]{1,0:T(8,128)}, /*index=5*/f32[8,1024]{1,0:T(8,128)}) custom-call(bf16[32,196,1024]{2,1,0:T(8,128)(2,1)} %copy.28.x_ref, bf16[32,200,1024]{2,1,0:T(8,128)(2,1)} %bitcast.114, ...), custom_call_target="tpu_custom_call" | custom-call | flops 60000002048 | bytes 140000000 | tf_op jit(solution)/shard_map/pallas_call | solution.py:85
  1457.6 18.9 %shard_map.213 = (f32[9768,128]{1,0:T(8,128)S(1)}, f32[8,208,128]{2,1,0:T(8,128)S(1)}, f32[8,128]{1,0:T(8,128)S(1)}) custom-call(f32[1664,128]{1,0:T(8,128)S(1)} %copy-done.4, f32[512,8,128]{2,1,0:T(8,128)S(1)} %bitcast.62, f32[8,128]{1,0:T(8,128)S(1)} %copy-done.5), custom_call_target="tpu_custom_call" | custom-call | flops 40000000000 | bytes 1000000 | tf_op jit(solution)/shard_map/pallas_call | solution.py:85
  1480.3 25.8 %shard_map.215 = (f32[21843,128]{1,0:T(8,128)}, f32[21843,128]{1,0:T(8,128)}, f32[21843,128]{1,0:T(8,128)}) custom-call(f32[8,128]{1,0:T(8,128)} %copy-done.2, bf16[22528,256]{1,0:T(8,128)(2,1)} %all-gather.10.cloned.1.call-done.dl_ref, bf16[256,128]{1,0:T(8,128)(2,1)} %constant_dynamic-slice_fusion.pc_ref, f32[21843,128]{1,0:T(8,128)} %bitcast.81, ...), custom_call_target="tpu_custom_call" | custom-call | flops 30000001024 | bytes 80000000 | tf_op jit(solution)/shard_map/pallas_call | solution.py:85
  1509.3 26.0 %shard_map.214 = (f32[8398,2,128]{2,1,0:T(2,128)}, f32[8398,2,128]{2,1,0:T(2,128)}, f32[8398,2,128]{2,1,0:T(2,128)}) custom-call(f32[8,128]{1,0:T(8,128)} %copy-done.2, f32[9768,128]{1,0:T(8,128)} %copy-done, f32[9768,128]{1,0:T(8,128)} %get-tuple-element.230.h0_ref, f32[9768,128]{1,0:T(8,128)} %get-tuple-element.231.g1_ref, f32[1664,128]{1,0:T(8,128)} %bitcast.61, ...), custom_call_target="tpu_custom_call" | custom-call | flops 1000000000 | bytes 60000000 | tf_op jit(solution)/shard_map/pallas_call | solution.py:85
  (58 shorter events, 75.4 us)
Async XLA Ops:
  7.2 146.6 %all-reduce.4.cloned.1.call-start = ((), (), s32[]{:S(2)}) async-start(), calls=%async_computation.4 | async-start | bytes 1605632 | tf_op jit(solution)/shard_map/psum | solution.py:1093
  18.1 138.6 %all-gather.6.cloned.1.call-start = ((), (), s32[]{:S(2)}) async-start(), calls=%async_computation.3 | async-start | bytes 18874368 | tf_op jit(solution)/shard_map/all_gather | solution.py:1092
  40.7 338.1 %all-gather.8.cloned.1.call-start = ((), (), s32[]{:S(2)}) async-start(), calls=%async_computation.5 | async-start | bytes 18874368 | tf_op jit(solution)/shard_map/all_gather | solution.py:1092
  40.8 11.4 collective-permute-start
  54.7 479.9 %all-gather.12.cloned.1.call-start = ((), (), s32[]{:S(2)}) async-start(), calls=%async_computation.11 | async-start | bytes 51904512 | tf_op jit(solution)/shard_map/all_gather | solution.py:1101
  153.6 562.6 %all-gather.10.cloned.1.call-start = ((), (), s32[]{:S(2)}) async-start(), calls=%async_computation.6 | async-start | bytes 12976128 | tf_op jit(solution)/shard_map/all_gather | solution.py:1109
  569.1 482.1 %all-reduce.6.cloned.1.call-start = ((), (), s32[]{:S(2)}) async-start(), calls=%async_computation.7 | async-start | bytes 1900544 | tf_op jit(solution)/shard_map/psum | solution.py:1145
  936.1 247.6 %reduce-scatter.4.cloned.1.call-start = ((), (), s32[]{:S(2)}) async-start(), calls=%async_computation.8 | async-start | bytes 37748736 | tf_op jit(solution)/shard_map/reduce_scatter | solution.py:1079
  936.9 358.3 %reduce-scatter.6.cloned.1.call-start = ((), (), s32[]{:S(2)}) async-start(), calls=%async_computation.9 | async-start | bytes 18874368 | tf_op jit(solution)/shard_map/reduce_scatter | solution.py:1079
  1086.1 368.1 %reduce-scatter.8.cloned.1.call-start = ((), (), s32[]{:S(2)}) async-start(), calls=%async_computation.10 | async-start | bytes 18874368 | tf_op jit(solution)/shard_map/reduce_scatter | solution.py:1079
  1381.0 73.2 %collective-permute-start.1 = (f32[1368,128]{1,0:T(8,128)}, f32[1368,128]{1,0:T(8,128)}, u32[]{:S(2)}, u32[]{:S(2)}) collective-permute-start(f32[1368,128]{1,0:T(8,128)} %get-tuple-element.224), channel_id=1, source_target_pairs={{0,1},{1,2},{2,3},{3,4},{4,5},{5,6},{6,7},{7,0}} | collective-permute-start | bytes 2101256 | tf_op jit(solution)/shard_map/ppermute | solution.py:1136
  1381.0 128.3 %collective-permute-start.2 = (f32[1368,128]{1,0:T(8,128)}, f32[1368,128]{1,0:T(8,128)}, u32[]{:S(2)}, u32[]{:S(2)}) collective-permute-start(f32[1368,128]{1,0:T(8,128)} %get-tuple-element.234), channel_id=1, source_target_pairs={{0,1},{1,2},{2,3},{3,4},{4,5},{5,6},{6,7},{7,0}} | collective-permute-start | bytes 2101256 | tf_op jit(solution)/shard_map/ppermute | solution.py:1128
  1454.2 1.6 copy-start.3
  1455.8 1.2 copy-start.4
  1456.9 0.7 copy-start.5
  1476.5 2.3 copy-start
  1478.8 0.9 copy-start.1
  1479.7 0.6 copy-start.2
Sparse Core Ops, SparseCore 0:
  18.2 51.5 all-reduce.3
  71.6 83.5 all-gather.5
  157.6 84.1 all-gather.7
  244.1 208.9 all-gather.11
  569.2 63.3 all-gather.9
  936.3 47.5 all-reduce.5
  987.4 196.3 reduce-scatter.3
  1187.3 107.8 reduce-scatter.5
  1298.7 118.2 reduce-scatter.7

commit v3 on v2

--- a/solution.py
+++ b/solution.py
@@ -196,6 +196,8 @@
 
 
 TQ = TOKR // ND
+HCH = FOUR
+HAB = ND * KC // HCH
 
 
 def prep_kernel(p_ref, o0_ref, o1_ref, shs0_ref, shs1_ref, toks_ref, tok1_ref, sms_ref, left0_ref, left1_ref):
@@ -257,7 +259,12 @@
     return run(fix_kernel, (shr, left, t), [VM, VM, HBM], sds(t.shape, BF), HBM, scratch=LAST_SCR + [SEM], alias={TWO: ZERO})
 
 
-def start_kernel(shs, toks, sms, misc_ref, left_ref, u_ref, o_ref, tok_o, sm_o, misc_o, z, w, shr, ss_m, rs_m, ss_s, rs_s, ss_t, rs_t, ss_u, ss_h, rs_h, ss_w):
+def start_kernel(shs, toks, sms, misc_ref, left_ref, u_ref, hw_ref, o_ref, tok_o, sm_o, misc_o, hb_ref, hin, hout, hsem, z, w, shr, ss_m, rs_m, ss_s, rs_s, ss_t, rs_t, ss_u, ss_h, rs_h, ss_w):
+    rows = [min(HAB, NCLS - k * HAB) for k in range(HCH)]
+    cin = [pltpu.make_async_copy(hw_ref.at[pl.ds(k * HAB, n)], hin.at[k, pl.ds(ZERO, n)], hsem.at[ZERO, k]) for k, n in enumerate(rows)]
+    cout = [pltpu.make_async_copy(hout.at[k], hb_ref.at[pl.ds(k * HAB, HAB)], hsem.at[ONE, k]) for k in range(HCH)]
+    for c in cin:
+        c.start()
     me = entry_barrier()
     sh = rcopy(shs, shr, ss_h, rs_h, lax.rem(me + ND - ONE, ND))
     sh.start()
@@ -297,6 +304,13 @@
         for d in range(ONE, ND - ONE):
             piece(me, d).start()
 
+    for k in range(HCH):
+        cin[k].wait()
+        v = hin[k]
+        if rows[k] < HAB:
+            v = jnp.where(lax.broadcasted_iota(jnp.int32, (HAB, LANE), ZERO) < rows[k], v, 0.0)
+        hout[k] = v.astype(BF)
+        cout[k].start()
     sh.wait()
     last_units(me, left_ref, shr, z, w)
     cw = put_last(w, o_ref, ss_w)
@@ -325,13 +339,14 @@
             small(d).wait_send()
 
     cw.wait()
-
-
-def start(shs, toks, sms, misc, left, t, cid):
+    wait_all(cout)
+
+
+def start(shs, toks, sms, misc, left, t, hw, cid):
     n = (ND,)
-    return run(start_kernel, (shs, toks, sms, misc, left, t), [VM] * 5 + [HBM],
-        [sds(t.shape, BF), sds(toks.shape, BF), sds(sms.shape, BF), sds(n + misc.shape, F32)], [HBM] + [VM] * THREE,
-        scratch=LAST_SCR + [pltpu.VMEM((SPR, LANE), BF), SEM(n), SEM(n), SEM(n), SEM, SEM(n), SEM(n), SEM(n), SEM, SEM, SEM],
+    return run(start_kernel, (shs, toks, sms, misc, left, t, hw), [VM] * 5 + [HBM] * TWO,
+        [sds(t.shape, BF), sds(toks.shape, BF), sds(sms.shape, BF), sds(n + misc.shape, F32), sds((ND * KC, LANE), BF)], [HBM] + [VM] * THREE + [HBM],
+        scratch=[pltpu.VMEM((HCH, HAB, LANE), F32), pltpu.VMEM((HCH, HAB, LANE), BF), SEM((TWO, HCH))] + LAST_SCR + [pltpu.VMEM((SPR, LANE), BF), SEM(n), SEM(n), SEM(n), SEM, SEM(n), SEM(n), SEM(n), SEM, SEM, SEM],
         alias={5: ZERO}, flops=TEN**TEN, cid=cid)
 
 
@@ -675,20 +690,6 @@
     return run(dw1_kernel, (n2,) * na + (dh, g.reshape(shape)), specs + [pl.BlockSpec((T, DC), lambda i: (ZERO, i)), HBM],
         sds(shape, F32), pl.BlockSpec((own, rb, DC // LANE, SUB, LANE), lambda i: (ZERO, ZERO, i, ZERO, ZERO)), alias={na + ONE: ZERO},
         grid=D // DC, flops=TWO * T * (rb * 32) * D, nbytes=T * D * THREE)
-
-
-HAB = 5632
-HAA = 5632
-
-
-def hconv_kernel(w_ref, o_ref):
-    r = pl.program_id(ZERO) * HAB + lax.broadcasted_iota(jnp.int32, (HAB, LANE), ZERO)
-    o_ref[:] = jnp.where(r < NCLS, w_ref[:], 0.0).astype(BF)
-
-
-def hconv(wt):
-    blk = pl.BlockSpec((HAB, LANE), lambda i: (i, ZERO))
-    return run(hconv_kernel, (wt,), [blk], sds((ND * KC, LANE), BF), blk, grid=ND * KC // HAB, nbytes=TWO * TEN**7)
 
 
 def head_kernel(*refs):
@@ -994,7 +995,7 @@
 def tail(x, g, sqi, cid):
     n = (ND,)
     return run(tail_kernel, (x, g, sqi), [VM] * THREE,
-        [sds((GROWS, LANE), F32), sds((ND, TP, LANE), F32), sds((SUB, LANE), F32)], [VM] * THREE,
+        [sds((TOKR + UR // TWO + SUB, LANE), F32), sds((ND, TP, LANE), F32), sds((SUB, LANE), F32)], [VM] * THREE,
         scratch=[pltpu.VMEM((ND, TP, LANE), F32), pltpu.VMEM((TP, LANE), F32), pltpu.VMEM((SUB, LANE), F32), pltpu.VMEM((ND, SUB, LANE), F32),
             SEM(n), SEM(n), SEM, SEM(n), SEM, SEM(n), SEM(n), SEM(n)], cid=cid, vlim=VTAIL, flops=40 * TEN**9)
 
@@ -1008,6 +1009,7 @@
 
 
 ABR = 2800
+HAA = 5632
 NAB = -(-RSH // ABR)
 
 
@@ -1064,7 +1066,7 @@
     blk = pl.BlockSpec((ABR, TWO, LANE), lambda i: (i, ZERO, ZERO))
     gb = pl.BlockSpec((ABR, LANE), lambda i: (i, ZERO))
     return run(layer_adam_kernel, (sc, g0, h0, g1, t0, t1, s0, s1, p, m, v),
-        [SMEM, gb, gb, gb] + [fixed(t.shape) for t in (t0, t1, s0, s1)] + [blk] * THREE, [sds(p.shape, F32)] * THREE, [blk] * THREE,
+        [SMEM, gb, pl.BlockSpec((ABR, LANE), lambda i: (jnp.maximum(i, ONE), ZERO)), gb] + [fixed(t.shape) for t in (t0, t1, s0, s1)] + [blk] * THREE, [sds(p.shape, F32)] * THREE, [blk] * THREE,
         scratch=[pltpu.VMEM((TWO * ABR, LANE), F32)], grid=NAB, nbytes=6 * TEN**7)
 
 
@@ -1085,7 +1087,7 @@
         misc = jnp.concatenate([small_p.reshape(SMD, LANE), lab], axis=ZERO)
         t0, t1, sh0, sh1, toks, tok1, sms, left0, left1 = prep(p3)
         sh1 = lax.ppermute(sh1, AX, [(b, a) for a, b in up])
-        t0, tok0, sm_all, misc_all = start(sh0, toks, sms, misc, left0, t0, ONE)
+        t0, tok0, sm_all, misc_all, hb = start(sh0, toks, sms, misc, left0, t0, head_w.T, ONE)
         t1 = fix(sh1, left1, t1)
         wg = []
         for t in (t0, t1):
@@ -1097,8 +1099,7 @@
         for l in range(TWO):
             x1, n2, ta, tg = tok_fwd(hidden, wp[l])
             if l == ZERO:
-                hw, x1 = lax.optimization_barrier((head_w, x1))
-                wall = lax.all_gather(hconv(hw.T), AX)
+                wall = lax.all_gather(hb, AX)
                 wp.append(wprep(ONE, tok1, sm_all, misc_all))
             x1 = x1.reshape(T, C)
             n2 = n2.reshape(T, C)

time: 1550 us -> 1540 us (level)
    pallas_call x30 -> x29, Pallas kernels: 1360 us -> 1350 us  [run(): pl.pallas_call(body, in_specs=in_specs, out_specs=out_specs, out_shape=ou...]
  transfers between devices with their start and end apart: 12 -> 12, of which waited for: 3 -> 4; matrix products, arithmetic and copies ran while one was open for 1% -> 1% of each run, Pallas kernels for 70% -> 69%
where the time goes in v3:
time: 1540 us
  Pallas kernels  1350 us (88%)
  waiting for transfers between devices  137 us (9%)
  local copies, waits for them, and re-layouts  21.7 us (1%)
    pallas_call x29, Pallas kernels, run(): pl.pallas_call(body, in_specs=in_specs, out_specs=out_specs, out_shape=ou...  1350 us
    reduce_scatter x3, waiting for transfers between devices, scatter(): lax.psum_scatter(grad.reshape(ND, n, LANE), AX, scatter_dimension=ZERO, t...  124 us
  transfers between devices with their start and end apart: 12, of which 4 were waited for; matrix products, arithmetic and copies ran while one was open for 1% of the time, Pallas kernels for 69%

profile of v3, /device:TPU:0, one launch (start us, length us, event | category | flops | bytes accessed | tf_op | source)
XLA Modules:
  0.0 1536.1 jit_solution(2904773339795386087)
XLA Ops:
  20.1 20.7 %shard_map.187 = (bf16[512,16,128]{2,1,0:T(8,128)(2,1)}, bf16[8,196,128]{2,1,0:T(8,128)(2,1)}, bf16[2,80,128]{2,1,0:T(8,128)(2,1)}, f32[8,32,128]{2,1,0:T(8,128)}, bf16[22528,128]{1,0:T(8,128)(2,1)}) custom-call(bf16[1368,128]{1,0:T(8,128)(2,1)} %get-tuple-element.126.shs, ...), custom_call_target="tpu_custom_call", output_to_operand_aliasing={{0}: (5, {})} | custom-call | flops 10000000000 | bytes 1000000 | tf_op jit(solution)/shard_map/pallas_call | solution.py:85
  55.4 11.3 copy.28.x_ref
  69.5 77.3 %shard_map.189 = (bf16[32,200,1024]{2,1,0:T(8,128)(2,1)}, bf16[32,200,1024]{2,1,0:T(8,128)(2,1)}, bf16[32,512,1024]{2,1,0:T(8,128)(2,1)}, f32[32,512,1024]{2,1,0:T(8,128)}) custom-call(bf16[32,196,1024]{2,1,0:T(8,128)(2,1)} %copy.28.x_ref, bf16[1,512,200]{2,1,0:T(8,128)(2,1)} %get-tuple-element.135.w1t_ref, bf16[1,200,512]{2,1,0:T(8,128)(2,1)} %get-tuple-element.136.w2t_ref, ...), custom_call_target="tpu_custom_call" | custom-call | flops 60000002048 | bytes 140000000 | tf_op jit(solution)/shard_map/pallas_call | solution.py:85
  155.3 143.7 %shard_map.190 = (bf16[6400,1024]{1,0:T(8,128)(2,1)}, bf16[6400,4096]{1,0:T(8,128)(2,1)}, f32[6400,4096]{1,0:T(8,128)}) custom-call(bf16[6400,1024]{1,0:T(8,128)(2,1)} %bitcast.62, bf16[6400,1024]{1,0:T(8,128)(2,1)} %bitcast.101, bf16[128,32,16,128]{3,2,1,0:T(8,128)(2,1)} %bitcast.85, bf16[512,8,16,128]{3,2,1,0:T(8,128)(2,1)} %bitcast.86, ...), custom_call_target="tpu_custom_call" | custom-call | flops 107374182400 | bytes 157286400 | tf_op jit(solution)/shard_map/pallas_call | solution.py:85
  299.0 77.7 %shard_map.192 = (bf16[32,200,1024]{2,1,0:T(8,128)(2,1)}, bf16[32,200,1024]{2,1,0:T(8,128)(2,1)}, bf16[32,512,1024]{2,1,0:T(8,128)(2,1)}, f32[32,512,1024]{2,1,0:T(8,128)}) custom-call(bf16[32,200,1024]{2,1,0:T(8,128)(2,1)} %bitcast.107, bf16[1,512,200]{2,1,0:T(8,128)(2,1)} %get-tuple-element.144.w1t_ref, bf16[1,200,512]{2,1,0:T(8,128)(2,1)} %get-tuple-element.145.w2t_ref, ...), custom_call_target="tpu_custom_call" | custom-call | flops 60000002048 | bytes 140000000 | tf_op jit(solution)/shard_map/pallas_call | solution.py:85
  376.7 155.9 %shard_map.194 = (bf16[6400,1024]{1,0:T(8,128)(2,1)}, bf16[6400,4096]{1,0:T(8,128)(2,1)}, f32[6400,4096]{1,0:T(8,128)}, f32[16,2,1024]{2,1,0:T(2,128)}) custom-call(bf16[6400,1024]{1,0:T(8,128)(2,1)} %bitcast.111, bf16[6400,1024]{1,0:T(8,128)(2,1)} %bitcast.109, bf16[128,32,16,128]{3,2,1,0:T(8,128)(2,1)} %bitcast.89, bf16[512,8,16,128]{3,2,1,0:T(8,128)(2,1)} %bitcast.90, ...), custom_call_target="tpu_custom_call" | custom-call | flops 107374182400 | bytes 157286400 | tf_op jit(solution)/shard_map/pallas_call | solution.py:85
  532.6 31.4 %shard_map.195 = (bf16[2816,256]{1,0:T(8,128)(2,1)}, f32[24,128]{1,0:T(8,128)}, f32[8,128]{1,0:T(8,128)}, f32[16,2,1024]{2,1,0:T(2,128)}, bf16[8,32,1024]{2,1,0:T(8,128)(2,1)}, /*index=5*/f32[8,128]{1,0:T(8,128)}) custom-call(bf16[8,22528,128]{2,1,0:T(8,128)(2,1)} %bitcast.84, f32[16,2,1024]{2,1,0:T(2,128)} %get-tuple-element.153.refs_1_, ...), custom_call_target="tpu_custom_call" | custom-call | flops 20000000000 | bytes 1000000 | tf_op jit(solution)/shard_map/pallas_call | solution.py:85
  564.0 83.5 %shard_map.196 = (bf16[6400,4096]{1,0:T(8,128)(2,1)}, f32[8,4096]{1,0:T(8,128)}, f32[8,1024]{1,0:T(8,128)}, bf16[6400,1024]{1,0:T(8,128)(2,1)}, f32[8,1024]{1,0:T(8,128)}, /*index=5*/f32[8,1024]{1,0:T(8,128)}) custom-call(bf16[6400,1024]{1,0:T(8,128)(2,1)} %get-tuple-element.158.x2_ref, f32[16,2,1024]{2,1,0:T(2,128)} %get-tuple-element.159.dp_ref, ...), custom_call_target="tpu_custom_call" | custom-call | flops 53687091200 | bytes 157286400 | tf_op jit(solution)/shard_map/pallas_call | solution.py:85
  647.5 63.7 %shard_map.197 = f32[8,128,8,8,128]{4,3,2,1,0:T(8,128)} custom-call(bf16[6400,4096]{1,0:T(8,128)(2,1)} %get-tuple-element.164.a_ref, bf16[6400,1024]{1,0:T(8,128)(2,1)} %get-tuple-element.165.b_ref.do_ref), custom_call_target="tpu_custom_call" | custom-call | flops 53687091200 | bytes 78643200 | tf_op jit(solution)/shard_map/pallas_call | solution.py:85
  711.2 63.8 %shard_map.198 = f32[8,32,32,8,128]{4,3,2,1,0:T(8,128)} custom-call(bf16[6400,1024]{1,0:T(8,128)(2,1)} %bitcast.112, bf16[6400,4096]{1,0:T(8,128)(2,1)} %get-tuple-element.166.refs_1_.dh_ref, f32[8,32,32,8,128]{4,3,2,1,0:T(8,128)} %bitcast.77), custom_call_target="tpu_custom_call", output_to_operand_aliasing={{}: (2, {})} | custom-call | flops 53687091200 | bytes 78643200 | tf_op jit(solution)/shard_map/pallas_call | solution.py:85
  775.0 78.4 %shard_map.199 = (bf16[6400,1024]{1,0:T(8,128)(2,1)}, f32[8,1024]{1,0:T(8,128)}, f32[8,1024]{1,0:T(8,128)}) custom-call(bf16[6400,4096]{1,0:T(8,128)(2,1)} %get-tuple-element.166.refs_1_.dh_ref, bf16[128,32,16,128]{3,2,1,0:T(8,128)(2,1)} %bitcast.92, bf16[6400,1024]{1,0:T(8,128)(2,1)} %bitcast.110, bf16[6400,1024]{1,0:T(8,128)(2,1)} %get-tuple-element.165.b_ref.do_ref, ...), custom_call_target="tpu_custom_call" | custom-call | flops 53687091200 | bytes 78643200 | tf_op jit(solution)/shard_map/pallas_call | solution.py:85
  853.4 74.6 %shard_map.200 = (bf16[32,200,1024]{2,1,0:T(8,128)(2,1)}, f32[512,200]{1,0:T(8,128)}, f32[512,200]{1,0:T(8,128)}, f32[512,128]{1,0:T(8,128)}, f32[200,128]{1,0:T...) custom-call(bf16[32,200,1024]{2,1,0:T(8,128)(2,1)} %bitcast.108, bf16[32,200,1024]{2,1,0:T(8,128)(2,1)} %bitcast.114, ...), custom_call_target="tpu_custom_call" | custom-call | flops 60000002048 | bytes 140000000 | tf_op jit(solution)/shard_map/pallas_call | solution.py:85
  931.9 36.2 %shard_map.202 = f32[8,64,8,8,128]{4,3,2,1,0:T(8,128)} custom-call(bf16[6400,4096]{1,0:T(8,128)(2,1)} %get-tuple-element.201.a_ref, bf16[6400,1024]{1,0:T(8,128)(2,1)} %bitcast.103), custom_call_target="tpu_custom_call" | custom-call | flops 26843545600 | bytes 78643200 | tf_op jit(solution)/shard_map/pallas_call | solution.py:85
  968.1 78.5 %shard_map.203 = (bf16[6400,4096]{1,0:T(8,128)(2,1)}, f32[8,4096]{1,0:T(8,128)}, f32[8,1024]{1,0:T(8,128)}) custom-call(bf16[6400,1024]{1,0:T(8,128)(2,1)} %bitcast.104, f32[6400,4096]{1,0:T(8,128)} %get-tuple-element.188.gp_ref, bf16[512,8,16,128]{3,2,1,0:T(8,128)(2,1)} %bitcast.87), custom_call_target="tpu_custom_call" | custom-call | flops 53687091200 | bytes 157286400 | tf_op jit(solution)/shard_map/pallas_call | solution.py:85
  1046.6 34.8 %shard_map.204 = f32[8,16,32,8,128]{4,3,2,1,0:T(8,128)} custom-call(bf16[6400,1024]{1,0:T(8,128)(2,1)} %bitcast.63, bf16[6400,1024]{1,0:T(8,128)(2,1)} %bitcast.64, bf16[6400,1024]{1,0:T(8,128)(2,1)} %bitcast.65, bf16[6400,1024]{1,0:T(8,128)(2,1)} %bitcast.66, bf16[6400,4096]{1,0:T(8,128)(2,1)} %get-tuple-element.202.refs_4_.dh_ref, ...), custom_call_target="tpu_custom_call", output_to_operand_aliasing={{}: (5, {})} | custom-call | flops 26843545600 | bytes 78643200 | tf_op jit(solution)/shard_map/pallas_call | solution.py:85
  1081.5 97.5 %reduce-scatter.4.cloned.1.call-done = f32[1,8192,128]{2,1,0:T(8,128)} async-done(((f32[8,8192,128]{2,1,0:T(8,128)}), f32[1,8192,128]{2,1,0:T(8,128)}) %reduce-scatter.4.cloned.1.call-update) | async-done | bytes 4194320 | tf_op jit(solution)/shard_map/reduce_scatter | solution.py:1081
  1186.8 39.8 %shard_map.206 = f32[8,64,8,8,128]{4,3,2,1,0:T(8,128)} custom-call(bf16[6400,4096]{1,0:T(8,128)(2,1)} %get-tuple-element.201.a_ref, bf16[6400,1024]{1,0:T(8,128)(2,1)} %bitcast.105), custom_call_target="tpu_custom_call" | custom-call | flops 26843545600 | bytes 78643200 | tf_op jit(solution)/shard_map/pallas_call | solution.py:85
  1226.6 34.9 %shard_map.207 = f32[8,16,32,8,128]{4,3,2,1,0:T(8,128)} custom-call(bf16[6400,1024]{1,0:T(8,128)(2,1)} %bitcast.67, bf16[6400,1024]{1,0:T(8,128)(2,1)} %bitcast.68, bf16[6400,1024]{1,0:T(8,128)(2,1)} %bitcast.69, bf16[6400,1024]{1,0:T(8,128)(2,1)} %bitcast.70, bf16[6400,4096]{1,0:T(8,128)(2,1)} %get-tuple-element.202.refs_4_.dh_ref, ...), custom_call_target="tpu_custom_call", output_to_operand_aliasing={{}: (5, {})} | custom-call | flops 26843545600 | bytes 78643200 | tf_op jit(solution)/shard_map/pallas_call | solution.py:85
  1264.1 26.3 %reduce-scatter.6.cloned.1.call-done = f32[1,4096,128]{2,1,0:T(8,128)} async-done(((f32[8,4096,128]{2,1,0:T(8,128)}), f32[1,4096,128]{2,1,0:T(8,128)}) %reduce-scatter.6.cloned.1.call-update) | async-done | bytes 2097168 | tf_op jit(solution)/shard_map/reduce_scatter | solution.py:1081
  1295.7 80.5 %shard_map.208 = (bf16[6400,1024]{1,0:T(8,128)(2,1)}, f32[8,1024]{1,0:T(8,128)}, f32[8,1024]{1,0:T(8,128)}) custom-call(bf16[6400,4096]{1,0:T(8,128)(2,1)} %get-tuple-element.202.refs_4_.dh_ref, bf16[128,32,16,128]{3,2,1,0:T(8,128)(2,1)} %bitcast.88, bf16[6400,1024]{1,0:T(8,128)(2,1)} %bitcast.102, bf16[6400,1024]{1,0:T(8,128)(2,1)} %bitcast.106, ...), custom_call_target="tpu_custom_call" | custom-call | flops 53687091200 | bytes 78643200 | tf_op jit(solution)/shard_map/pallas_call | solution.py:85
  1378.1 68.3 %shard_map.210 = (f32[512,200]{1,0:T(8,128)}, f32[512,200]{1,0:T(8,128)}, f32[512,128]{1,0:T(8,128)}, f32[200,128]{1,0:T(8,128)}, f32[8,1024]{1,0:T(8,128)}, /*index=5*/f32[8,1024]{1,0:T(8,128)}) custom-call(bf16[32,196,1024]{2,1,0:T(8,128)(2,1)} %copy.28.x_ref, bf16[32,200,1024]{2,1,0:T(8,128)(2,1)} %bitcast.113, ...), custom_call_target="tpu_custom_call" | custom-call | flops 60000002048 | bytes 140000000 | tf_op jit(solution)/shard_map/pallas_call | solution.py:85
  1452.9 18.9 %shard_map.212 = (f32[5672,128]{1,0:T(8,128)S(1)}, f32[8,208,128]{2,1,0:T(8,128)S(1)}, f32[8,128]{1,0:T(8,128)S(1)}) custom-call(f32[1664,128]{1,0:T(8,128)S(1)} %copy-done.4, f32[512,8,128]{2,1,0:T(8,128)S(1)} %bitcast.61, f32[8,128]{1,0:T(8,128)S(1)} %copy-done.5), custom_call_target="tpu_custom_call" | custom-call | flops 40000000000 | bytes 1000000 | tf_op jit(solution)/shard_map/pallas_call | solution.py:85
  1474.9 25.8 %shard_map.214 = (f32[21843,128]{1,0:T(8,128)}, f32[21843,128]{1,0:T(8,128)}, f32[21843,128]{1,0:T(8,128)}) custom-call(f32[8,128]{1,0:T(8,128)} %copy-done.2, bf16[22528,256]{1,0:T(8,128)(2,1)} %all-gather.10.cloned.1.call-done.dl_ref, bf16[256,128]{1,0:T(8,128)(2,1)} %constant_dynamic-slice_fusion.pc_ref, f32[21843,128]{1,0:T(8,128)} %bitcast.94, ...), custom_call_target="tpu_custom_call" | custom-call | flops 30000001024 | bytes 80000000 | tf_op jit(solution)/shard_map/pallas_call | solution.py:85
  1503.9 25.4 %shard_map.213 = (f32[8398,2,128]{2,1,0:T(2,128)}, f32[8398,2,128]{2,1,0:T(2,128)}, f32[8398,2,128]{2,1,0:T(2,128)}) custom-call(f32[8,128]{1,0:T(8,128)} %copy-done.2, f32[5672,128]{1,0:T(8,128)} %copy-done, f32[9768,128]{1,0:T(8,128)} %get-tuple-element.228.h0_ref, f32[9768,128]{1,0:T(8,128)} %get-tuple-element.229.g1_ref, f32[1664,128]{1,0:T(8,128)} %bitcast.60, ...), custom_call_target="tpu_custom_call" | custom-call | flops 1000000000 | bytes 60000000 | tf_op jit(solution)/shard_map/pallas_call | solution.py:85
  (57 shorter events, 73.3 us)
Async XLA Ops:
  7.2 139.7 %all-reduce.4.cloned.1.call-start = ((), (), s32[]{:S(2)}) async-start(), calls=%async_computation.4 | async-start | bytes 1605632 | tf_op jit(solution)/shard_map/psum | solution.py:1095
  18.1 137.2 %all-gather.6.cloned.1.call-start = ((), (), s32[]{:S(2)}) async-start(), calls=%async_computation.3 | async-start | bytes 18874368 | tf_op jit(solution)/shard_map/all_gather | solution.py:1094
  40.8 335.9 %all-gather.8.cloned.1.call-start = ((), (), s32[]{:S(2)}) async-start(), calls=%async_computation.5 | async-start | bytes 18874368 | tf_op jit(solution)/shard_map/all_gather | solution.py:1094
  40.9 11.4 collective-permute-start
  54.8 477.8 %all-gather.12.cloned.1.call-start = ((), (), s32[]{:S(2)}) async-start(), calls=%async_computation.11 | async-start | bytes 51904512 | tf_op jit(solution)/shard_map/all_gather | solution.py:1102
  55.4 655.8 %all-gather.10.cloned.1.call-start = ((), (), s32[]{:S(2)}) async-start(), calls=%async_computation.6 | async-start | bytes 12976128 | tf_op jit(solution)/shard_map/all_gather | solution.py:1110
  564.0 482.6 %all-reduce.6.cloned.1.call-start = ((), (), s32[]{:S(2)}) async-start(), calls=%async_computation.7 | async-start | bytes 1900544 | tf_op jit(solution)/shard_map/psum | solution.py:1146
  931.1 247.9 %reduce-scatter.4.cloned.1.call-start = ((), (), s32[]{:S(2)}) async-start(), calls=%async_computation.8 | async-start | bytes 37748736 | tf_op jit(solution)/shard_map/reduce_scatter | solution.py:1081
  931.9 358.5 %reduce-scatter.6.cloned.1.call-start = ((), (), s32[]{:S(2)}) async-start(), calls=%async_computation.9 | async-start | bytes 18874368 | tf_op jit(solution)/shard_map/reduce_scatter | solution.py:1081
  1081.4 368.0 %reduce-scatter.8.cloned.1.call-start = ((), (), s32[]{:S(2)}) async-start(), calls=%async_computation.10 | async-start | bytes 18874368 | tf_op jit(solution)/shard_map/reduce_scatter | solution.py:1081
  1376.2 73.2 %collective-permute-start.1 = (f32[1368,128]{1,0:T(8,128)}, f32[1368,128]{1,0:T(8,128)}, u32[]{:S(2)}, u32[]{:S(2)}) collective-permute-start(f32[1368,128]{1,0:T(8,128)} %get-tuple-element.222), channel_id=1, source_target_pairs={{0,1},{1,2},{2,3},{3,4},{4,5},{5,6},{6,7},{7,0}} | collective-permute-start | bytes 2101256 | tf_op jit(solution)/shard_map/ppermute | solution.py:1137
  1376.2 127.7 %collective-permute-start.2 = (f32[1368,128]{1,0:T(8,128)}, f32[1368,128]{1,0:T(8,128)}, u32[]{:S(2)}, u32[]{:S(2)}) collective-permute-start(f32[1368,128]{1,0:T(8,128)} %get-tuple-element.232), channel_id=1, source_target_pairs={{0,1},{1,2},{2,3},{3,4},{4,5},{5,6},{6,7},{7,0}} | collective-permute-start | bytes 2101256 | tf_op jit(solution)/shard_map/ppermute | solution.py:1129
  1449.4 1.6 copy-start.3
  1451.0 1.2 copy-start.4
  1452.2 0.7 copy-start.5
  1471.8 1.6 copy-start
  1473.4 0.9 copy-start.1
  1474.3 0.6 copy-start.2
Sparse Core Ops, SparseCore 0:
  18.2 51.6 all-reduce.3
  71.7 83.5 all-gather.5
  157.7 84.1 all-gather.7
  243.6 208.9 all-gather.11
  564.1 63.3 all-gather.9
  931.2 47.8 all-reduce.5
  982.6 196.3 reduce-scatter.3
  1182.5 107.8 reduce-scatter.5
  1293.9 118.2 reduce-scatter.7
